TPU v7x, 128 devices: a whole 4x4x4 slice. The times are simulated.
128 devices in a mesh: seq: 8 (over z, core), exp: 16 (over y, x).
Axes of the slice: x: 4, y: 4, z: 4, core: 2. Of those that a mesh axis runs over, the one named last changes fastest.
Arguments:
- tokens: bfloat16 [81920, 4096], P(('seq', 'exp')), may hold values from -6 to 6
- routes: int32 [81920, 2], P(('seq', 'exp')), may hold values from 0 to 31, all different within a row; in each aligned block of 640 rows (0 to 639, 640 to 1279, ...) at most 50 rows name the same one
- gates: float32 [81920, 2], P(('seq', 'exp')), may hold values from 0.1 to 1
- weights: bfloat16 [32, 4096, 1024], P('exp', 'seq'), may hold values from -0.09375 to 0.09375
Outputs:
- mixed: bfloat16 [81920, 1024], P(('seq', 'exp'))
Inputs may be any that keep to these rules, and one draw needn't show every extreme that they name: `routes`: the two experts of a token differ. Among the rows of one device no expert is named more than 50 times, a bound that some block reaches.
All inputs are finite; a program needn't handle non-finite values.
Results may differ from a plain program's by a relative error of at most 0.0049.
Values may be sent and summed in bfloat16 or wider, within the bound.
No kernel may reach another device: no remote copies, remote signals or barrier semaphores. Data moves between devices by JAX's collectives and lax.ppermute only.
A program may use at most 192 MiB of HBM per device.

v0:
```python
import jax
import jax.numpy as jnp
from jax import lax
from jax.sharding import PartitionSpec as P


def route_slots(route_block, experts, capacity):
    expert_ids = route_block.reshape(-1)
    one_hot = (expert_ids[:, None] == jnp.arange(experts, dtype=jnp.int32)[None, :]).astype(
        jnp.int32
    )
    earlier = jnp.cumsum(one_hot, axis=0) - one_hot
    slot_index = jnp.sum(earlier * one_hot, axis=1)
    return expert_ids * capacity + slot_index


def body(tokens, routes, gates, weights):
    groups = lax.axis_size("exp")
    per_group = weights.shape[0]
    experts = per_group * groups
    count_rows = tokens.shape[0]
    width = tokens.shape[1]
    capacity = 5 * count_rows // (2 * experts)
    position = route_slots(routes, experts, capacity)
    local_rows = jnp.arange(2 * count_rows, dtype=jnp.int32) // 2
    slot_rows = jnp.full((experts * capacity,), count_rows, jnp.int32).at[position].set(local_rows)
    padded = jnp.concatenate([tokens, jnp.zeros((1, width), jnp.bfloat16)], axis=0)
    outgoing = padded[slot_rows].reshape(groups, per_group, capacity, width)
    whole_weights = lax.all_gather(weights, "seq", axis=1, tiled=True)
    returned = lax.all_to_all(
        jnp.einsum(
            "sjcd,jdf->sjcf",
            lax.all_to_all(outgoing, "exp", split_axis=0, concat_axis=0, tiled=True),
            whole_weights,
            preferred_element_type=jnp.float32,
        ).astype(jnp.bfloat16),
        "exp",
        split_axis=0,
        concat_axis=0,
        tiled=True,
    )
    hidden = returned.shape[-1]
    results = returned.reshape(experts * capacity, hidden)
    picked = results[position].reshape(count_rows, 2, hidden).astype(jnp.float32)
    mixed = jnp.sum(picked * gates[:, :, None], axis=1)
    return mixed.astype(jnp.bfloat16)


def solution(mesh):
    return jax.shard_map(
        body,
        mesh=mesh,
        in_specs=(
            P(("seq", "exp"), None),
            P(("seq", "exp"), None),
            P(("seq", "exp"), None),
            P("exp", "seq", None),
        ),
        out_specs=P(("seq", "exp"), None),
        check_vma=False,
    )
```

profile of v0, /device:TPU:64, one launch (start us, length us, event | category | flops | bytes accessed | tf_op | source)
XLA Modules:
  0.0 392.0 jit_solution(17907543015240691202)
XLA Ops:
  6.5 0.0 all-gather.2.cloned.1.call-start
  6.5 0.7 all-gather.2.cloned.1.call-update
  7.3 0.9 copy.15
  8.1 0.2 eq.29
  8.3 0.2 eq.25
  8.6 9.1 %reduce-window.6 = s32[32,10,128]{2,1,0:T(8,128)S(1)} reduce-window(s32[32,10,128]{2,1,0:T(8,128)S(1)} %fusion.7, s32[]{:T(128)} %constant.29.clone.1), window={size=1x1x128 pad=0_0x0_0x127_0}, to_apply=%region_0.0 | reduce-window | flops 5201920 | bytes 327684 | tf_op jit(solution)/shard_map/reduce-window
  17.6 0.1 slice.12
  17.8 0.2 copy.17
  18.0 0.1 copy.18
  18.1 0.7 broadcast_multiply_fusion
  18.8 0.2 copy.14
  19.0 0.2 mul.29
  19.2 6.8 %concatenate.3 = bf16[641,4096]{1,0:T(8,128)(2,1)} pad(bf16[640,4096]{1,0:T(8,128)(2,1)} %param.4, bf16[]{:T(256)} %constant.26.clone.1), padding=0_1x0_0 | pad | bytes 10493954 | tf_op jit(solution)/shard_map/concatenate | solution.py:27
  26.0 0.1 broadcast_add_fusion
  26.2 0.1 fusion.10
  26.3 5.2 %scatter_custom_fusion = s32[1600]{0:T(1024)S(1)} fusion(s32[1280]{0:T(1024)S(1)} %fusion.14, s32[1280]{0:T(1024)S(1)} %add_select_fusion, s32[]{:T(128)} %constant.27.clone.1), kind=kCustom, calls=%fused_computation.28 | custom fusion | bytes 6404 | tf_op jit(solution)/shard_map/scatter | solution.py:26
  31.6 28.3 %gather_fusion = bf16[1600,4096]{1,0:T(8,128)(2,1)} fusion(bf16[641,4096]{1,0:T(8,128)(2,1)} %concatenate.3, s32[2048]{0:T(1024)S(1)} %pad_clamp_fusion.1), kind=kCustom, calls=%fused_computation | custom fusion | bytes 26220800 | tf_op jit(solution)/shard_map/gather | solution.py:28
  59.9 13.3 %reshape.57 = bf16[16,2,50,4096]{3,2,1,0:T(8,128)(2,1)} reshape(bf16[1600,4096]{1,0:T(8,128)(2,1)} %gather_fusion) | data formatting | bytes 26214400 | tf_op jit(solution)/shard_map/reshape | solution.py:28
  73.2 19.4 %copy.19 = bf16[16,2,50,4096]{3,1,2,0:T(2,128)(2,1)S(1)} copy(bf16[16,2,50,4096]{3,2,1,0:T(8,128)(2,1)} %reshape.57) | data formatting | bytes 26214400 | tf_op jit(solution)/shard_map/reshape | solution.py:28
  92.6 153.2 %all_to_all.10 = bf16[16,2,50,4096]{3,1,2,0:T(2,128)(2,1)} all-to-all(bf16[16,2,50,4096]{3,1,2,0:T(2,128)(2,1)S(1)} %copy.19), channel_id=1, replica_groups=mesh['seq'=8,'exp'=16] {'exp'}, dimensions={0} | all-to-all | bytes 26214400 | tf_op jit(solution)/shard_map/all_to_all | solution.py:33
  245.8 0.0 all-gather.2.cloned.1.call-done
  245.8 53.3 %convert_bitcast_fusion = bf16[16,2,50,1024]{3,2,0,1:T(8,128)(2,1)} fusion(bf16[2,4096,1024]{2,1,0:T(8,128)(2,1)} %all-gather.2.cloned.1.call-done, bf16[16,2,50,4096]{3,1,2,0:T(2,128)(2,1)} %all_to_all.10), kind=kOutput, calls=%fused_computation.7 | convolution fusion | flops 13423411200 | bytes 33161216 | tf_op jit(solution)/shard_map/sjcd,jdf->sjcf/dot_general | solution.py:31
  299.1 0.0 copy-start.1
  299.1 7.1 %copy.21 = bf16[16,2,50,1024]{3,1,2,0:T(2,128)(2,1)} copy(bf16[16,2,50,1024]{3,2,0,1:T(8,128)(2,1)} %convert_bitcast_fusion) | data formatting | bytes 6553600 | tf_op jit(solution)/shard_map/convert_element_type | solution.py:36
  306.2 3.7 all-to-all-start.1
  310.0 0.0 copy-done.1
  310.0 0.9 copy.23
  310.9 45.9 %all-to-all-done.1 = bf16[16,2,50,1024]{3,1,2,0:T(2,128)(2,1)S(1)} async-done(((bf16[16,2,50,1024]{3,1,2,0:T(2,128)(2,1)}), bf16[16,2,50,1024]{3,1,2,0:T(2,128)(2,1)S(1)}, u32[]{:S(2)}, u32[]{:S(2)}) %all-to-all-start.1) | async-done | bytes 3276832 | tf_op jit(solution)/shard_map/all_to_all | solution.py:30
  356.8 3.0 copy.22
  359.7 3.2 reshape.58
  362.9 5.1 %gather_fusion.1 = bf16[1280,1024]{1,0:T(8,128)(2,1)} fusion(bf16[1600,1024]{1,0:T(8,128)(2,1)S(1)} %reshape.58, s32[2048]{0:T(1024)S(1)} %pad_clamp_fusion), kind=kCustom, calls=%fused_computation.1 | custom fusion | bytes 5248000 | tf_op jit(solution)/shard_map/gather | solution.py:44
  368.0 0.0 copy-start
  368.0 6.8 %reshape.59 = f32[640,2,1024]{2,1,0:T(2,128)} reshape(bf16[1280,1024]{1,0:T(8,128)(2,1)} %gather_fusion.1) | data formatting | bytes 7864320 | tf_op jit(solution)/shard_map/convert_element_type | solution.py:44
  374.8 0.0 copy-done
  374.8 10.3 %multiply_reduce_fusion = bf16[640,1024]{1,0:T(8,128)(2,1)} fusion(f32[640,2,1024]{2,1,0:T(2,128)} %reshape.59, f32[640,2]{1,0:T(8,128)S(1)} %copy-done), kind=kLoop, calls=%fused_computation.6 | loop fusion | flops 1966080 | bytes 6558720 | tf_op jit(solution)/shard_map/reduce_sum | solution.py:45
  (7 shorter events, 0.1 us)
Async XLA Ops:
  6.5 239.3 %all-gather.2.cloned.1.call-start = ((), (), s32[]{:S(2)}) async-start(), calls=%async_computation.2 | async-start | bytes 18874368 | tf_op jit(solution)/shard_map/all_gather | solution.py:29
  299.1 10.9 %copy-start.1 = (f32[640,2]{0,1:T(2,128)S(1)}, f32[640,2]{0,1:T(2,128)}, u32[]{:S(2)}) copy-start(f32[640,2]{0,1:T(2,128)} %param.6) | copy-start | bytes 15364
  306.2 50.5 %all-to-all-start.1 = ((bf16[16,2,50,1024]{3,1,2,0:T(2,128)(2,1)}), bf16[16,2,50,1024]{3,1,2,0:T(2,128)(2,1)S(1)}, u32[]{:S(2)}, u32[]{:S(2)}) async-start(bf16[16,2,50,1024]{3,1,2,0:T(2,128)(2,1)} %copy.21), calls=%async_computation.1 | async-start | bytes 6553600 | tf_op jit(solution)/shard_map/all_to_all | solution.py:30
  368.0 6.8 %copy-start = (f32[640,2]{1,0:T(8,128)S(1)}, f32[640,2]{1,0:T(8,128)}, u32[]{:S(2)}) copy-start(f32[640,2]{1,0:T(8,128)} %copy.23) | copy-start | bytes 15364
Sparse Core Ops, SparseCore 0:
  9.0 85.9 all-gather.1
where the time goes:
time: 393 us; the launch traced here: 392 us
  blocking collectives  153 us (39%)
  local copies, waits for them, and re-layouts  101 us (26%)
  matrix products  53.3 us (14%)
  waiting for transfers between devices  46.6 us (12%)
  other arithmetic  20.4 us (5%)
  between operations  13.5 us (3%)
    all_to_all x1, blocking collectives, body(): lax.all_to_all(outgoing, 'exp', split_axis=0, concat_axis=0, tiled=True)  153 us
    dot_general x1, matrix products, body(): jnp.einsum('sjcd,jdf->sjcf', lax.all_to_all(outgoing, 'exp', split_axis=0...  53.3 us
    all_to_all x1, waiting for transfers between devices, body(): lax.all_to_all(jnp.einsum('sjcd,jdf->sjcf', lax.all_to_all(outgoing, 'exp...  45.9 us
    reshape x2, local copies, waits for them, and re-layouts, body(): outgoing = padded[slot_rows].reshape(groups, per_group, capacity, width)  32.7 us
    gather x1, local copies, waits for them, and re-layouts, body(): outgoing = padded[slot_rows].reshape(groups, per_group, capacity, width)  28.3 us
    reduce_sum x1, other arithmetic, body(): mixed = jnp.sum(picked * gates[:, :, None], axis=1)  10.3 us
    another operation x3, other arithmetic  9.23 us
  transfers between devices with their start and end apart: 2, of which 1 were waited for; matrix products, arithmetic and copies ran while one was open for 22% of the time, Pallas kernels for 0%

commit v1 on v0

v1 whole, which is shorter than its diff:
```python
import jax
import jax.numpy as jnp
from jax import lax
from jax.sharding import Mesh, PartitionSpec as P

CHUNKS = ((0, 2), (2, 32), (34, 16))
RETURNS = ((0, 1), (2,))


def gather_weights(weights):
    core = lax.axis_index("core")
    depth = weights.shape[1]
    z_size = lax.axis_size("z")
    mine = lax.dynamic_index_in_dim(weights, core, 0, keepdims=False)
    other = lax.dynamic_index_in_dim(weights, 1 - core, 0, keepdims=False)
    got = lax.ppermute(other, "core", [(0, 1), (1, 0)])
    own = jnp.where(core == 0, jnp.concatenate([mine, got]), jnp.concatenate([got, mine]))
    place = lax.axis_index("z")
    up = [(i, (i + 1) % z_size) for i in range(z_size)]
    down = [(j, i) for i, j in up]
    half = depth
    below = lax.ppermute(own, "z", up)
    above = lax.ppermute(own, "z", down)
    far_first = lax.ppermute(below[:half], "z", up)
    far_last = lax.ppermute(above[half:], "z", down)
    blocks = ((own, 0), (below, -1), (above, 1), (jnp.concatenate([far_first, far_last]), 2))
    whole = jnp.zeros((z_size * 2 * depth, weights.shape[2]), weights.dtype)
    for block, shift in blocks:
        at = ((place + shift) % z_size) * (2 * depth)
        whole = lax.dynamic_update_slice(whole, block, (at, 0))
    return whole


def body(tokens, routes, gates, weights):
    rows, width = tokens.shape
    groups = lax.axis_size("exp")
    cores = lax.axis_size("core")
    experts = groups * cores
    capacity = 5 * rows // (2 * experts)
    dest = jnp.arange(experts, dtype=jnp.int32)
    ids = (cores * (dest % groups) + dest // groups)[:, None]
    first, second = routes[:, 0][None, :], routes[:, 1][None, :]
    in_first, in_second = ids == first, ids == second
    named = in_first | in_second
    earlier = (
        lax.broadcasted_iota(jnp.int32, (rows, rows), 0)
        < lax.broadcasted_iota(jnp.int32, (rows, rows), 1)
    )
    rank = jnp.dot(
        named.astype(jnp.bfloat16), earlier.astype(jnp.bfloat16), preferred_element_type=jnp.float32
    ).astype(jnp.int32)
    slot = jnp.where(named, rank, -1)
    gate = jnp.where(in_first, gates[:, 0][None, :], jnp.where(in_second, gates[:, 1][None, :], 0.0))
    gate_hi = gate.astype(jnp.bfloat16)
    gate_lo = (gate - gate_hi.astype(jnp.float32)).astype(jnp.bfloat16)
    slot = slot[:, None, :]

    def chosen(start, size):
        return slot == (start + jnp.arange(size, dtype=jnp.int32))[None, :, None]

    whole = gather_weights(weights)
    axes = ("core", "exp")
    outs = []
    for start, size in CHUNKS:
        pick = chosen(start, size).astype(jnp.bfloat16).reshape(experts * size, rows)
        packed = jnp.dot(pick, tokens, preferred_element_type=jnp.float32).astype(jnp.bfloat16)
        packed = packed.reshape(experts, size, width)
        got = lax.all_to_all(packed, axes, split_axis=0, concat_axis=0, tiled=True)
        out = jnp.dot(
            got.reshape(experts * size, width), whole, preferred_element_type=jnp.float32
        ).astype(jnp.bfloat16)
        outs.append(out.reshape(experts, size, -1))
    mixed = 0.0
    for part in RETURNS:
        start = CHUNKS[part[0]][0]
        size = sum(CHUNKS[i][1] for i in part)
        sent = outs[part[0]] if len(part) == 1 else jnp.concatenate([outs[i] for i in part], axis=1)
        back = lax.all_to_all(sent, axes, split_axis=0, concat_axis=0, tiled=True)
        back = back.reshape(experts * size, -1)
        here = chosen(start, size)
        for gate_part in (gate_hi, gate_lo):
            weight = jnp.where(here, gate_part[:, None, :], jnp.bfloat16(0)).reshape(experts * size, rows)
            mixed = mixed + lax.dot_general(
                weight, back, (((0,), (0,)), ((), ())), preferred_element_type=jnp.float32
            )
    return mixed.astype(jnp.bfloat16)


def solution(mesh):
    cores = 2
    seq, exp = mesh.devices.shape
    fine = Mesh(mesh.devices.reshape(seq // cores, cores, exp), ("z", "core", "exp"))
    every = ("z", "core", "exp")
    return jax.shard_map(
        body,
        mesh=fine,
        in_specs=(P(every, None), P(every, None), P(every, None), P("exp", ("z", "core"), None)),
        out_specs=P(every, None),
        check_vma=False,
    )
```

time: 393 us -> 275 us (0.70)
  blocking collectives: 153 us -> 0 us
  waiting for transfers between devices: 46.6 us -> 152 us
  local copies, waits for them, and re-layouts: 101 us -> 17.3 us
  starting transfers between devices: 3.75 us -> 33.8 us
  between operations: 13.5 us -> 0.25 us
  other arithmetic: 20.4 us -> 8.84 us
  matrix products: 53.3 us -> 61 us
    all_to_all x1 -> x0, blocking collectives: 153 us -> none  [body(): lax.all_to_all(outgoing, 'exp', split_axis=0, concat_axis=0, tiled=True)]
    ppermute x0 -> x5, waiting for transfers between devices: none -> 68.4 us  [the longest x1 45.7 us: gather_weights(): below = lax.ppermute(own, 'z', up)]
    all_to_all x1 -> x5, waiting for transfers between devices: 45.9 us -> 84 us  [the longest x3 51.7 us: body(): got = lax.all_to_all(packed, axes, split_axis=0, concat_axis=0, tiled=True)]
    reshape x3, local copies, waits for them, and re-layouts: 35.9 us -> 1.38 us  [the longest x1 1.13 us: body(): packed = packed.reshape(experts, size, width)]
    gather x2 -> x0, local copies, waits for them, and re-layouts: 33.4 us -> none  [the longest x1 28.3 us: body(): outgoing = padded[slot_rows].reshape(groups, per_group, capacity, width)]
    all_to_all x1 -> x5, starting transfers between devices: 3.74 us -> 29.5 us  [the longest x3 17.3 us: body(): got = lax.all_to_all(packed, axes, split_axis=0, concat_axis=0, tiled=True)]
    convert_element_type x2 -> x0, local copies, waits for them, and re-layouts: 13.9 us -> none  [the longest x1 7.11 us: body(): returned = lax.all_to_all(jnp.einsum('sjcd,jdf->sjcf', lax.all_to_all(out...]
    reduce_sum x2 -> x0, other arithmetic: 10.4 us -> none  [the longest x1 10.3 us: body(): mixed = jnp.sum(picked * gates[:, :, None], axis=1)]
  transfers between devices with their start and end apart: 2 -> 10, of which waited for: 1 -> 9; matrix products, arithmetic and copies ran while one was open for 22% -> 26% of each run, Pallas kernels for 0% -> 0%
where the time goes in v1:
time: 275 us; the launch traced here: 274 us
  waiting for transfers between devices  152 us (55%)
  matrix products  61 us (22%)
  starting transfers between devices  33.8 us (12%)
  local copies, waits for them, and re-layouts  17.3 us (6%)
  other arithmetic  8.84 us (3%)
    all_to_all x3, waiting for transfers between devices, body(): got = lax.all_to_all(packed, axes, split_axis=0, concat_axis=0, tiled=True)  51.7 us
    ppermute x1, waiting for transfers between devices, gather_weights(): below = lax.ppermute(own, 'z', up)  45.7 us
    all_to_all x2, waiting for transfers between devices, body(): back = lax.all_to_all(sent, axes, split_axis=0, concat_axis=0, tiled=True)  32.3 us
    dot_general x3, matrix products, body(): jnp.dot(got.reshape(experts * size, width), whole, preferred_element_type...  28.7 us
    dot_general x3, matrix products, body(): jnp.dot(pick, tokens, preferred_element_type=jnp.float32)  22.3 us
    all_to_all x3, starting transfers between devices, body(): got = lax.all_to_all(packed, axes, split_axis=0, concat_axis=0, tiled=True)  17.3 us
    ppermute x1, waiting for transfers between devices, gather_weights(): far_first = lax.ppermute(below[:half], 'z', up)  16.3 us
    all_to_all x2, starting transfers between devices, body(): back = lax.all_to_all(sent, axes, split_axis=0, concat_axis=0, tiled=True)  12.2 us
  transfers between devices with their start and end apart: 10, of which 9 were waited for; matrix products, arithmetic and copies ran while one was open for 26% of the time, Pallas kernels for 0%

profile of v1, /device:TPU:64, one launch (start us, length us, event | category | flops | bytes accessed | tf_op | source)
XLA Modules:
  0.0 273.6 jit_solution(1237925652086539010)
XLA Ops:
  0.0 0.8 slice_reduce_fusion.3
  0.8 0.3 fusion.11
  1.1 0.1 eq.148
  1.1 0.1 eq.149
  1.3 0.1 eq.151
  1.4 3.6 %convolution_convert_fusion.2 = bf16[64,4096]{1,0:T(8,128)(2,1)S(1)} fusion(bf16[640,4096]{1,0:T(8,128)(2,1)} %param.4, s32[64,640]{1,0:T(8,128)S(1)} %eq.149, s32[64]{0:T(128)S(1)} %eq.151), kind=kOutput, calls=%fused_computation.2 | convolution fusion | flops 335847424 | bytes 5931264 | tf_op jit(solution)/shard_map/dot_general | solution.py:66
  4.9 1.1 reshape.233
  6.1 7.3 %all-to-all-start = ((bf16[32,2,4096]{2,1,0:T(2,128)(2,1)}), bf16[32,2,4096]{2,1,0:T(2,128)(2,1)S(1)}, u32[]{:S(2)}, u32[]{:S(2)}) async-start(bf16[32,2,4096]{2,1,0:T(2,128)(2,1)} %reshape.233), calls=%async_computation | async-start | bytes 1048576 | tf_op jit(solution)/shard_map/all_to_all | solution.py:68
  13.4 0.1 eq.166
  13.5 0.3 bitcast_compare_fusion.1
  13.8 7.5 %convolution_convert_fusion.1 = bf16[512,4096]{1,0:T(8,128)(2,1)} fusion(pred[512,640]{1,0:T(32,128)(4,1)S(1)} %bitcast_compare_fusion.1, bf16[640,4096]{1,0:T(8,128)(2,1)} %param.4), kind=kOutput, calls=%fused_computation.1 | convolution fusion | flops 2686451712 | bytes 9764864 | tf_op jit(solution)/shard_map/dot_general | solution.py:66
  21.2 4.2 %all-to-all-done = bf16[32,2,4096]{2,1,0:T(2,128)(2,1)S(1)} async-done(((bf16[32,2,4096]{2,1,0:T(2,128)(2,1)}), bf16[32,2,4096]{2,1,0:T(2,128)(2,1)S(1)}, u32[]{:S(2)}, u32[]{:S(2)}) %all-to-all-start) | async-done | bytes 524320 | tf_op jit(solution)/shard_map/all_to_all | solution.py:68
  25.4 0.8 copy-done.3
  26.2 4.9 %all-to-all-start.3 = ((bf16[32,16,4096]{2,1,0:T(8,128)(2,1)}), bf16[32,16,4096]{2,1,0:T(8,128)(2,1)}, u32[]{:S(2)}, u32[]{:S(2)}) async-start(bf16[32,16,4096]{2,1,0:T(8,128)(2,1)} %bitcast.44), calls=%async_computation.3 | async-start | bytes 8388608 | tf_op jit(solution)/shard_map/all_to_all | solution.py:68
  31.1 0.1 eq.158
  31.1 0.4 bitcast_compare_fusion
  31.6 11.3 %convolution_convert_fusion = bf16[1024,4096]{1,0:T(8,128)(2,1)} fusion(pred[1024,640]{1,0:T(32,128)(4,1)S(1)} %bitcast_compare_fusion, bf16[640,4096]{1,0:T(8,128)(2,1)} %param.4), kind=kOutput, calls=%fused_computation | convolution fusion | flops 5372903424 | bytes 14286848 | tf_op jit(solution)/shard_map/dot_general | solution.py:66
  42.9 43.8 %all-to-all-done.3 = bf16[32,16,4096]{2,1,0:T(8,128)(2,1)} async-done(((bf16[32,16,4096]{2,1,0:T(8,128)(2,1)}), bf16[32,16,4096]{2,1,0:T(8,128)(2,1)}, u32[]{:S(2)}, u32[]{:S(2)}) %all-to-all-start.3) | async-done | bytes 4194336 | tf_op jit(solution)/shard_map/all_to_all | solution.py:68
  86.7 5.1 %all-to-all-start.1 = ((bf16[32,32,4096]{2,1,0:T(8,128)(2,1)}), bf16[32,32,4096]{2,1,0:T(8,128)(2,1)}, u32[]{:S(2)}, u32[]{:S(2)}) async-start(bf16[32,32,4096]{2,1,0:T(8,128)(2,1)} %bitcast.43), calls=%async_computation.1 | async-start | bytes 16777216 | tf_op jit(solution)/shard_map/all_to_all | solution.py:68
  91.8 0.0 copy-done.2
  91.8 1.1 dynamic-slice_bitcast_fusion
  93.0 0.2 collective-permute-start
  93.2 2.7 collective-permute-done
  95.9 4.3 %broadcast_in_dim.86 = bf16[4096,1024]{1,0:T(8,128)(2,1)} broadcast(bf16[]{:T(256)} %constant.81.clone.1), dimensions={} | broadcast | bytes 8388610 | tf_op jit(solution)/shard_map/broadcast_in_dim | solution.py:27
  100.2 2.2 constant_dynamic-update-slice_fusion.2
  102.3 1.6 collective-permute-start.1
  103.9 0.5 collective-permute-start.2
  104.4 45.7 %collective-permute-done.1 = bf16[1024,1024]{1,0:T(8,128)(2,1)S(1)} collective-permute-done((bf16[1024,1024]{1,0:T(8,128)(2,1)S(1)}, bf16[1024,1024]{1,0:T(8,128)(2,1)S(1)}, u32[]{:S(2)}, u32[]{:S(2)}) %collective-permute-start.1) | collective-permute-done | bytes 2097184 | tf_op jit(solution)/shard_map/ppermute | solution.py:22
  150.1 1.1 slice.24
  151.1 1.6 collective-permute-start.3
  152.7 0.0 collective-permute-done.2
  152.7 1.4 copy-done
  154.1 1.0 slice.25
  155.1 0.5 collective-permute-start.4
  155.6 0.0 copy-done.4
  155.6 0.2 reshape.234
  155.8 0.0 copy-start.1
  155.8 1.5 constant_dynamic-update-slice_fusion.1
  157.3 0.8 copy-done.1
  158.1 1.5 constant_dynamic-update-slice_fusion
  159.6 16.3 %collective-permute-done.3 = bf16[512,1024]{1,0:T(8,128)(2,1)} collective-permute-done((bf16[512,1024]{1,0:T(8,128)(2,1)}, bf16[512,1024]{1,0:T(8,128)(2,1)}, u32[]{:S(2)}, u32[]{:S(2)}) %collective-permute-start.3) | collective-permute-done | bytes 1048608 | tf_op jit(solution)/shard_map/ppermute | solution.py:24
  175.9 3.7 %collective-permute-done.4 = bf16[512,1024]{1,0:T(8,128)(2,1)} collective-permute-done((bf16[512,1024]{1,0:T(8,128)(2,1)}, bf16[512,1024]{1,0:T(8,128)(2,1)}, u32[]{:S(2)}, u32[]{:S(2)}) %collective-permute-start.4) | collective-permute-done | bytes 1048608 | tf_op jit(solution)/shard_map/ppermute | solution.py:25
  179.7 3.0 %maximum_dynamic-update-slice_fusion = bf16[4096,1024]{1,0:T(8,128)(2,1)} fusion(bf16[4096,1024]{1,0:T(8,128)(2,1)} %constant_dynamic-update-slice_fusion, s32[]{:T(128)S(6)} %select_n.126, bf16[512,1024]{1,0:T(8,128)(2,1)} %collective-permute-done.4, bf16[512,1024]{1,0:T(8,128)(2,1)} %collective-permute-done.3), kind=kLoop, calls=%fused_computation.13 | loop fusion | flops 4194304 | bytes 4194308 | tf_op jit(solution)/shard_map/dynamic_update_slice | solution.py:30
  182.7 4.9 %convolution_convert_fusion.5 = bf16[64,1024]{1,0:T(8,128)(2,1)S(1)} fusion(bf16[64,4096]{1,0:T(8,128)(2,1)S(1)} %reshape.234, bf16[4096,1024]{1,0:T(8,128)(2,1)} %maximum_dynamic-update-slice_fusion), kind=kOutput, calls=%fused_computation.25 | convolution fusion | flops 536936448 | bytes 9043968 | tf_op jit(solution)/shard_map/dot_general | solution.py:69
  187.7 0.1 reshape.235
  187.7 10.1 %convolution_convert_fusion.4 = bf16[512,1024]{1,0:T(8,128)(2,1)} fusion(bf16[512,4096]{1,0:T(8,128)(2,1)} %bitcast.10, bf16[4096,1024]{1,0:T(8,128)(2,1)} %maximum_dynamic-update-slice_fusion), kind=kOutput, calls=%fused_computation.23 | convolution fusion | flops 4295491584 | bytes 13631488 | tf_op jit(solution)/shard_map/dot_general | solution.py:69
  197.8 3.8 %all-to-all-done.1 = bf16[32,32,4096]{2,1,0:T(8,128)(2,1)} async-done(((bf16[32,32,4096]{2,1,0:T(8,128)(2,1)}), bf16[32,32,4096]{2,1,0:T(8,128)(2,1)}, u32[]{:S(2)}, u32[]{:S(2)}) %all-to-all-start.1) | async-done | bytes 8388640 | tf_op jit(solution)/shard_map/all_to_all | solution.py:68
  201.6 6.0 %all-to-all-start.4 = ((bf16[32,16,1024]{2,1,0:T(8,128)(2,1)}), bf16[32,16,1024]{2,1,0:T(8,128)(2,1)S(1)}, u32[]{:S(2)}, u32[]{:S(2)}) async-start(bf16[32,16,1024]{2,1,0:T(8,128)(2,1)} %bitcast.11), calls=%async_computation.4 | async-start | bytes 2097152 | tf_op jit(solution)/shard_map/all_to_all | solution.py:78
  207.6 13.7 %convolution_convert_fusion.3 = bf16[1024,1024]{1,0:T(8,128)(2,1)S(1)} fusion(bf16[1024,4096]{1,0:T(8,128)(2,1)} %bitcast.4, bf16[4096,1024]{1,0:T(8,128)(2,1)} %maximum_dynamic-update-slice_fusion), kind=kOutput, calls=%fused_computation.14 | convolution fusion | flops 8590983168 | bytes 18874368 | tf_op jit(solution)/shard_map/dot_general | solution.py:69
  221.3 2.7 %pad_maximum_fusion = bf16[32,34,1024]{2,1,0:T(8,128)(2,1)} fusion(bf16[32,32,1024]{2,1,0:T(8,128)(2,1)S(1)} %bitcast.45, bf16[32,2,1024]{2,1,0:T(2,128)(2,1)S(1)} %reshape.235), kind=kLoop, calls=%fused_computation.6 | loop fusion | flops 4456448 | bytes 4456448 | tf_op jit(solution)/shard_map/concatenate | solution.py:77
  224.0 1.3 all-to-all-done.4
  225.4 1.0 copy-done.5
  226.3 6.2 %all-to-all-start.2 = ((bf16[32,34,1024]{2,1,0:T(8,128)(2,1)}), bf16[32,34,1024]{2,1,0:T(8,128)(2,1)S(1)}, u32[]{:S(2)}, u32[]{:S(2)}) async-start(bf16[32,34,1024]{2,1,0:T(8,128)(2,1)} %pad_maximum_fusion), calls=%async_computation.2 | async-start | bytes 5242880 | tf_op jit(solution)/shard_map/all_to_all | solution.py:78
  232.6 0.0 copy-done.7
  232.6 0.1 fusion.27
  232.7 0.1 fusion.28
  232.8 3.7 %fusion.16 = f32[640,1024,1]{1,0,2:T(8,128)} fusion(bf16[32,16,1024]{2,1,0:T(8,128)(2,1)} %copy-done.5, s32[32,640]{1,0:T(8,128)S(1)} %fusion.11, s32[16]{0:T(128)S(1)} %iota_add_fusion, bf16[32,640]{1,0:T(8,128)(2,1)S(1)} %fusion.27), kind=kOutput, calls=%fused_computation.34 | convolution fusion | flops 671744000 | bytes 3792960 | tf_op jit(solution)/shard_map/dot_general | solution.py:83
  236.5 31.0 %all-to-all-done.2 = bf16[32,34,1024]{2,1,0:T(8,128)(2,1)S(1)} async-done(((bf16[32,34,1024]{2,1,0:T(8,128)(2,1)}), bf16[32,34,1024]{2,1,0:T(8,128)(2,1)S(1)}, u32[]{:S(2)}, u32[]{:S(2)}) %all-to-all-start.2) | async-done | bytes 2228256 | tf_op jit(solution)/shard_map/all_to_all | solution.py:78
  267.5 1.9 fusion.3
  269.4 0.0 copy-start.6
  269.4 0.0 copy-start.8
  269.4 1.9 fusion.5
  271.4 0.1 copy-done.8
  271.5 2.1 fusion.2
  (14 shorter events, 0.1 us)
Async XLA Ops:
  6.1 19.3 %all-to-all-start = ((bf16[32,2,4096]{2,1,0:T(2,128)(2,1)}), bf16[32,2,4096]{2,1,0:T(2,128)(2,1)S(1)}, u32[]{:S(2)}, u32[]{:S(2)}) async-start(bf16[32,2,4096]{2,1,0:T(2,128)(2,1)} %reshape.233), calls=%async_computation | async-start | bytes 1048576 | tf_op jit(solution)/shard_map/all_to_all | solution.py:68
  25.4 0.8 copy-start.3
  26.2 60.5 %all-to-all-start.3 = ((bf16[32,16,4096]{2,1,0:T(8,128)(2,1)}), bf16[32,16,4096]{2,1,0:T(8,128)(2,1)}, u32[]{:S(2)}, u32[]{:S(2)}) async-start(bf16[32,16,4096]{2,1,0:T(8,128)(2,1)} %bitcast.44), calls=%async_computation.3 | async-start | bytes 8388608 | tf_op jit(solution)/shard_map/all_to_all | solution.py:68
  86.7 5.1 %copy-start.2 = (bf16[2,512,1024]{2,1,0:T(8,128)(2,1)S(1)}, bf16[2,512,1024]{2,1,0:T(8,128)(2,1)}, u32[]{:S(2)}) copy-start(bf16[2,512,1024]{2,1,0:T(8,128)(2,1)} %param.7) | copy-start | bytes 6291460
  86.7 114.9 %all-to-all-start.1 = ((bf16[32,32,4096]{2,1,0:T(8,128)(2,1)}), bf16[32,32,4096]{2,1,0:T(8,128)(2,1)}, u32[]{:S(2)}, u32[]{:S(2)}) async-start(bf16[32,32,4096]{2,1,0:T(8,128)(2,1)} %bitcast.43), calls=%async_computation.1 | async-start | bytes 16777216 | tf_op jit(solution)/shard_map/all_to_all | solution.py:68
  93.0 2.9 %collective-permute-start = (bf16[512,1024]{1,0:T(8,128)(2,1)}, bf16[512,1024]{1,0:T(8,128)(2,1)S(1)}, u32[]{:S(2)}, u32[]{:S(2)}) collective-permute-start(bf16[512,1024]{1,0:T(8,128)(2,1)} %get-tuple-element.11), channel_id=1, source_target_pairs={{0,16},{16,0},{1,17},{17,1},{2,18},{18,2},{3,19},{19,3},{4,20},{20... | collective-permute-start | bytes 3145736 | tf_op jit(solution)/shard_map/ppermute | solution.py:16
  102.3 53.2 %copy-start.4 = (bf16[32,2,4096]{2,1,0:T(2,128)(2,1)S(1)}, bf16[32,2,4096]{2,1,0:T(2,128)(2,1)}, u32[]{:S(2)}) copy-start(bf16[32,2,4096]{2,1,0:T(2,128)(2,1)} %copy-done.3) | copy-start | bytes 1572868
  102.3 47.7 %collective-permute-start.1 = (bf16[1024,1024]{1,0:T(8,128)(2,1)S(1)}, bf16[1024,1024]{1,0:T(8,128)(2,1)S(1)}, u32[]{:S(2)}, u32[]{:S(2)}) collective-permute-start(bf16[1024,1024]{1,0:T(8,128)(2,1)S(1)} %get-tuple-element.10), channel_id=1, source_target_pairs={{0,32},{32,64},{64,96},{96,0},{1,33},{33,65},{65,97},{97,1},{2,34}... | collective-permute-start | bytes 6291464 | tf_op jit(solution)/shard_map/ppermute | solution.py:22
  103.9 48.8 %collective-permute-start.2 = (bf16[1024,1024]{1,0:T(8,128)(2,1)S(1)}, bf16[1024,1024]{1,0:T(8,128)(2,1)S(1)}, u32[]{:S(2)}, u32[]{:S(2)}) collective-permute-start(bf16[1024,1024]{1,0:T(8,128)(2,1)S(1)} %get-tuple-element.10), channel_id=1, source_target_pairs={{32,0},{64,32},{96,64},{0,96},{33,1},{65,33},{97,65},{1,97},{34,2}... | collective-permute-start | bytes 6291464 | tf_op jit(solution)/shard_map/ppermute | solution.py:23
  151.1 24.8 %collective-permute-start.3 = (bf16[512,1024]{1,0:T(8,128)(2,1)}, bf16[512,1024]{1,0:T(8,128)(2,1)}, u32[]{:S(2)}, u32[]{:S(2)}) collective-permute-start(bf16[512,1024]{1,0:T(8,128)(2,1)} %slice.24), channel_id=1, source_target_pairs={{0,32},{32,64},{64,96},{96,0},{1,33},{33,65},{65,97},{97,1},{2,34}... | collective-permute-start | bytes 3145736 | tf_op jit(solution)/shard_map/ppermute | solution.py:24
  152.7 1.4 copy-start
  155.1 24.6 %collective-permute-start.4 = (bf16[512,1024]{1,0:T(8,128)(2,1)}, bf16[512,1024]{1,0:T(8,128)(2,1)}, u32[]{:S(2)}, u32[]{:S(2)}) collective-permute-start(bf16[512,1024]{1,0:T(8,128)(2,1)} %slice.25), channel_id=1, source_target_pairs={{32,0},{64,32},{96,64},{0,96},{33,1},{65,33},{97,65},{1,97},{34,2}... | collective-permute-start | bytes 3145736 | tf_op jit(solution)/shard_map/ppermute | solution.py:25
  155.8 2.3 copy-start.1
  201.6 23.8 %all-to-all-start.4 = ((bf16[32,16,1024]{2,1,0:T(8,128)(2,1)}), bf16[32,16,1024]{2,1,0:T(8,128)(2,1)S(1)}, u32[]{:S(2)}, u32[]{:S(2)}) async-start(bf16[32,16,1024]{2,1,0:T(8,128)(2,1)} %bitcast.11), calls=%async_computation.4 | async-start | bytes 2097152 | tf_op jit(solution)/shard_map/all_to_all | solution.py:78
  224.0 8.6 %copy-start.7 = (f32[640,2]{0,1:T(2,128)S(1)}, f32[640,2]{0,1:T(2,128)}, u32[]{:S(2)}) copy-start(f32[640,2]{0,1:T(2,128)} %param.6) | copy-start | bytes 15364
  225.4 1.0 copy-start.5
  226.3 41.1 %all-to-all-start.2 = ((bf16[32,34,1024]{2,1,0:T(8,128)(2,1)}), bf16[32,34,1024]{2,1,0:T(8,128)(2,1)S(1)}, u32[]{:S(2)}, u32[]{:S(2)}) async-start(bf16[32,34,1024]{2,1,0:T(8,128)(2,1)} %pad_maximum_fusion), calls=%async_computation.2 | async-start | bytes 5242880 | tf_op jit(solution)/shard_map/all_to_all | solution.py:78
  269.4 1.9 copy-start.6
  269.4 2.1 copy-start.8

commit v2 on v0

v2 whole, which is shorter than its diff:
```python
import functools

import jax
import jax.numpy as jnp
import numpy as np
from jax import lax
from jax.experimental import pallas as pl
from jax.experimental.pallas import tpu as pltpu
from jax.sharding import Mesh, PartitionSpec as P

CORES = 2
SIDE = 4
LOOSE = 2
PLANE = ("core", "y", "x")
SETS = (((0, 0), (1, 1)), ((0, -1), (-1, 2)))
BLOCKS = SETS[0] + SETS[1]
EXPERT_CALLS = (((1, 3, 2, 0),), ((1, 3), (2, 0)))
INTERPRET = False


def flat(core, y, x):
    return (core * SIDE + y % SIDE) * SIDE + x % SIDE


def pairs(first, second):
    out = []
    for core in range(CORES):
        dy, dx = (second, first) if core == 0 else (first, second)
        for y in range(SIDE):
            for x in range(SIDE):
                out.append((flat(core, y, x), flat(core, y + dy, x + dx)))
    return out


def crossed(moves):
    side = SIDE * SIDE
    return [(source, (1 - target // side) * side + target % side) for source, target in moves]


def back(moves):
    return [(target, source) for source, target in moves]


SWAP = [(0, 1), (1, 0)]
SHIFTS = (0, SIDE - 1, 1, 2)
PARTS = 2 * SIDE
UP = [(i, (i + 1) % SIDE) for i in range(SIDE)]


def regroup_kernel(main, *refs):
    ins, outs = refs[:SIDE], refs[SIDE:]
    for i, source in enumerate(ins):
        for j, target in enumerate(outs):
            target[i * main : (i + 1) * main] = source[j * main : (j + 1) * main]
    rest = SIDE * main
    for j, target in enumerate(outs):
        tail = [source[rest + j * LOOSE : rest + (j + 1) * LOOSE] for source in ins]
        target[rest:] = jnp.concatenate(tail + [source_pad(target, rest)], axis=0)


def source_pad(target, rest):
    rows = target.shape[0] - rest - SIDE * LOOSE
    return jnp.zeros((rows, target.shape[1]), target.dtype)


def regroup(arrays, main):
    rows, width = arrays[0].shape
    step = min(width, 1024)
    spec = pl.BlockSpec((rows, step), lambda i: (0, i))
    size = SIDE * rows * width * 2
    return pl.pallas_call(
        functools.partial(regroup_kernel, main),
        grid=(width // step,),
        in_specs=[spec] * SIDE,
        out_specs=[spec] * SIDE,
        out_shape=[jax.ShapeDtypeStruct((rows, width), arrays[0].dtype)] * SIDE,
        cost_estimate=pl.CostEstimate(flops=size, bytes_accessed=2 * size, transcendentals=0),
        interpret=INTERPRET,
        name="regroup",
    )(*arrays)


def dispatch_kernel(spread_ref, row_slot_ref, slot_ref, tokens_ref, *refs):
    outs, pick_ref = refs[:-1], refs[-1]
    length = outs[0].shape[0]

    @pl.when(pl.program_id(0) == 0)
    def _():
        at_row = jnp.dot(spread_ref[...], slot_ref[...], preferred_element_type=jnp.float32)
        pick_ref[...] = jnp.where(at_row == row_slot_ref[...], 1.0, 0.0).astype(pick_ref.dtype)

    values = tokens_ref[...]
    for i, out in enumerate(outs):
        rows = pick_ref[i * length : (i + 1) * length]
        out[...] = jnp.dot(rows, values, preferred_element_type=jnp.float32).astype(out.dtype)


def dispatch(spread, row_slot, slot, tokens, messages):
    count, width = tokens.shape
    total = spread.shape[0]
    length = total // messages
    step = min(width, 1024)
    return pl.pallas_call(
        dispatch_kernel,
        grid=(width // step,),
        in_specs=[
            pl.BlockSpec(spread.shape, lambda i: (0, 0)),
            pl.BlockSpec(row_slot.shape, lambda i: (0, 0)),
            pl.BlockSpec(slot.shape, lambda i: (0, 0)),
            pl.BlockSpec((count, step), lambda i: (0, i)),
        ],
        out_specs=[pl.BlockSpec((length, step), lambda i: (0, i))] * messages,
        out_shape=[jax.ShapeDtypeStruct((length, width), tokens.dtype)] * messages,
        scratch_shapes=[pltpu.VMEM((total, count), tokens.dtype)],
        cost_estimate=pl.CostEstimate(
            flops=2 * total * count * width,
            bytes_accessed=2 * width * (count + total),
            transcendentals=0,
        ),
        interpret=INTERPRET,
        name="dispatch",
    )(spread, row_slot, slot, tokens)


def expert_kernel(count, place_ref, *refs):
    values, parts, outs = refs[:count], refs[count : count + PARTS], refs[count + PARTS :]
    place, core = place_ref[0], place_ref[1]
    half = parts[0].shape[0]
    for value, out in zip(values, outs):
        total = jnp.zeros(out.shape, jnp.float32)
        for i, part in enumerate(parts):
            side = core if i % 2 == 0 else 1 - core
            start = (lax.rem(place + SHIFTS[i // 2], SIDE) * 2 + side) * half
            span = pl.ds(pl.multiple_of(start, half), half)
            total += jnp.dot(value[:, span], part[...], preferred_element_type=jnp.float32)
        out[...] = total.astype(out.dtype)


def expert(place, values, parts):
    rows, width = values[0].shape
    half, hidden = parts[0].shape
    step = min(hidden, 256)
    left = pl.BlockSpec((rows, width), lambda i: (0, 0))
    right = pl.BlockSpec((half, step), lambda i: (0, i))
    result = pl.BlockSpec((rows, step), lambda i: (0, i))
    return pl.pallas_call(
        functools.partial(expert_kernel, len(values)),
        grid=(hidden // step,),
        in_specs=[pl.BlockSpec(memory_space=pltpu.SMEM)] + [left] * len(values) + [right] * PARTS,
        out_specs=[result] * len(values),
        out_shape=[jax.ShapeDtypeStruct((rows, hidden), values[0].dtype)] * len(values),
        cost_estimate=pl.CostEstimate(
            flops=2 * len(values) * rows * width * hidden,
            bytes_accessed=2 * (len(values) * rows * (width + hidden) + width * hidden),
            transcendentals=0,
        ),
        interpret=INTERPRET,
        name="expert",
    )(place, *values, *parts)


def combine_kernel(count, hi_ref, lo_ref, *refs):
    blocks, base, out_ref, rows_ref = refs[:count], refs[count:-2], refs[-2], refs[-1]
    rows = blocks[0].shape[0]
    for i, block in enumerate(blocks):
        rows_ref[i * rows : (i + 1) * rows] = block[...]
    used = count * rows
    if used < rows_ref.shape[0]:
        rows_ref[used:] = jnp.zeros((rows_ref.shape[0] - used, rows_ref.shape[1]), rows_ref.dtype)
    values = rows_ref[...]
    total = jnp.dot(hi_ref[...], values, preferred_element_type=jnp.float32)
    total += jnp.dot(lo_ref[...], values, preferred_element_type=jnp.float32)
    for other in base:
        total += other[...]
    out_ref[...] = total.astype(out_ref.dtype)


def combine(hi, lo, blocks, base, dtype):
    count, depth = hi.shape
    hidden = blocks[0].shape[1]
    step = min(hidden, 256)
    left = pl.BlockSpec((count, depth), lambda i: (0, 0))
    right = pl.BlockSpec((blocks[0].shape[0], step), lambda i: (0, i))
    sums = pl.BlockSpec((count, step), lambda i: (0, i))
    return pl.pallas_call(
        functools.partial(combine_kernel, len(blocks)),
        grid=(hidden // step,),
        in_specs=[left, left] + [right] * len(blocks) + [sums] * len(base),
        out_specs=sums,
        out_shape=jax.ShapeDtypeStruct((count, hidden), dtype),
        scratch_shapes=[pltpu.VMEM((depth, step), blocks[0].dtype)],
        cost_estimate=pl.CostEstimate(
            flops=4 * count * depth * hidden,
            bytes_accessed=4 * count * (depth + hidden) + 2 * depth * hidden,
            transcendentals=0,
        ),
        interpret=INTERPRET,
        name="combine",
    )(hi, lo, *blocks, *base)


def expert_order(kind):
    y, x = lax.axis_index("y"), lax.axis_index("x")
    ahead = np.repeat([goff for _, goff in BLOCKS], SIDE).astype(np.int32)
    turn = np.tile(np.arange(SIDE), len(BLOCKS)).astype(np.int32)
    first = (jnp.where(kind == 0, x, y) + ahead + SIDE) % SIDE
    second = (jnp.where(kind == 0, y, x) + turn) % SIDE
    group = jnp.where(kind == 0, second * SIDE + first, first * SIDE + second)
    return (CORES * group + kind)[:, None].astype(jnp.float32)


def move(array, moves):
    return lax.ppermute(array, PLANE, moves)


def across(array, moves, axis):
    return lax.ppermute(array, axis, moves)


def compute(tokens, routes, gates, weights):
    rows, _ = tokens.shape
    experts = CORES * SIDE * SIDE
    capacity = 5 * rows // (2 * experts)
    main = capacity - LOOSE
    mine = experts // CORES
    core = lax.axis_index("core")
    place = jnp.stack([lax.axis_index("z"), core])

    kept = lax.dynamic_index_in_dim(weights, core, 0, keepdims=False)
    given = lax.dynamic_index_in_dim(weights, 1 - core, 0, keepdims=False)
    given = across(given, SWAP, "core")
    ways = jnp.concatenate([routes.T.astype(jnp.float32), gates.T])
    other_ways = across(ways, SWAP, "core")
    other_tokens = across(tokens, SWAP, "core")

    parts = []
    for s in range(len(SETS)):
        pair = [kept, given]
        if s:
            pair = [move(part, pairs(1, 0)) for part in pair]
        below = [across(part, UP, "z") for part in pair]
        above = [across(part, back(UP), "z") for part in pair]
        far = [across(below[0], UP, "z"), across(above[1], back(UP), "z")]
        parts.append(pair + below + above + far)

    used = SIDE * capacity
    length = -(-used // 16) * 16
    unit_of = np.full((length,), -1)
    slot_of = np.full((length,), -1)
    unit_of[: SIDE * main] = np.repeat(np.arange(SIDE), main)
    slot_of[: SIDE * main] = np.tile(np.arange(main), SIDE)
    unit_of[SIDE * main : used] = np.repeat(np.arange(SIDE), LOOSE)
    slot_of[SIDE * main : used] = np.tile(np.arange(main, capacity), SIDE)

    def layout(blocks, classes, depth):
        row_expert = np.full((depth,), -1)
        row_slot = np.full((depth,), -2.0, np.float32)
        at = 0
        for kind in range(classes):
            for b in blocks:
                here = slice(at, at + length)
                row_expert[here] = np.where(unit_of >= 0, kind * mine + b * SIDE + unit_of, -1)
                row_slot[here] = np.where(unit_of >= 0, slot_of, -2)
                at += length
        spread = row_expert[:, None] == np.arange(classes * mine)[None, :]
        return jnp.asarray(spread, jnp.bfloat16), jnp.asarray(row_slot)

    earlier = (
        lax.broadcasted_iota(jnp.int32, (rows, rows), 0)
        < lax.broadcasted_iota(jnp.int32, (rows, rows), 1)
    ).astype(jnp.bfloat16)

    def slots(ids, way):
        in_first, in_second = ids == way[0:1], ids == way[1:2]
        named = in_first | in_second
        rank = jnp.dot(named.astype(jnp.bfloat16), earlier, preferred_element_type=jnp.float32)
        slot = jnp.where(named, jnp.minimum(rank, capacity), -1.0).astype(jnp.bfloat16)
        gate = jnp.where(in_first, way[2:3], jnp.where(in_second, way[3:4], 0.0))
        return slot, gate

    ids = expert_order(core)
    slot, gate = slots(jnp.concatenate([ids, expert_order(1 - core)]), ways)
    other_slot, _ = slots(ids, other_ways)

    arrived = {}
    for group in ((1, 3), (0, 2)):
        spread, row_slot = layout(group, 1, len(group) * length)
        for q, (table, values) in enumerate(((slot[:mine], tokens), (other_slot, other_tokens))):
            blocks = dispatch(spread, row_slot[:, None], table, values, len(group))
            for b, block in zip(group, blocks):
                shift = BLOCKS[b][0]
                if shift:
                    block = move(block, pairs(shift, 0))
                arrived[q, b] = block

    shares = []
    high = lax.reduce_precision(gate, 8, 7)
    turned = (((0,), (1,)), ((), ()))
    per_set = len(BLOCKS) // len(SETS)
    for s in range(len(SETS)):
        held = CORES * per_set * length
        spread, row_slot = layout(range(s * per_set, (s + 1) * per_set), CORES, -(-held // 128) * 128)
        at_row = lax.dot_general(slot, spread, turned, preferred_element_type=jnp.float32)
        share = []
        for part in (high, gate - high):
            part = lax.dot_general(
                part.astype(jnp.bfloat16), spread, turned, preferred_element_type=jnp.float32
            )
            share.append(jnp.where(at_row == row_slot[None, :], part, 0.0).astype(jnp.bfloat16))
        shares.append(share)

    total = ()
    for s in range(len(SETS)):
        members = [(q, s * per_set + i) for i in range(per_set) for q in range(CORES)]
        turns = list(regroup([arrived[m] for m in members], main))
        for turn in (1, 3, 2):
            turns[turn] = move(turns[turn], pairs(0, turn))
        if s == 0:
            place, shares = lax.optimization_barrier((place, shares))
        outs = {}
        for group in EXPERT_CALLS[s]:
            outs.update(zip(group, expert(place, [turns[t] for t in group], parts[s])))
        for turn in (1, 3, 2):
            outs[turn] = move(outs[turn], back(pairs(0, turn)))
        blocks = {}
        for (q, b), block in zip(members, regroup([outs[t] for t in range(SIDE)], main)):
            moves = back(pairs(BLOCKS[b][0], 0))
            if q:
                moves = crossed(moves)
            if q or BLOCKS[b][0]:
                block = move(block, moves)
            blocks[q, b] = block
        ordered = [blocks[q, s * per_set + i] for q in range(CORES) for i in range(per_set)]
        last = s == len(SETS) - 1
        total = (combine(*shares[s], ordered, total, jnp.bfloat16 if last else jnp.float32),)
    return total[0]


def solution(mesh):
    seq, _ = mesh.devices.shape
    fine = Mesh(mesh.devices.reshape(seq // CORES, CORES, SIDE, SIDE), ("z",) + PLANE)
    every = ("z",) + PLANE
    return jax.shard_map(
        compute,
        mesh=fine,
        in_specs=(P(every, None), P(every, None), P(every, None), P(("y", "x"), ("z", "core"), None)),
        out_specs=P(every, None),
        check_vma=False,
    )
```

time: 393 us -> 269 us (0.68); the launches traced: 392 us -> 264 us
  blocking collectives: 153 us -> 0 us
  local copies, waits for them, and re-layouts: 101 us -> 7.46 us
  Pallas kernels: 0 us -> 87.8 us
  waiting for transfers between devices: 46.6 us -> 112 us
  matrix products: 53.3 us -> 8.54 us
  starting transfers between devices: 3.75 us -> 46.8 us
  other arithmetic: 20.4 us -> 0.77 us
  between operations: 13.5 us -> 0.26 us
    all_to_all x1 -> x0, blocking collectives: 153 us -> none  [body(): lax.all_to_all(outgoing, 'exp', split_axis=0, concat_axis=0, tiled=True)]
    ppermute x0 -> x39, waiting for transfers between devices: none -> 112 us  [the longest x15 92.6 us: across(): return lax.ppermute(array, axis, moves)]
    pallas_call x0 -> x13, Pallas kernels: none -> 87.8 us  [the longest x3 30.1 us: expert(): pl.pallas_call(functools.partial(expert_kernel, len(values)), grid=(hidde...]
    ppermute x0 -> x39, starting transfers between devices: none -> 46.8 us  [the longest x24 32.6 us: move(): return lax.ppermute(array, PLANE, moves)]
    all_to_all x1 -> x0, waiting for transfers between devices: 45.9 us -> none  [body(): lax.all_to_all(jnp.einsum('sjcd,jdf->sjcf', lax.all_to_all(outgoing, 'exp...]
    dot_general x1 -> x8, matrix products: 53.3 us -> 8.54 us  [the longest x4 6.41 us: compute(): lax.dot_general(part.astype(jnp.bfloat16), spread, turned, preferred_elem...]
    reshape x3 -> x0, local copies, waits for them, and re-layouts: 35.9 us -> none  [the longest x2 32.7 us: body(): outgoing = padded[slot_rows].reshape(groups, per_group, capacity, width)]
    gather x2 -> x0, local copies, waits for them, and re-layouts: 33.4 us -> none  [the longest x1 28.3 us: body(): outgoing = padded[slot_rows].reshape(groups, per_group, capacity, width)]
  transfers between devices with their start and end apart: 2 -> 39, of which waited for: 1 -> 16; matrix products, arithmetic and copies ran while one was open for 22% -> 4% of each run, Pallas kernels for 0% -> 31%
where the time goes in v2:
time: 269 us; the launch traced here: 264 us
  waiting for transfers between devices  112 us (42%)
  Pallas kernels  87.8 us (33%)
  starting transfers between devices  46.8 us (17%)
  matrix products  8.54 us (3%)
  local copies, waits for them, and re-layouts  7.46 us (3%)
    ppermute x15, waiting for transfers between devices, across(): return lax.ppermute(array, axis, moves)  92.6 us
    ppermute x24, starting transfers between devices, move(): return lax.ppermute(array, PLANE, moves)  32.6 us
    pallas_call x3, Pallas kernels, expert(): pl.pallas_call(functools.partial(expert_kernel, len(values)), grid=(hidde...  30.1 us
    pallas_call x4, Pallas kernels, dispatch(): pl.pallas_call(dispatch_kernel, grid=(width // step,), in_specs=[pl.Block...  26.3 us
    ppermute x24, waiting for transfers between devices, move(): return lax.ppermute(array, PLANE, moves)  19.8 us
    pallas_call x4, Pallas kernels, regroup(): pl.pallas_call(functools.partial(regroup_kernel, main), grid=(width // st...  17.8 us
    ppermute x15, starting transfers between devices, across(): return lax.ppermute(array, axis, moves)  14.2 us
    pallas_call x2, Pallas kernels, combine(): pl.pallas_call(functools.partial(combine_kernel, len(blocks)), grid=(hidd...  13.5 us
  transfers between devices with their start and end apart: 39, of which 16 were waited for; matrix products, arithmetic and copies ran while one was open for 4% of the time, Pallas kernels for 31%

profile of v2, /device:TPU:64, one launch (start us, length us, event | category | flops | bytes accessed | tf_op | source)
XLA Modules:
  0.0 264.0 jit_solution(5055633343554336243)
XLA Ops:
  0.0 1.7 dynamic-slice_bitcast_fusion
  1.8 0.6 collective-permute-start.6
  2.8 0.6 slice.33.slot_ref
  3.5 6.6 %dispatch.6 = (bf16[208,4096]{1,0:T(8,128)(2,1)}, bf16[208,4096]{1,0:T(8,128)(2,1)}) custom-call(bf16[416,16]{1,0:T(8,128)(2,1)} %constant.85.clone.spread_ref, f32[416,1]{1,0:T(8,128)} %constant.92.row_slot_ref, bf16[16,640]{1,0:T(8,128)(2,1)} %slice.33.slot_ref, bf16[640,4096]{1,0:T(8,128)(2,1)} %tokens_ref.3), custom_call_target="tpu_custom_call" | custom-call | flops 2181038080 | bytes 8650752 | tf_op jit(solution)/shard_map/dispatch/pallas_call | solution.py:103
  10.0 1.5 collective-permute-start.22
  11.5 1.6 collective-permute-start.27
  13.3 1.2 collective-permute-done
  14.8 2.0 collective-permute-start.2
  16.9 0.8 fusion.7.slot_ref
  17.7 6.6 %dispatch.7 = (bf16[208,4096]{1,0:T(8,128)(2,1)}, bf16[208,4096]{1,0:T(8,128)(2,1)}) custom-call(bf16[416,16]{1,0:T(8,128)(2,1)} %constant.85.clone.spread_ref, f32[416,1]{1,0:T(8,128)} %constant.92.row_slot_ref, bf16[16,640]{1,0:T(8,128)(2,1)} %fusion.7.slot_ref, bf16[640,4096]{1,0:T(8,128)(2,1)} %collective-permute-done.1.tokens_ref), custom_call_target="tpu_custom_call" | custom-call | flops 2181038080 | bytes 8650752 | tf_op jit(solution)/shard_map/dispatch/pallas_call | solution.py:103
  24.3 12.3 %collective-permute-done.27.refs_6_ = bf16[512,1024]{1,0:T(8,128)(2,1)} collective-permute-done((bf16[512,1024]{1,0:T(8,128)(2,1)S(1)}, bf16[512,1024]{1,0:T(8,128)(2,1)}, u32[]{:S(2)}, u32[]{:S(2)}) %collective-permute-start.27) | collective-permute-done | bytes 1048608 | tf_op jit(solution)/shard_map/ppermute | solution.py:217
  36.6 1.5 collective-permute-start.23
  38.1 1.7 collective-permute-done.29.refs_8_
  40.2 4.5 %collective-permute-done.5.refs_2_ = bf16[512,1024]{1,0:T(8,128)(2,1)} collective-permute-done((bf16[512,1024]{1,0:T(8,128)(2,1)S(1)}, bf16[512,1024]{1,0:T(8,128)(2,1)}, u32[]{:S(2)}, u32[]{:S(2)}) %collective-permute-start.5) | collective-permute-done | bytes 1048608 | tf_op jit(solution)/shard_map/ppermute | solution.py:213
  44.6 1.6 collective-permute-start.31
  46.3 1.6 collective-permute-start.3
  47.9 16.6 %collective-permute-done.30.refs_9_ = bf16[512,1024]{1,0:T(8,128)(2,1)} collective-permute-done((bf16[512,1024]{1,0:T(8,128)(2,1)}, bf16[512,1024]{1,0:T(8,128)(2,1)}, u32[]{:S(2)}, u32[]{:S(2)}) %collective-permute-start.30) | collective-permute-done | bytes 1048608 | tf_op jit(solution)/shard_map/ppermute | solution.py:217
  64.5 1.5 collective-permute-start.7
  65.9 4.9 %collective-permute-done.31.refs_10_ = bf16[512,1024]{1,0:T(8,128)(2,1)S(1)} collective-permute-done((bf16[512,1024]{1,0:T(8,128)(2,1)}, bf16[512,1024]{1,0:T(8,128)(2,1)S(1)}, u32[]{:S(2)}, u32[]{:S(2)}) %collective-permute-start.31) | collective-permute-done | bytes 1048608 | tf_op jit(solution)/shard_map/ppermute | solution.py:217
  70.9 1.6 collective-permute-start.8
  72.5 20.9 %collective-permute-done.28.refs_7_ = bf16[512,1024]{1,0:T(8,128)(2,1)} collective-permute-done((bf16[512,1024]{1,0:T(8,128)(2,1)}, bf16[512,1024]{1,0:T(8,128)(2,1)}, u32[]{:S(2)}, u32[]{:S(2)}) %collective-permute-start.28) | collective-permute-done | bytes 1048608 | tf_op jit(solution)/shard_map/ppermute | solution.py:217
  93.6 2.1 collective-permute-start.32
  95.7 6.5 %dispatch.4 = (bf16[208,4096]{1,0:T(8,128)(2,1)}, bf16[208,4096]{1,0:T(8,128)(2,1)}) custom-call(bf16[416,16]{1,0:T(8,128)(2,1)} %constant.87.clone.spread_ref, f32[416,1]{1,0:T(8,128)} %constant.92.row_slot_ref, bf16[16,640]{1,0:T(8,128)(2,1)} %slice.33.slot_ref, bf16[640,4096]{1,0:T(8,128)(2,1)} %tokens_ref.3), custom_call_target="tpu_custom_call" | custom-call | flops 2181038080 | bytes 8650752 | tf_op jit(solution)/shard_map/dispatch/pallas_call | solution.py:103
  102.2 6.6 %dispatch.5 = (bf16[208,4096]{1,0:T(8,128)(2,1)}, bf16[208,4096]{1,0:T(8,128)(2,1)}) custom-call(bf16[416,16]{1,0:T(8,128)(2,1)} %constant.87.clone.spread_ref, f32[416,1]{1,0:T(8,128)} %constant.92.row_slot_ref, bf16[16,640]{1,0:T(8,128)(2,1)} %fusion.7.slot_ref, bf16[640,4096]{1,0:T(8,128)(2,1)} %collective-permute-done.1.tokens_ref), custom_call_target="tpu_custom_call" | custom-call | flops 2181038080 | bytes 8650752 | tf_op jit(solution)/shard_map/dispatch/pallas_call | solution.py:103
  108.9 6.3 %regroup.6 = (bf16[208,4096]{1,0:T(8,128)(2,1)}, bf16[208,4096]{1,0:T(8,128)(2,1)}, bf16[208,4096]{1,0:T(8,128)(2,1)}, bf16[208,4096]{1,0:T(8,128)(2,1)}) custom-call(bf16[208,4096]{1,0:T(8,128)(2,1)} %get-tuple-element.63.refs_0_, bf16[208,4096]{1,0:T(8,128)(2,1)} %get-tuple-element.64.refs_1_, bf16[208,4096]{1,0:T(8,128)(2,1)} %collective-permute-done.22.refs_2_, ...), custom_call_target="tpu_custom_call" | custom-call | flops 6815744 | bytes 13631488 | tf_op jit(solution)/shard_map/regroup/pallas_call | solution.py:71
  115.2 1.6 collective-permute-start.24
  116.9 1.7 collective-permute-start.25
  118.5 1.2 collective-permute-done.10.refs_6_
  119.8 3.2 %collective-permute-start.26 = (bf16[208,4096]{1,0:T(8,128)(2,1)}, bf16[208,4096]{1,0:T(8,128)(2,1)}, u32[]{:S(2)}, u32[]{:S(2)}) collective-permute-start(bf16[208,4096]{1,0:T(8,128)(2,1)} %get-tuple-element.69), channel_id=1, source_target_pairs={{0,8},{1,9},{2,10},{3,11},{4,12},{5,13},{6,14},{7,15},{8,0},{9,1},... | collective-permute-start | bytes 5111816 | tf_op jit(solution)/shard_map/ppermute | solution.py:213
  123.0 15.2 %collective-permute-done.32.refs_11_ = bf16[512,1024]{1,0:T(8,128)(2,1)} collective-permute-done((bf16[512,1024]{1,0:T(8,128)(2,1)}, bf16[512,1024]{1,0:T(8,128)(2,1)}, u32[]{:S(2)}, u32[]{:S(2)}) %collective-permute-start.32) | collective-permute-done | bytes 1048608 | tf_op jit(solution)/shard_map/ppermute | solution.py:217
  138.2 0.8 collective-permute-start.11
  139.0 1.9 collective-permute-start.12
  141.4 1.6 select_convert_fusion.lo_ref
  143.0 6.1 %regroup.4 = (bf16[208,4096]{1,0:T(8,128)(2,1)}, bf16[208,4096]{1,0:T(8,128)(2,1)}, bf16[208,4096]{1,0:T(8,128)(2,1)}, bf16[208,4096]{1,0:T(8,128)(2,1)}) custom-call(bf16[208,4096]{1,0:T(8,128)(2,1)} %get-tuple-element.45.refs_0_, bf16[208,4096]{1,0:T(8,128)(2,1)} %get-tuple-element.46.refs_1_, bf16[208,4096]{1,0:T(8,128)(2,1)} %copy-done, ...), custom_call_target="tpu_custom_call" | custom-call | flops 6815744 | bytes 13631488 | tf_op jit(solution)/shard_map/regroup/pallas_call | solution.py:71
  149.2 11.3 %collective-permute-done.11.refs_7_ = bf16[512,1024]{1,0:T(8,128)(2,1)} collective-permute-done((bf16[512,1024]{1,0:T(8,128)(2,1)}, bf16[512,1024]{1,0:T(8,128)(2,1)}, u32[]{:S(2)}, u32[]{:S(2)}) %collective-permute-start.11) | collective-permute-done | bytes 1048608 | tf_op jit(solution)/shard_map/ppermute | solution.py:217
  160.6 3.2 %collective-permute-start.15 = (bf16[208,4096]{1,0:T(8,128)(2,1)}, bf16[208,4096]{1,0:T(8,128)(2,1)}, u32[]{:S(2)}, u32[]{:S(2)}) collective-permute-start(bf16[208,4096]{1,0:T(8,128)(2,1)} %get-tuple-element.53), channel_id=1, source_target_pairs={{0,12},{1,13},{2,14},{3,15},{4,0},{5,1},{6,2},{7,3},{8,4},{9,5},{1... | collective-permute-start | bytes 5111816 | tf_op jit(solution)/shard_map/ppermute | solution.py:213
  163.7 1.6 select_convert_fusion.1.hi_ref
  165.9 0.7 copy-done.14
  166.5 2.8 %collective-permute-start.9 = (bf16[512,1024]{1,0:T(8,128)(2,1)}, bf16[512,1024]{1,0:T(8,128)(2,1)S(1)}, u32[]{:S(2)}, u32[]{:S(2)}) collective-permute-start(bf16[512,1024]{1,0:T(8,128)(2,1)} %collective-permute-done.7.refs_3_), channel_id=1, source_target_pairs={{0,32},{32,64},{64,96},{96,0},{1,33},{33,65},{65,97},{97,1},{2,34}... | collective-permute-start | bytes 3145736 | tf_op jit(solution)/shard_map/ppermute | solution.py:217
  169.4 1.6 select_convert_fusion.2.lo_ref
  171.0 0.7 pad_add_fusion.place_ref
  171.6 1.6 select_convert_fusion.3.hi_ref
  173.2 12.7 %expert.5 = (bf16[208,1024]{1,0:T(8,128)(2,1)}, bf16[208,1024]{1,0:T(8,128)(2,1)}, bf16[208,1024]{1,0:T(8,128)(2,1)}, bf16[208,1024]{1,0:T(8,128)(2,1)}) custom-call(s32[2]{0:T(128)} %pad_add_fusion.place_ref, bf16[208,4096]{1,0:T(8,128)(2,1)} %copy-done.14, bf16[208,4096]{1,0:T(8,128)(2,1)} %collective-permute-done.25.refs_1_, ...), custom_call_target="tpu_custom_call" | custom-call | flops 6979321856 | bytes 16908288 | tf_op jit(solution)/shard_map/expert/pallas_call | solution.py:146
  185.9 6.0 %collective-permute-done.9.refs_5_ = bf16[512,1024]{1,0:T(8,128)(2,1)S(1)} collective-permute-done((bf16[512,1024]{1,0:T(8,128)(2,1)}, bf16[512,1024]{1,0:T(8,128)(2,1)S(1)}, u32[]{:S(2)}, u32[]{:S(2)}) %collective-permute-start.9) | collective-permute-done | bytes 1048608 | tf_op jit(solution)/shard_map/ppermute | solution.py:217
  191.9 1.0 copy-done.16
  192.9 1.2 collective-permute-done.13.refs_9_
  194.1 12.6 %collective-permute-done.14.refs_0_ = bf16[208,4096]{1,0:T(8,128)(2,1)} collective-permute-done((bf16[208,4096]{1,0:T(8,128)(2,1)}, bf16[208,4096]{1,0:T(8,128)(2,1)}, u32[]{:S(2)}, u32[]{:S(2)}) %collective-permute-start.14) | collective-permute-done | bytes 1703968 | tf_op jit(solution)/shard_map/ppermute | solution.py:213
  206.7 8.7 %expert.4 = (bf16[208,1024]{1,0:T(8,128)(2,1)}, bf16[208,1024]{1,0:T(8,128)(2,1)}) custom-call(s32[2]{0:T(128)} %pad_add_fusion.place_ref, bf16[208,4096]{1,0:T(8,128)(2,1)} %collective-permute-done.14.refs_0_, bf16[208,4096]{1,0:T(8,128)(2,1)} %collective-permute-done.15.refs_1_, bf16[512,1024]{1,0:T(8,128)(2,1)} %collective-permute-done.5.refs_2_, ...), custom_call_target="tpu_custom_call" | custom-call | flops 3489660928 | bytes 12648448 | tf_op jit(solution)/shard_map/expert/pallas_call | solution.py:146
  215.3 3.3 %collective-permute-start.16 = (bf16[208,1024]{1,0:T(8,128)(2,1)}, bf16[208,1024]{1,0:T(8,128)(2,1)S(1)}, u32[]{:S(2)}, u32[]{:S(2)}) collective-permute-start(bf16[208,1024]{1,0:T(8,128)(2,1)} %get-tuple-element.54), channel_id=1, source_target_pairs={{4,0},{5,1},{6,2},{7,3},{8,4},{9,5},{10,6},{11,7},{12,8},{13,9},{1... | collective-permute-start | bytes 1277960 | tf_op jit(solution)/shard_map/ppermute | solution.py:213
  218.6 8.7 %expert.3 = (bf16[208,1024]{1,0:T(8,128)(2,1)}, bf16[208,1024]{1,0:T(8,128)(2,1)}) custom-call(s32[2]{0:T(128)} %pad_add_fusion.place_ref, bf16[208,4096]{1,0:T(8,128)(2,1)} %collective-permute-done.4.refs_0_, bf16[208,4096]{1,0:T(8,128)(2,1)} %get-tuple-element.50.refs_1_, bf16[512,1024]{1,0:T(8,128)(2,1)} %collective-permute-done.5.refs_2_, ...), custom_call_target="tpu_custom_call" | custom-call | flops 3489660928 | bytes 12648448 | tf_op jit(solution)/shard_map/expert/pallas_call | solution.py:146
  227.4 1.6 collective-permute-start.17
  229.0 0.7 copy-done.7
  229.9 2.7 %regroup.7 = (bf16[208,1024]{1,0:T(8,128)(2,1)}, bf16[208,1024]{1,0:T(8,128)(2,1)}, bf16[208,1024]{1,0:T(8,128)(2,1)}, bf16[208,1024]{1,0:T(8,128)(2,1)}) custom-call(bf16[208,1024]{1,0:T(8,128)(2,1)} %get-tuple-element.71.refs_0_, bf16[208,1024]{1,0:T(8,128)(2,1)} %copy-done.5, bf16[208,1024]{1,0:T(8,128)(2,1)} %copy-done.7, bf16[208,1024]{1,0:T(8,128)(2,1)} %copy-done.8), custom_call_target="tpu_custom_call" | custom-call | flops 1703936 | bytes 3407872 | tf_op jit(solution)/shard_map/regroup/pallas_call | solution.py:71
  232.6 5.1 %collective-permute-start.36 = (bf16[208,1024]{1,0:T(8,128)(2,1)}, bf16[208,1024]{1,0:T(8,128)(2,1)S(1)}, u32[]{:S(2)}, u32[]{:S(2)}) collective-permute-start(bf16[208,1024]{1,0:T(8,128)(2,1)} %get-tuple-element.76), channel_id=1, source_target_pairs={{1,0},{2,1},{3,2},{0,3},{5,4},{6,5},{7,6},{4,7},{9,8},{10,9},{11,1... | collective-permute-start | bytes 1277960 | tf_op jit(solution)/shard_map/ppermute | solution.py:213
  237.7 0.9 collective-permute-start.38
  238.7 0.7 copy-done.6
  239.5 2.7 %regroup.5 = (bf16[208,1024]{1,0:T(8,128)(2,1)}, bf16[208,1024]{1,0:T(8,128)(2,1)}, bf16[208,1024]{1,0:T(8,128)(2,1)}, bf16[208,1024]{1,0:T(8,128)(2,1)}) custom-call(bf16[208,1024]{1,0:T(8,128)(2,1)} %get-tuple-element.51.refs_0_, bf16[208,1024]{1,0:T(8,128)(2,1)} %copy-done.4, bf16[208,1024]{1,0:T(8,128)(2,1)} %copy-done.9, bf16[208,1024]{1,0:T(8,128)(2,1)} %copy-done.6), custom_call_target="tpu_custom_call" | custom-call | flops 1703936 | bytes 3407872 | tf_op jit(solution)/shard_map/regroup/pallas_call | solution.py:71
  242.2 2.3 collective-permute-start.19
  244.6 1.6 collective-permute-start.21
  246.2 2.0 collective-permute-done.38.refs_3_
  248.2 0.8 copy-done.19
  249.0 6.6 %combine.2.refs_4_ = f32[640,1024]{1,0:T(8,128)} custom-call(bf16[640,896]{1,0:T(8,128)(2,1)} %select_convert_fusion.3.hi_ref, bf16[640,896]{1,0:T(8,128)(2,1)} %select_convert_fusion.2.lo_ref, bf16[208,1024]{1,0:T(8,128)(2,1)} %get-tuple-element.75.refs_0_, bf16[208,1024]{1,0:T(8,128)(2,1)} %copy-done.17, bf16[208,1024]{1,0:T(8,128)(2,1)} %copy-done.18, ...), custom_call_target="tpu_custom_call" | custom-call | flops 2348810240 | bytes 6750208 | tf_op jit(solution)/shard_map/combine/pallas_call | solution.py:185
  255.6 0.7 collective-permute-done.21.refs_3_
  257.1 6.8 %combine.3 = bf16[640,1024]{1,0:T(8,128)(2,1)} custom-call(bf16[640,896]{1,0:T(8,128)(2,1)} %select_convert_fusion.1.hi_ref, bf16[640,896]{1,0:T(8,128)(2,1)} %select_convert_fusion.lo_ref, bf16[208,1024]{1,0:T(8,128)(2,1)} %get-tuple-element.57.refs_0_, bf16[208,1024]{1,0:T(8,128)(2,1)} %copy-done.20, bf16[208,1024]{1,0:T(8,128)(2,1)} %copy-done.21, ...), custom_call_target="tpu_custom_call" | custom-call | flops 2348810240 | bytes 6750208 | tf_op jit(solution)/shard_map/combine/pallas_call | solution.py:185
  (92 shorter events, 3.8 us)
Async XLA Ops:
  0.0 16.8 %collective-permute-start.1 = (bf16[640,4096]{1,0:T(8,128)(2,1)}, bf16[640,4096]{1,0:T(8,128)(2,1)}, u32[]{:S(2)}, u32[]{:S(2)}) collective-permute-start(bf16[640,4096]{1,0:T(8,128)(2,1)} %tokens_ref.3), channel_id=1, source_target_pairs={{0,16},{16,0},{1,17},{17,1},{2,18},{18,2},{3,19},{19,3},{4,20},{20... | collective-permute-start | bytes 15728648 | tf_op jit(solution)/shard_map/ppermute | solution.py:217
  0.0 2.4 copy-start.11
  0.0 2.4 copy-start.10
  0.0 2.4 copy-start.12
  0.0 2.4 copy-start.13
  1.8 15.1 %copy-start.1 = (bf16[512,1024]{1,0:T(8,128)(2,1)}, bf16[512,1024]{1,0:T(8,128)(2,1)S(1)}, u32[]{:S(2)}) copy-start(bf16[512,1024]{1,0:T(8,128)(2,1)S(1)} %get-tuple-element.86.refs_4_) | copy-start | bytes 3145732
  1.8 13.0 %collective-permute-start.6 = (bf16[512,1024]{1,0:T(8,128)(2,1)S(1)}, bf16[512,1024]{1,0:T(8,128)(2,1)}, u32[]{:S(2)}, u32[]{:S(2)}) collective-permute-start(bf16[512,1024]{1,0:T(8,128)(2,1)S(1)} %get-tuple-element.85), channel_id=1, source_target_pairs={{0,16},{16,0},{1,17},{17,1},{2,18},{18,2},{3,19},{19,3},{4,20},{20... | collective-permute-start | bytes 3145736 | tf_op jit(solution)/shard_map/ppermute | solution.py:217
  10.0 36.2 %collective-permute-start.22 = (bf16[208,4096]{1,0:T(8,128)(2,1)}, bf16[208,4096]{1,0:T(8,128)(2,1)}, u32[]{:S(2)}, u32[]{:S(2)}) collective-permute-start(bf16[208,4096]{1,0:T(8,128)(2,1)} %get-tuple-element.65), channel_id=1, source_target_pairs={{0,1},{1,2},{2,3},{3,0},{4,5},{5,6},{6,7},{7,4},{8,9},{9,10},{10,1... | collective-permute-start | bytes 5111816 | tf_op jit(solution)/shard_map/ppermute | solution.py:213
  11.5 25.0 %collective-permute-start.27 = (bf16[512,1024]{1,0:T(8,128)(2,1)S(1)}, bf16[512,1024]{1,0:T(8,128)(2,1)}, u32[]{:S(2)}, u32[]{:S(2)}) collective-permute-start(bf16[512,1024]{1,0:T(8,128)(2,1)S(1)} %get-tuple-element.86.refs_4_), channel_id=1, source_target_pairs={{0,32},{32,64},{64,96},{96,0},{1,33},{33,65},{65,97},{97,1},{2,34}... | collective-permute-start | bytes 3145736 | tf_op jit(solution)/shard_map/ppermute | solution.py:217
  13.2 1.3 collective-permute-start
  14.4 25.3 %collective-permute-start.29 = (bf16[512,1024]{1,0:T(8,128)(2,1)S(1)}, bf16[512,1024]{1,0:T(8,128)(2,1)}, u32[]{:S(2)}, u32[]{:S(2)}) collective-permute-start(bf16[512,1024]{1,0:T(8,128)(2,1)S(1)} %get-tuple-element.86.refs_4_), channel_id=1, source_target_pairs={{32,0},{64,32},{96,64},{0,96},{33,1},{65,33},{97,65},{1,97},{34,2}... | collective-permute-start | bytes 3145736 | tf_op jit(solution)/shard_map/ppermute | solution.py:217
  14.8 31.4 %collective-permute-start.2 = (bf16[208,4096]{1,0:T(8,128)(2,1)}, bf16[208,4096]{1,0:T(8,128)(2,1)S(1)}, u32[]{:S(2)}, u32[]{:S(2)}) collective-permute-start(bf16[208,4096]{1,0:T(8,128)(2,1)} %get-tuple-element.47), channel_id=1, source_target_pairs={{0,3},{1,0},{2,1},{3,2},{4,7},{5,4},{6,5},{7,6},{8,11},{9,8},{10,9... | collective-permute-start | bytes 5111816 | tf_op jit(solution)/shard_map/ppermute | solution.py:213
  16.8 27.8 %collective-permute-start.5 = (bf16[512,1024]{1,0:T(8,128)(2,1)S(1)}, bf16[512,1024]{1,0:T(8,128)(2,1)}, u32[]{:S(2)}, u32[]{:S(2)}) collective-permute-start(bf16[512,1024]{1,0:T(8,128)(2,1)S(1)} %get-tuple-element.86.refs_4_), channel_id=1, source_target_pairs={{0,1},{1,2},{2,3},{3,0},{4,5},{5,6},{6,7},{7,4},{8,9},{9,10},{10,1... | collective-permute-start | bytes 3145736 | tf_op jit(solution)/shard_map/ppermute | solution.py:213
  36.6 57.0 %collective-permute-start.23 = (bf16[208,4096]{1,0:T(8,128)(2,1)}, bf16[208,4096]{1,0:T(8,128)(2,1)}, u32[]{:S(2)}, u32[]{:S(2)}) collective-permute-start(bf16[208,4096]{1,0:T(8,128)(2,1)} %get-tuple-element.66), channel_id=1, source_target_pairs={{0,1},{1,2},{2,3},{3,0},{4,5},{5,6},{6,7},{7,4},{8,9},{9,10},{10,1... | collective-permute-start | bytes 5111816 | tf_op jit(solution)/shard_map/ppermute | solution.py:213
  39.8 24.7 %collective-permute-start.30 = (bf16[512,1024]{1,0:T(8,128)(2,1)}, bf16[512,1024]{1,0:T(8,128)(2,1)}, u32[]{:S(2)}, u32[]{:S(2)}) collective-permute-start(bf16[512,1024]{1,0:T(8,128)(2,1)} %collective-permute-done.6.refs_5_), channel_id=1, source_target_pairs={{32,0},{64,32},{96,64},{0,96},{33,1},{65,33},{97,65},{1,97},{34,2}... | collective-permute-start | bytes 3145736 | tf_op jit(solution)/shard_map/ppermute | solution.py:217
  44.6 26.2 %collective-permute-start.31 = (bf16[512,1024]{1,0:T(8,128)(2,1)}, bf16[512,1024]{1,0:T(8,128)(2,1)S(1)}, u32[]{:S(2)}, u32[]{:S(2)}) collective-permute-start(bf16[512,1024]{1,0:T(8,128)(2,1)} %collective-permute-done.27.refs_6_), channel_id=1, source_target_pairs={{0,32},{32,64},{64,96},{96,0},{1,33},{33,65},{65,97},{97,1},{2,34}... | collective-permute-start | bytes 3145736 | tf_op jit(solution)/shard_map/ppermute | solution.py:217
  46.3 47.2 %collective-permute-start.28 = (bf16[512,1024]{1,0:T(8,128)(2,1)}, bf16[512,1024]{1,0:T(8,128)(2,1)}, u32[]{:S(2)}, u32[]{:S(2)}) collective-permute-start(bf16[512,1024]{1,0:T(8,128)(2,1)} %collective-permute-done.6.refs_5_), channel_id=1, source_target_pairs={{0,32},{32,64},{64,96},{96,0},{1,33},{33,65},{65,97},{97,1},{2,34}... | collective-permute-start | bytes 3145736 | tf_op jit(solution)/shard_map/ppermute | solution.py:217
  46.3 56.0 %copy-start = (bf16[208,4096]{1,0:T(8,128)(2,1)}, bf16[208,4096]{1,0:T(8,128)(2,1)S(1)}, u32[]{:S(2)}) copy-start(bf16[208,4096]{1,0:T(8,128)(2,1)S(1)} %collective-permute-done.2.refs_2_) | copy-start | bytes 5111812
  46.3 92.7 %collective-permute-start.3 = (bf16[208,4096]{1,0:T(8,128)(2,1)}, bf16[208,4096]{1,0:T(8,128)(2,1)}, u32[]{:S(2)}, u32[]{:S(2)}) collective-permute-start(bf16[208,4096]{1,0:T(8,128)(2,1)} %get-tuple-element.48), channel_id=1, source_target_pairs={{0,3},{1,0},{2,1},{3,2},{4,7},{5,4},{6,5},{7,6},{8,11},{9,8},{10,9... | collective-permute-start | bytes 5111816 | tf_op jit(solution)/shard_map/ppermute | solution.py:213
  64.5 50.8 %collective-permute-start.7 = (bf16[512,1024]{1,0:T(8,128)(2,1)}, bf16[512,1024]{1,0:T(8,128)(2,1)}, u32[]{:S(2)}, u32[]{:S(2)}) collective-permute-start(bf16[512,1024]{1,0:T(8,128)(2,1)} %collective-permute-done.6.refs_5_), channel_id=1, source_target_pairs={{0,1},{1,2},{2,3},{3,0},{4,5},{5,6},{6,7},{7,4},{8,9},{9,10},{10,1... | collective-permute-start | bytes 3145736 | tf_op jit(solution)/shard_map/ppermute | solution.py:213
  70.9 31.4 %copy-start.15 = (bf16[512,1024]{1,0:T(8,128)(2,1)}, bf16[512,1024]{1,0:T(8,128)(2,1)S(1)}, u32[]{:S(2)}) copy-start(bf16[512,1024]{1,0:T(8,128)(2,1)S(1)} %collective-permute-done.31.refs_10_) | copy-start | bytes 3145732
  70.9 46.0 %collective-permute-start.8 = (bf16[512,1024]{1,0:T(8,128)(2,1)}, bf16[512,1024]{1,0:T(8,128)(2,1)}, u32[]{:S(2)}, u32[]{:S(2)}) collective-permute-start(bf16[512,1024]{1,0:T(8,128)(2,1)} %collective-permute-done.5.refs_2_), channel_id=1, source_target_pairs={{0,32},{32,64},{64,96},{96,0},{1,33},{33,65},{65,97},{97,1},{2,34}... | collective-permute-start | bytes 3145736 | tf_op jit(solution)/shard_map/ppermute | solution.py:217
  93.4 26.3 %collective-permute-start.10 = (bf16[512,1024]{1,0:T(8,128)(2,1)}, bf16[512,1024]{1,0:T(8,128)(2,1)}, u32[]{:S(2)}, u32[]{:S(2)}) collective-permute-start(bf16[512,1024]{1,0:T(8,128)(2,1)} %collective-permute-done.5.refs_2_), channel_id=1, source_target_pairs={{32,0},{64,32},{96,64},{0,96},{33,1},{65,33},{97,65},{1,97},{34,2}... | collective-permute-start | bytes 3145736 | tf_op jit(solution)/shard_map/ppermute | solution.py:217
  93.6 44.6 %collective-permute-start.32 = (bf16[512,1024]{1,0:T(8,128)(2,1)}, bf16[512,1024]{1,0:T(8,128)(2,1)}, u32[]{:S(2)}, u32[]{:S(2)}) collective-permute-start(bf16[512,1024]{1,0:T(8,128)(2,1)} %collective-permute-done.30.refs_9_), channel_id=1, source_target_pairs={{32,0},{64,32},{96,64},{0,96},{33,1},{65,33},{97,65},{1,97},{34,2}... | collective-permute-start | bytes 3145736 | tf_op jit(solution)/shard_map/ppermute | solution.py:217
  108.9 32.0 %copy-start.3 = (bf16[896,32]{1,0:T(8,128)(2,1)S(1)}, bf16[896,32]{1,0:T(8,128)(2,1)}, u32[]{:S(2)}) copy-start(bf16[896,32]{1,0:T(8,128)(2,1)} %constant.90.clone) | copy-start | bytes 172036
  108.9 32.0 %copy-start.23 = (f32[896]{0:T(1024)S(1)}, f32[896]{0:T(1024)}, u32[]{:S(2)}) copy-start(f32[896]{0:T(1024)} %constant.89.clone) | copy-start | bytes 10756
  115.2 50.1 %collective-permute-start.24 = (bf16[208,4096]{1,0:T(8,128)(2,1)}, bf16[208,4096]{1,0:T(8,128)(2,1)S(1)}, u32[]{:S(2)}, u32[]{:S(2)}) collective-permute-start(bf16[208,4096]{1,0:T(8,128)(2,1)} %get-tuple-element.67), channel_id=1, source_target_pairs={{0,4},{1,5},{2,6},{3,7},{4,8},{5,9},{6,10},{7,11},{8,12},{9,13},{1... | collective-permute-start | bytes 5111816 | tf_op jit(solution)/shard_map/ppermute | solution.py:213
  116.9 49.7 %collective-permute-start.25 = (bf16[208,4096]{1,0:T(8,128)(2,1)}, bf16[208,4096]{1,0:T(8,128)(2,1)}, u32[]{:S(2)}, u32[]{:S(2)}) collective-permute-start(bf16[208,4096]{1,0:T(8,128)(2,1)} %get-tuple-element.68), channel_id=1, source_target_pairs={{0,12},{1,13},{2,14},{3,15},{4,0},{5,1},{6,2},{7,3},{8,4},{9,5},{1... | collective-permute-start | bytes 5111816 | tf_op jit(solution)/shard_map/ppermute | solution.py:213
  119.8 49.6 %collective-permute-start.26 = (bf16[208,4096]{1,0:T(8,128)(2,1)}, bf16[208,4096]{1,0:T(8,128)(2,1)}, u32[]{:S(2)}, u32[]{:S(2)}) collective-permute-start(bf16[208,4096]{1,0:T(8,128)(2,1)} %get-tuple-element.69), channel_id=1, source_target_pairs={{0,8},{1,9},{2,10},{3,11},{4,12},{5,13},{6,14},{7,15},{8,0},{9,1},... | collective-permute-start | bytes 5111816 | tf_op jit(solution)/shard_map/ppermute | solution.py:213
  138.2 22.3 %collective-permute-start.11 = (bf16[512,1024]{1,0:T(8,128)(2,1)}, bf16[512,1024]{1,0:T(8,128)(2,1)}, u32[]{:S(2)}, u32[]{:S(2)}) collective-permute-start(bf16[512,1024]{1,0:T(8,128)(2,1)} %collective-permute-done.7.refs_3_), channel_id=1, source_target_pairs={{32,0},{64,32},{96,64},{0,96},{33,1},{65,33},{97,65},{1,97},{34,2}... | collective-permute-start | bytes 3145736 | tf_op jit(solution)/shard_map/ppermute | solution.py:217
  139.0 21.6 %collective-permute-start.12 = (bf16[512,1024]{1,0:T(8,128)(2,1)}, bf16[512,1024]{1,0:T(8,128)(2,1)}, u32[]{:S(2)}, u32[]{:S(2)}) collective-permute-start(bf16[512,1024]{1,0:T(8,128)(2,1)} %collective-permute-done.8.refs_4_), channel_id=1, source_target_pairs={{0,32},{32,64},{64,96},{96,0},{1,33},{33,65},{65,97},{97,1},{2,34}... | collective-permute-start | bytes 3145736 | tf_op jit(solution)/shard_map/ppermute | solution.py:217
  149.2 16.2 %copy-start.2 = (bf16[896,32]{1,0:T(8,128)(2,1)S(1)}, bf16[896,32]{1,0:T(8,128)(2,1)}, u32[]{:S(2)}) copy-start(bf16[896,32]{1,0:T(8,128)(2,1)} %constant.88.clone) | copy-start | bytes 172036
  160.5 46.2 %collective-permute-start.14 = (bf16[208,4096]{1,0:T(8,128)(2,1)}, bf16[208,4096]{1,0:T(8,128)(2,1)}, u32[]{:S(2)}, u32[]{:S(2)}) collective-permute-start(bf16[208,4096]{1,0:T(8,128)(2,1)} %get-tuple-element.52), channel_id=1, source_target_pairs={{0,4},{1,5},{2,6},{3,7},{4,8},{5,9},{6,10},{7,11},{8,12},{9,13},{1... | collective-permute-start | bytes 5111816 | tf_op jit(solution)/shard_map/ppermute | solution.py:213
  160.6 46.1 %collective-permute-start.15 = (bf16[208,4096]{1,0:T(8,128)(2,1)}, bf16[208,4096]{1,0:T(8,128)(2,1)}, u32[]{:S(2)}, u32[]{:S(2)}) collective-permute-start(bf16[208,4096]{1,0:T(8,128)(2,1)} %get-tuple-element.53), channel_id=1, source_target_pairs={{0,12},{1,13},{2,14},{3,15},{4,0},{5,1},{6,2},{7,3},{8,4},{9,5},{1... | collective-permute-start | bytes 5111816 | tf_op jit(solution)/shard_map/ppermute | solution.py:213
  165.3 1.2 copy-start.14
  165.3 53.3 %collective-permute-start.4 = (bf16[208,4096]{1,0:T(8,128)(2,1)}, bf16[208,4096]{1,0:T(8,128)(2,1)}, u32[]{:S(2)}, u32[]{:S(2)}) collective-permute-start(bf16[208,4096]{1,0:T(8,128)(2,1)} %get-tuple-element.49), channel_id=1, source_target_pairs={{0,8},{1,9},{2,10},{3,11},{4,12},{5,13},{6,14},{7,15},{8,0},{9,1},... | collective-permute-start | bytes 5111816 | tf_op jit(solution)/shard_map/ppermute | solution.py:213
  166.5 25.4 %collective-permute-start.9 = (bf16[512,1024]{1,0:T(8,128)(2,1)}, bf16[512,1024]{1,0:T(8,128)(2,1)S(1)}, u32[]{:S(2)}, u32[]{:S(2)}) collective-permute-start(bf16[512,1024]{1,0:T(8,128)(2,1)} %collective-permute-done.7.refs_3_), channel_id=1, source_target_pairs={{0,32},{32,64},{64,96},{96,0},{1,33},{33,65},{65,97},{97,1},{2,34}... | collective-permute-start | bytes 3145736 | tf_op jit(solution)/shard_map/ppermute | solution.py:217
  169.4 24.7 %collective-permute-start.13 = (bf16[512,1024]{1,0:T(8,128)(2,1)}, bf16[512,1024]{1,0:T(8,128)(2,1)}, u32[]{:S(2)}, u32[]{:S(2)}) collective-permute-start(bf16[512,1024]{1,0:T(8,128)(2,1)} %collective-permute-done.11.refs_7_), channel_id=1, source_target_pairs={{32,0},{64,32},{96,64},{0,96},{33,1},{65,33},{97,65},{1,97},{34,2}... | collective-permute-start | bytes 3145736 | tf_op jit(solution)/shard_map/ppermute | solution.py:217
  191.9 1.0 copy-start.16
  192.9 34.5 %collective-permute-start.33 = (bf16[208,1024]{1,0:T(8,128)(2,1)}, bf16[208,1024]{1,0:T(8,128)(2,1)S(1)}, u32[]{:S(2)}, u32[]{:S(2)}) collective-permute-start(bf16[208,1024]{1,0:T(8,128)(2,1)} %get-tuple-element.72), channel_id=1, source_target_pairs={{4,0},{5,1},{6,2},{7,3},{8,4},{9,5},{10,6},{11,7},{12,8},{13,9},{1... | collective-permute-start | bytes 1277960 | tf_op jit(solution)/shard_map/ppermute | solution.py:213
  194.1 34.9 %collective-permute-start.34 = (bf16[208,1024]{1,0:T(8,128)(2,1)}, bf16[208,1024]{1,0:T(8,128)(2,1)S(1)}, u32[]{:S(2)}, u32[]{:S(2)}) collective-permute-start(bf16[208,1024]{1,0:T(8,128)(2,1)} %get-tuple-element.73), channel_id=1, source_target_pairs={{8,0},{9,1},{10,2},{11,3},{12,4},{13,5},{14,6},{15,7},{0,8},{1,9},... | collective-permute-start | bytes 1277960 | tf_op jit(solution)/shard_map/ppermute | solution.py:213
  206.7 22.3 %collective-permute-start.35 = (bf16[208,1024]{1,0:T(8,128)(2,1)}, bf16[208,1024]{1,0:T(8,128)(2,1)S(1)}, u32[]{:S(2)}, u32[]{:S(2)}) collective-permute-start(bf16[208,1024]{1,0:T(8,128)(2,1)} %get-tuple-element.74), channel_id=1, source_target_pairs={{12,0},{13,1},{14,2},{15,3},{0,4},{1,5},{2,6},{3,7},{4,8},{5,9},{6... | collective-permute-start | bytes 1277960 | tf_op jit(solution)/shard_map/ppermute | solution.py:213
  215.3 22.3 %collective-permute-start.16 = (bf16[208,1024]{1,0:T(8,128)(2,1)}, bf16[208,1024]{1,0:T(8,128)(2,1)S(1)}, u32[]{:S(2)}, u32[]{:S(2)}) collective-permute-start(bf16[208,1024]{1,0:T(8,128)(2,1)} %get-tuple-element.54), channel_id=1, source_target_pairs={{4,0},{5,1},{6,2},{7,3},{8,4},{9,5},{10,6},{11,7},{12,8},{13,9},{1... | collective-permute-start | bytes 1277960 | tf_op jit(solution)/shard_map/ppermute | solution.py:213
  218.6 20.0 %collective-permute-start.18 = (bf16[208,1024]{1,0:T(8,128)(2,1)}, bf16[208,1024]{1,0:T(8,128)(2,1)S(1)}, u32[]{:S(2)}, u32[]{:S(2)}) collective-permute-start(bf16[208,1024]{1,0:T(8,128)(2,1)} %get-tuple-element.56), channel_id=1, source_target_pairs={{12,0},{13,1},{14,2},{15,3},{0,4},{1,5},{2,6},{3,7},{4,8},{5,9},{6... | collective-permute-start | bytes 1277960 | tf_op jit(solution)/shard_map/ppermute | solution.py:213
  227.4 1.7 copy-start.5
  227.4 11.3 %collective-permute-start.17 = (bf16[208,1024]{1,0:T(8,128)(2,1)}, bf16[208,1024]{1,0:T(8,128)(2,1)S(1)}, u32[]{:S(2)}, u32[]{:S(2)}) collective-permute-start(bf16[208,1024]{1,0:T(8,128)(2,1)} %get-tuple-element.55), channel_id=1, source_target_pairs={{8,0},{9,1},{10,2},{11,3},{12,4},{13,5},{14,6},{15,7},{0,8},{1,9},... | collective-permute-start | bytes 1277960 | tf_op jit(solution)/shard_map/ppermute | solution.py:213
  229.0 0.8 copy-start.7
  229.0 0.9 copy-start.8
  232.6 12.0 %collective-permute-start.36 = (bf16[208,1024]{1,0:T(8,128)(2,1)}, bf16[208,1024]{1,0:T(8,128)(2,1)S(1)}, u32[]{:S(2)}, u32[]{:S(2)}) collective-permute-start(bf16[208,1024]{1,0:T(8,128)(2,1)} %get-tuple-element.76), channel_id=1, source_target_pairs={{1,0},{2,1},{3,2},{0,3},{5,4},{6,5},{7,6},{4,7},{9,8},{10,9},{11,1... | collective-permute-start | bytes 1277960 | tf_op jit(solution)/shard_map/ppermute | solution.py:213
  237.7 8.5 %collective-permute-start.37 = (bf16[208,1024]{1,0:T(8,128)(2,1)}, bf16[208,1024]{1,0:T(8,128)(2,1)S(1)}, u32[]{:S(2)}, u32[]{:S(2)}) collective-permute-start(bf16[208,1024]{1,0:T(8,128)(2,1)} %get-tuple-element.77), channel_id=1, source_target_pairs={{0,16},{1,17},{2,18},{3,19},{4,20},{5,21},{6,22},{7,23},{8,24},{9,... | collective-permute-start | bytes 1277960 | tf_op jit(solution)/shard_map/ppermute | solution.py:213
  237.7 1.0 copy-start.4
  237.7 10.5 %collective-permute-start.38 = (bf16[208,1024]{1,0:T(8,128)(2,1)}, bf16[208,1024]{1,0:T(8,128)(2,1)S(1)}, u32[]{:S(2)}, u32[]{:S(2)}) collective-permute-start(bf16[208,1024]{1,0:T(8,128)(2,1)} %get-tuple-element.78), channel_id=1, source_target_pairs={{1,16},{2,17},{3,18},{0,19},{5,20},{6,21},{7,22},{4,23},{9,24},{10... | collective-permute-start | bytes 1277960 | tf_op jit(solution)/shard_map/ppermute | solution.py:213
  238.6 0.8 copy-start.6
  238.6 0.9 copy-start.9
  242.2 13.4 %collective-permute-start.19 = (bf16[208,1024]{1,0:T(8,128)(2,1)}, bf16[208,1024]{1,0:T(8,128)(2,1)S(1)}, u32[]{:S(2)}, u32[]{:S(2)}) collective-permute-start(bf16[208,1024]{1,0:T(8,128)(2,1)} %get-tuple-element.58), channel_id=1, source_target_pairs={{3,0},{0,1},{1,2},{2,3},{7,4},{4,5},{5,6},{6,7},{11,8},{8,9},{9,10... | collective-permute-start | bytes 1277960 | tf_op jit(solution)/shard_map/ppermute | solution.py:213
  244.6 11.1 %collective-permute-start.20 = (bf16[208,1024]{1,0:T(8,128)(2,1)}, bf16[208,1024]{1,0:T(8,128)(2,1)S(1)}, u32[]{:S(2)}, u32[]{:S(2)}) collective-permute-start(bf16[208,1024]{1,0:T(8,128)(2,1)} %get-tuple-element.59), channel_id=1, source_target_pairs={{0,16},{1,17},{2,18},{3,19},{4,20},{5,21},{6,22},{7,23},{8,24},{9,... | collective-permute-start | bytes 1277960 | tf_op jit(solution)/shard_map/ppermute | solution.py:213
  244.6 3.6 %copy-start.17 = (bf16[208,1024]{1,0:T(8,128)(2,1)}, bf16[208,1024]{1,0:T(8,128)(2,1)S(1)}, u32[]{:S(2)}) copy-start(bf16[208,1024]{1,0:T(8,128)(2,1)S(1)} %collective-permute-done.36.refs_1_) | copy-start | bytes 1277956
  244.6 11.8 %collective-permute-start.21 = (bf16[208,1024]{1,0:T(8,128)(2,1)}, bf16[208,1024]{1,0:T(8,128)(2,1)S(1)}, u32[]{:S(2)}, u32[]{:S(2)}) collective-permute-start(bf16[208,1024]{1,0:T(8,128)(2,1)} %get-tuple-element.60), channel_id=1, source_target_pairs={{3,16},{0,17},{1,18},{2,19},{7,20},{4,21},{5,22},{6,23},{11,24},{8... | collective-permute-start | bytes 1277960 | tf_op jit(solution)/shard_map/ppermute | solution.py:213
  246.2 2.0 copy-start.18
  248.2 0.8 copy-start.19
  255.6 0.8 copy-start.20
  255.6 0.9 copy-start.21
  256.4 0.8 copy-start.22

commit v3 on v2

--- a/solution.py
+++ b/solution.py
@@ -14,7 +14,7 @@
 PLANE = ("core", "y", "x")
 SETS = (((0, 0), (1, 1)), ((0, -1), (-1, 2)))
 BLOCKS = SETS[0] + SETS[1]
-EXPERT_CALLS = (((1, 3, 2, 0),), ((1, 3), (2, 0)))
+EXPERT_CALLS = (((1, 3, 2, 0),), ((1, 3, 2, 0),))
 INTERPRET = False
 
 
@@ -55,12 +55,7 @@
     rest = SIDE * main
     for j, target in enumerate(outs):
         tail = [source[rest + j * LOOSE : rest + (j + 1) * LOOSE] for source in ins]
-        target[rest:] = jnp.concatenate(tail + [source_pad(target, rest)], axis=0)
-
-
-def source_pad(target, rest):
-    rows = target.shape[0] - rest - SIDE * LOOSE
-    return jnp.zeros((rows, target.shape[1]), target.dtype)
+        target[rest:] = jnp.concatenate(tail, axis=0)
 
 
 def regroup(arrays, main):
@@ -83,6 +78,7 @@
 def dispatch_kernel(spread_ref, row_slot_ref, slot_ref, tokens_ref, *refs):
     outs, pick_ref = refs[:-1], refs[-1]
     length = outs[0].shape[0]
+    stride = pick_ref.shape[0] // len(outs)
 
     @pl.when(pl.program_id(0) == 0)
     def _():
@@ -91,14 +87,14 @@
 
     values = tokens_ref[...]
     for i, out in enumerate(outs):
-        rows = pick_ref[i * length : (i + 1) * length]
-        out[...] = jnp.dot(rows, values, preferred_element_type=jnp.float32).astype(out.dtype)
-
-
-def dispatch(spread, row_slot, slot, tokens, messages):
+        rows = pick_ref[i * stride : (i + 1) * stride]
+        block = jnp.dot(rows, values, preferred_element_type=jnp.float32)
+        out[...] = block[:length].astype(out.dtype)
+
+
+def dispatch(spread, row_slot, slot, tokens, messages, length):
     count, width = tokens.shape
     total = spread.shape[0]
-    length = total // messages
     step = min(width, 1024)
     return pl.pallas_call(
         dispatch_kernel,
@@ -123,17 +119,18 @@
 
 
 def expert_kernel(count, place_ref, *refs):
-    values, parts, outs = refs[:count], refs[count : count + PARTS], refs[count + PARTS :]
+    values, parts = refs[:count], refs[count : count + PARTS]
+    outs, whole_ref = refs[count + PARTS : -1], refs[-1]
     place, core = place_ref[0], place_ref[1]
     half = parts[0].shape[0]
+    for i, part in enumerate(parts):
+        side = core if i % 2 == 0 else 1 - core
+        start = (lax.rem(place + SHIFTS[i // 2], SIDE) * 2 + side) * half
+        whole_ref[pl.ds(pl.multiple_of(start, half), half)] = part[...]
     for value, out in zip(values, outs):
-        total = jnp.zeros(out.shape, jnp.float32)
-        for i, part in enumerate(parts):
-            side = core if i % 2 == 0 else 1 - core
-            start = (lax.rem(place + SHIFTS[i // 2], SIDE) * 2 + side) * half
-            span = pl.ds(pl.multiple_of(start, half), half)
-            total += jnp.dot(value[:, span], part[...], preferred_element_type=jnp.float32)
-        out[...] = total.astype(out.dtype)
+        out[...] = jnp.dot(
+            value[...], whole_ref[...], preferred_element_type=jnp.float32
+        ).astype(out.dtype)
 
 
 def expert(place, values, parts):
@@ -149,6 +146,7 @@
         in_specs=[pl.BlockSpec(memory_space=pltpu.SMEM)] + [left] * len(values) + [right] * PARTS,
         out_specs=[result] * len(values),
         out_shape=[jax.ShapeDtypeStruct((rows, hidden), values[0].dtype)] * len(values),
+        scratch_shapes=[pltpu.VMEM((width, step), values[0].dtype)],
         cost_estimate=pl.CostEstimate(
             flops=2 * len(values) * rows * width * hidden,
             bytes_accessed=2 * (len(values) * rows * (width + hidden) + width * hidden),
@@ -159,33 +157,32 @@
     )(place, *values, *parts)
 
 
-def combine_kernel(count, hi_ref, lo_ref, *refs):
+def combine_kernel(count, share_ref, *refs):
     blocks, base, out_ref, rows_ref = refs[:count], refs[count:-2], refs[-2], refs[-1]
     rows = blocks[0].shape[0]
+    stride = -(-rows // 16) * 16
+    rows_ref[...] = jnp.zeros_like(rows_ref)
     for i, block in enumerate(blocks):
-        rows_ref[i * rows : (i + 1) * rows] = block[...]
-    used = count * rows
-    if used < rows_ref.shape[0]:
-        rows_ref[used:] = jnp.zeros((rows_ref.shape[0] - used, rows_ref.shape[1]), rows_ref.dtype)
-    values = rows_ref[...]
-    total = jnp.dot(hi_ref[...], values, preferred_element_type=jnp.float32)
-    total += jnp.dot(lo_ref[...], values, preferred_element_type=jnp.float32)
+        rows_ref[i * stride : i * stride + rows] = block[...]
+    both = jnp.dot(share_ref[...], rows_ref[...], preferred_element_type=jnp.float32)
+    tokens = out_ref.shape[0]
+    total = both[:tokens] + both[tokens:]
     for other in base:
         total += other[...]
     out_ref[...] = total.astype(out_ref.dtype)
 
 
-def combine(hi, lo, blocks, base, dtype):
-    count, depth = hi.shape
+def combine(share, blocks, base, dtype):
+    depth = share.shape[1]
+    count = share.shape[0] // 2
     hidden = blocks[0].shape[1]
     step = min(hidden, 256)
-    left = pl.BlockSpec((count, depth), lambda i: (0, 0))
     right = pl.BlockSpec((blocks[0].shape[0], step), lambda i: (0, i))
     sums = pl.BlockSpec((count, step), lambda i: (0, i))
     return pl.pallas_call(
         functools.partial(combine_kernel, len(blocks)),
         grid=(hidden // step,),
-        in_specs=[left, left] + [right] * len(blocks) + [sums] * len(base),
+        in_specs=[pl.BlockSpec(share.shape, lambda i: (0, 0))] + [right] * len(blocks) + [sums] * len(base),
         out_specs=sums,
         out_shape=jax.ShapeDtypeStruct((count, hidden), dtype),
         scratch_shapes=[pltpu.VMEM((depth, step), blocks[0].dtype)],
@@ -196,7 +193,7 @@
         ),
         interpret=INTERPRET,
         name="combine",
-    )(hi, lo, *blocks, *base)
+    )(share, *blocks, *base)
 
 
 def expert_order(kind):
@@ -286,7 +283,7 @@
     for group in ((1, 3), (0, 2)):
         spread, row_slot = layout(group, 1, len(group) * length)
         for q, (table, values) in enumerate(((slot[:mine], tokens), (other_slot, other_tokens))):
-            blocks = dispatch(spread, row_slot[:, None], table, values, len(group))
+            blocks = dispatch(spread, row_slot[:, None], table, values, len(group), used)
             for b, block in zip(group, blocks):
                 shift = BLOCKS[b][0]
                 if shift:
@@ -307,7 +304,7 @@
                 part.astype(jnp.bfloat16), spread, turned, preferred_element_type=jnp.float32
             )
             share.append(jnp.where(at_row == row_slot[None, :], part, 0.0).astype(jnp.bfloat16))
-        shares.append(share)
+        shares.append(jnp.concatenate(share))
 
     total = ()
     for s in range(len(SETS)):
@@ -322,8 +319,14 @@
             outs.update(zip(group, expert(place, [turns[t] for t in group], parts[s])))
         for turn in (1, 3, 2):
             outs[turn] = move(outs[turn], back(pairs(0, turn)))
+        grouped = regroup([outs[t] for t in range(SIDE)], main)
+        if s == 0:
+            first_members, early = members, grouped
+        else:
+            finish = ((0, first_members, early), (1, members, grouped))
+    for s, members, grouped in finish:
         blocks = {}
-        for (q, b), block in zip(members, regroup([outs[t] for t in range(SIDE)], main)):
+        for (q, b), block in zip(members, grouped):
             moves = back(pairs(BLOCKS[b][0], 0))
             if q:
                 moves = crossed(moves)
@@ -332,7 +335,7 @@
             blocks[q, b] = block
         ordered = [blocks[q, s * per_set + i] for q in range(CORES) for i in range(per_set)]
         last = s == len(SETS) - 1
-        total = (combine(*shares[s], ordered, total, jnp.bfloat16 if last else jnp.float32),)
+        total = (combine(shares[s], ordered, total, jnp.bfloat16 if last else jnp.float32),)
     return total[0]
 
 

time: 269 us -> 277 us (1.030)
  the two profiles are of different devices: /device:TPU:64 before, /device:TPU:2 now
where the time goes in v3:
time: 277 us; the launch traced here: 276 us
  waiting for transfers between devices  126 us (45%)
  Pallas kernels  83.5 us (30%)
  starting transfers between devices  46.3 us (17%)
  local copies, waits for them, and re-layouts  8.13 us (3%)
  matrix products  7.61 us (3%)
  other arithmetic  3.93 us (1%)
    ppermute x15, waiting for transfers between devices, across(): return lax.ppermute(array, axis, moves)  91.3 us
    ppermute x24, waiting for transfers between devices, move(): return lax.ppermute(array, PLANE, moves)  34.9 us
    ppermute x24, starting transfers between devices, move(): return lax.ppermute(array, PLANE, moves)  29.1 us
    pallas_call x4, Pallas kernels, dispatch(): pl.pallas_call(dispatch_kernel, grid=(width // step,), in_specs=[pl.Block...  26.3 us
    pallas_call x2, Pallas kernels, expert(): pl.pallas_call(functools.partial(expert_kernel, len(values)), grid=(hidde...  26.1 us
    pallas_call x4, Pallas kernels, regroup(): pl.pallas_call(functools.partial(regroup_kernel, main), grid=(width // st...  17.5 us
    ppermute x15, starting transfers between devices, across(): return lax.ppermute(array, axis, moves)  17.2 us
    pallas_call x2, Pallas kernels, combine(): pl.pallas_call(functools.partial(combine_kernel, len(blocks)), grid=(hidd...  13.7 us
  transfers between devices with their start and end apart: 39, of which 13 were waited for; matrix products, arithmetic and copies ran while one was open for 5% of the time, Pallas kernels for 28%

profile of v3, /device:TPU:2, one launch (start us, length us, event | category | flops | bytes accessed | tf_op | source)
XLA Modules:
  0.0 275.9 jit_solution(4811723541745576951)
XLA Ops:
  0.0 2.7 dynamic-slice_bitcast_fusion
  2.7 0.5 collective-permute-start.8
  3.7 0.6 slice.33.slot_ref
  4.3 6.6 %dispatch.6 = (bf16[200,4096]{1,0:T(8,128)(2,1)}, bf16[200,4096]{1,0:T(8,128)(2,1)}) custom-call(bf16[416,16]{1,0:T(8,128)(2,1)} %constant.85.clone.spread_ref, f32[416,1]{1,0:T(8,128)} %constant.92.row_slot_ref, bf16[16,640]{1,0:T(8,128)(2,1)} %slice.33.slot_ref, bf16[640,4096]{1,0:T(8,128)(2,1)} %tokens_ref.3), custom_call_target="tpu_custom_call" | custom-call | flops 2181038080 | bytes 8650752 | tf_op jit(solution)/shard_map/dispatch/pallas_call | solution.py:99
  10.9 1.5 collective-permute-start.22
  12.5 2.0 collective-permute-start.27
  14.5 3.2 %collective-permute-start.29 = (bf16[512,1024]{1,0:T(8,128)(2,1)}, bf16[512,1024]{1,0:T(8,128)(2,1)}, u32[]{:S(2)}, u32[]{:S(2)}) collective-permute-start(bf16[512,1024]{1,0:T(8,128)(2,1)} %get-tuple-element.82.refs_4_), channel_id=1, source_target_pairs={{32,0},{64,32},{96,64},{0,96},{33,1},{65,33},{97,65},{1,97},{34,2}... | collective-permute-start | bytes 3145736 | tf_op jit(solution)/shard_map/ppermute | solution.py:214
  17.7 0.5 collective-permute-start.2
  18.2 1.5 collective-permute-start.7
  19.8 0.8 fusion.7.slot_ref
  20.6 6.6 %dispatch.7 = (bf16[200,4096]{1,0:T(8,128)(2,1)}, bf16[200,4096]{1,0:T(8,128)(2,1)}) custom-call(bf16[416,16]{1,0:T(8,128)(2,1)} %constant.85.clone.spread_ref, f32[416,1]{1,0:T(8,128)} %constant.92.row_slot_ref, bf16[16,640]{1,0:T(8,128)(2,1)} %fusion.7.slot_ref, bf16[640,4096]{1,0:T(8,128)(2,1)} %collective-permute-done.1.tokens_ref), custom_call_target="tpu_custom_call" | custom-call | flops 2181038080 | bytes 8650752 | tf_op jit(solution)/shard_map/dispatch/pallas_call | solution.py:99
  27.2 13.5 %collective-permute-done.27.refs_6_ = bf16[512,1024]{1,0:T(8,128)(2,1)} collective-permute-done((bf16[512,1024]{1,0:T(8,128)(2,1)}, bf16[512,1024]{1,0:T(8,128)(2,1)}, u32[]{:S(2)}, u32[]{:S(2)}) %collective-permute-start.27) | collective-permute-done | bytes 1048608 | tf_op jit(solution)/shard_map/ppermute | solution.py:214
  40.7 1.2 collective-permute-start.23
  41.9 2.6 collective-permute-start.30
  44.5 1.0 collective-permute-start.31
  45.5 1.9 collective-permute-start.28
  47.4 1.5 collective-permute-start.9
  48.9 18.3 %collective-permute-done.30.refs_9_ = bf16[512,1024]{1,0:T(8,128)(2,1)} collective-permute-done((bf16[512,1024]{1,0:T(8,128)(2,1)}, bf16[512,1024]{1,0:T(8,128)(2,1)}, u32[]{:S(2)}, u32[]{:S(2)}) %collective-permute-start.30) | collective-permute-done | bytes 1048608 | tf_op jit(solution)/shard_map/ppermute | solution.py:214
  67.2 0.5 collective-permute-start.3
  67.7 4.3 %collective-permute-done.31.refs_10_ = bf16[512,1024]{1,0:T(8,128)(2,1)} collective-permute-done((bf16[512,1024]{1,0:T(8,128)(2,1)}, bf16[512,1024]{1,0:T(8,128)(2,1)}, u32[]{:S(2)}, u32[]{:S(2)}) %collective-permute-start.31) | collective-permute-done | bytes 1048608 | tf_op jit(solution)/shard_map/ppermute | solution.py:214
  72.0 22.5 %collective-permute-done.28.refs_7_ = bf16[512,1024]{1,0:T(8,128)(2,1)} collective-permute-done((bf16[512,1024]{1,0:T(8,128)(2,1)}, bf16[512,1024]{1,0:T(8,128)(2,1)}, u32[]{:S(2)}, u32[]{:S(2)}) %collective-permute-start.28) | collective-permute-done | bytes 1048608 | tf_op jit(solution)/shard_map/ppermute | solution.py:214
  94.5 1.9 collective-permute-start.12
  96.8 6.6 %dispatch.4 = (bf16[200,4096]{1,0:T(8,128)(2,1)}, bf16[200,4096]{1,0:T(8,128)(2,1)}) custom-call(bf16[416,16]{1,0:T(8,128)(2,1)} %constant.87.clone.spread_ref, f32[416,1]{1,0:T(8,128)} %constant.92.row_slot_ref, bf16[16,640]{1,0:T(8,128)(2,1)} %slice.33.slot_ref, bf16[640,4096]{1,0:T(8,128)(2,1)} %tokens_ref.3), custom_call_target="tpu_custom_call" | custom-call | flops 2181038080 | bytes 8650752 | tf_op jit(solution)/shard_map/dispatch/pallas_call | solution.py:99
  103.4 6.6 %dispatch.5 = (bf16[200,4096]{1,0:T(8,128)(2,1)}, bf16[200,4096]{1,0:T(8,128)(2,1)}) custom-call(bf16[416,16]{1,0:T(8,128)(2,1)} %constant.87.clone.spread_ref, f32[416,1]{1,0:T(8,128)} %constant.92.row_slot_ref, bf16[16,640]{1,0:T(8,128)(2,1)} %fusion.7.slot_ref, bf16[640,4096]{1,0:T(8,128)(2,1)} %collective-permute-done.1.tokens_ref), custom_call_target="tpu_custom_call" | custom-call | flops 2181038080 | bytes 8650752 | tf_op jit(solution)/shard_map/dispatch/pallas_call | solution.py:99
  110.0 6.1 %regroup.6 = (bf16[200,4096]{1,0:T(8,128)(2,1)}, bf16[200,4096]{1,0:T(8,128)(2,1)}, bf16[200,4096]{1,0:T(8,128)(2,1)}, bf16[200,4096]{1,0:T(8,128)(2,1)}) custom-call(bf16[200,4096]{1,0:T(8,128)(2,1)} %get-tuple-element.59.refs_0_, bf16[200,4096]{1,0:T(8,128)(2,1)} %get-tuple-element.60.refs_1_, bf16[200,4096]{1,0:T(8,128)(2,1)} %copy-done.1, ...), custom_call_target="tpu_custom_call" | custom-call | flops 6553600 | bytes 13107200 | tf_op jit(solution)/shard_map/regroup/pallas_call | solution.py:66
  116.1 1.6 collective-permute-start.24
  118.1 2.8 %collective-permute-done.12.refs_8_ = bf16[512,1024]{1,0:T(8,128)(2,1)} collective-permute-done((bf16[512,1024]{1,0:T(8,128)(2,1)}, bf16[512,1024]{1,0:T(8,128)(2,1)}, u32[]{:S(2)}, u32[]{:S(2)}) %collective-permute-start.12) | collective-permute-done | bytes 1048608 | tf_op jit(solution)/shard_map/ppermute | solution.py:214
  120.8 22.5 %collective-permute-done.32.refs_11_ = bf16[512,1024]{1,0:T(8,128)(2,1)} collective-permute-done((bf16[512,1024]{1,0:T(8,128)(2,1)}, bf16[512,1024]{1,0:T(8,128)(2,1)}, u32[]{:S(2)}, u32[]{:S(2)}) %collective-permute-start.32) | collective-permute-done | bytes 1048608 | tf_op jit(solution)/shard_map/ppermute | solution.py:214
  143.3 3.0 %collective-permute-start.25 = (bf16[200,4096]{1,0:T(8,128)(2,1)}, bf16[200,4096]{1,0:T(8,128)(2,1)}, u32[]{:S(2)}, u32[]{:S(2)}) collective-permute-start(bf16[200,4096]{1,0:T(8,128)(2,1)} %get-tuple-element.64), channel_id=1, source_target_pairs={{0,12},{1,13},{2,14},{3,15},{4,0},{5,1},{6,2},{7,3},{8,4},{9,5},{1... | collective-permute-start | bytes 4915208 | tf_op jit(solution)/shard_map/ppermute | solution.py:210
  146.3 0.6 collective-permute-start.26
  147.0 0.5 convolution_compare_fusion
  147.5 1.3 convolution_compare_fusion.1
  148.8 0.6 select_convert_fusion
  149.4 0.6 select_convert_fusion.1
  150.0 6.1 %regroup.4 = (bf16[200,4096]{1,0:T(8,128)(2,1)}, bf16[200,4096]{1,0:T(8,128)(2,1)}, bf16[200,4096]{1,0:T(8,128)(2,1)}, bf16[200,4096]{1,0:T(8,128)(2,1)}) custom-call(bf16[200,4096]{1,0:T(8,128)(2,1)} %get-tuple-element.42.refs_0_, bf16[200,4096]{1,0:T(8,128)(2,1)} %get-tuple-element.43.refs_1_, bf16[200,4096]{1,0:T(8,128)(2,1)} %copy-done, ...), custom_call_target="tpu_custom_call" | custom-call | flops 6553600 | bytes 13107200 | tf_op jit(solution)/shard_map/regroup/pallas_call | solution.py:66
  156.1 7.5 %collective-permute-done.13.refs_9_ = bf16[512,1024]{1,0:T(8,128)(2,1)} collective-permute-done((bf16[512,1024]{1,0:T(8,128)(2,1)}, bf16[512,1024]{1,0:T(8,128)(2,1)}, u32[]{:S(2)}, u32[]{:S(2)}) %collective-permute-start.13) | collective-permute-done | bytes 1048608 | tf_op jit(solution)/shard_map/ppermute | solution.py:214
  163.6 3.2 %collective-permute-start.5 = (bf16[200,4096]{1,0:T(8,128)(2,1)}, bf16[200,4096]{1,0:T(8,128)(2,1)}, u32[]{:S(2)}, u32[]{:S(2)}) collective-permute-start(bf16[200,4096]{1,0:T(8,128)(2,1)} %get-tuple-element.47), channel_id=1, source_target_pairs={{0,12},{1,13},{2,14},{3,15},{4,0},{5,1},{6,2},{7,3},{8,4},{9,5},{1... | collective-permute-start | bytes 4915208 | tf_op jit(solution)/shard_map/ppermute | solution.py:210
  166.9 1.8 select_convert_fusion.3
  168.7 1.8 select_convert_fusion.2
  170.4 1.6 pad_maximum_fusion.1.share_ref
  172.0 10.8 %collective-permute-done.25.refs_1_ = bf16[200,4096]{1,0:T(8,128)(2,1)} collective-permute-done((bf16[200,4096]{1,0:T(8,128)(2,1)}, bf16[200,4096]{1,0:T(8,128)(2,1)}, u32[]{:S(2)}, u32[]{:S(2)}) %collective-permute-start.25) | collective-permute-done | bytes 1638432 | tf_op jit(solution)/shard_map/ppermute | solution.py:210
  182.8 3.2 %collective-permute-start.15 = (bf16[512,1024]{1,0:T(8,128)(2,1)}, bf16[512,1024]{1,0:T(8,128)(2,1)S(1)}, u32[]{:S(2)}, u32[]{:S(2)}) collective-permute-start(bf16[512,1024]{1,0:T(8,128)(2,1)} %collective-permute-done.13.refs_9_), channel_id=1, source_target_pairs={{32,0},{64,32},{96,64},{0,96},{33,1},{65,33},{97,65},{1,97},{34,2}... | collective-permute-start | bytes 3145736 | tf_op jit(solution)/shard_map/ppermute | solution.py:214
  186.1 0.7 pad_add_fusion.place_ref
  186.7 1.6 pad_maximum_fusion.share_ref
  188.3 13.1 %expert.3 = (bf16[200,1024]{1,0:T(8,128)(2,1)}, bf16[200,1024]{1,0:T(8,128)(2,1)}, bf16[200,1024]{1,0:T(8,128)(2,1)}, bf16[200,1024]{1,0:T(8,128)(2,1)}) custom-call(s32[2]{0:T(128)} %pad_add_fusion.place_ref, bf16[200,4096]{1,0:T(8,128)(2,1)} %collective-permute-done.24.refs_0_, bf16[200,4096]{1,0:T(8,128)(2,1)} %collective-permute-done.25.refs_1_, ...), custom_call_target="tpu_custom_call" | custom-call | flops 6710886400 | bytes 16580608 | tf_op jit(solution)/shard_map/expert/pallas_call | solution.py:143
  201.4 1.0 copy-done.14
  202.3 3.7 %collective-permute-start.33 = (bf16[200,1024]{1,0:T(8,128)(2,1)}, bf16[200,1024]{1,0:T(8,128)(2,1)S(1)}, u32[]{:S(2)}, u32[]{:S(2)}) collective-permute-start(bf16[200,1024]{1,0:T(8,128)(2,1)} %get-tuple-element.68), channel_id=1, source_target_pairs={{4,0},{5,1},{6,2},{7,3},{8,4},{9,5},{10,6},{11,7},{12,8},{13,9},{1... | collective-permute-start | bytes 1228808 | tf_op jit(solution)/shard_map/ppermute | solution.py:210
  206.0 0.4 collective-permute-start.34
  206.5 0.6 copy-done.15
  207.1 10.9 %collective-permute-done.5.refs_1_ = bf16[200,4096]{1,0:T(8,128)(2,1)} collective-permute-done((bf16[200,4096]{1,0:T(8,128)(2,1)}, bf16[200,4096]{1,0:T(8,128)(2,1)}, u32[]{:S(2)}, u32[]{:S(2)}) %collective-permute-start.5) | collective-permute-done | bytes 1638432 | tf_op jit(solution)/shard_map/ppermute | solution.py:210
  217.9 13.0 %expert.2 = (bf16[200,1024]{1,0:T(8,128)(2,1)}, bf16[200,1024]{1,0:T(8,128)(2,1)}, bf16[200,1024]{1,0:T(8,128)(2,1)}, bf16[200,1024]{1,0:T(8,128)(2,1)}) custom-call(s32[2]{0:T(128)} %pad_add_fusion.place_ref, bf16[200,4096]{1,0:T(8,128)(2,1)} %collective-permute-done.4.refs_0_, bf16[200,4096]{1,0:T(8,128)(2,1)} %collective-permute-done.5.refs_1_, ...), custom_call_target="tpu_custom_call" | custom-call | flops 6710886400 | bytes 16580608 | tf_op jit(solution)/shard_map/expert/pallas_call | solution.py:143
  231.0 3.8 %collective-permute-start.16 = (bf16[200,1024]{1,0:T(8,128)(2,1)}, bf16[200,1024]{1,0:T(8,128)(2,1)S(1)}, u32[]{:S(2)}, u32[]{:S(2)}) collective-permute-start(bf16[200,1024]{1,0:T(8,128)(2,1)} %get-tuple-element.51), channel_id=1, source_target_pairs={{4,0},{5,1},{6,2},{7,3},{8,4},{9,5},{10,6},{11,7},{12,8},{13,9},{1... | collective-permute-start | bytes 1228808 | tf_op jit(solution)/shard_map/ppermute | solution.py:210
  234.8 0.6 collective-permute-start.17
  236.6 2.6 regroup.7
  239.2 1.7 collective-permute-start.36
  240.9 7.4 %collective-permute-done.16.refs_1_ = bf16[200,1024]{1,0:T(8,128)(2,1)S(1)} collective-permute-done((bf16[200,1024]{1,0:T(8,128)(2,1)}, bf16[200,1024]{1,0:T(8,128)(2,1)S(1)}, u32[]{:S(2)}, u32[]{:S(2)}) %collective-permute-start.16) | collective-permute-done | bytes 409632 | tf_op jit(solution)/shard_map/ppermute | solution.py:210
  248.3 0.5 collective-permute-done.18.refs_3_
  249.6 2.6 regroup.5
  252.2 1.4 collective-permute-start.19
  253.6 1.8 collective-permute-start.20
  256.6 6.7 %combine.2.refs_4_ = f32[640,1024]{1,0:T(8,128)} custom-call(bf16[1280,896]{1,0:T(8,128)(2,1)} %pad_maximum_fusion.share_ref, bf16[200,1024]{1,0:T(8,128)(2,1)} %get-tuple-element.71.refs_0_, bf16[200,1024]{1,0:T(8,128)(2,1)} %copy-done.16, bf16[200,1024]{1,0:T(8,128)(2,1)} %copy-done.17, bf16[200,1024]{1,0:T(8,128)(2,1)} %copy-done.18), custom_call_target="tpu_custom_call" | custom-call | flops 2348810240 | bytes 6750208 | tf_op jit(solution)/shard_map/combine/pallas_call | solution.py:182
  263.4 4.9 %collective-permute-done.21.refs_3_ = bf16[200,1024]{1,0:T(8,128)(2,1)S(1)} collective-permute-done((bf16[200,1024]{1,0:T(8,128)(2,1)}, bf16[200,1024]{1,0:T(8,128)(2,1)S(1)}, u32[]{:S(2)}, u32[]{:S(2)}) %collective-permute-start.21) | collective-permute-done | bytes 409632 | tf_op jit(solution)/shard_map/ppermute | solution.py:210
  268.2 0.8 copy-done.21
  269.0 6.9 %combine.3 = bf16[640,1024]{1,0:T(8,128)(2,1)} custom-call(bf16[1280,896]{1,0:T(8,128)(2,1)} %pad_maximum_fusion.1.share_ref, bf16[200,1024]{1,0:T(8,128)(2,1)} %get-tuple-element.54.refs_0_, bf16[200,1024]{1,0:T(8,128)(2,1)} %copy-done.19, bf16[200,1024]{1,0:T(8,128)(2,1)} %copy-done.20, bf16[200,1024]{1,0:T(8,128)(2,1)} %copy-done.21, ...), custom_call_target="tpu_custom_call" | custom-call | flops 2348810240 | bytes 6750208 | tf_op jit(solution)/shard_map/combine/pallas_call | solution.py:182
  (91 shorter events, 4.6 us)
Async XLA Ops:
  0.0 18.2 %collective-permute-start.1 = (bf16[640,4096]{1,0:T(8,128)(2,1)}, bf16[640,4096]{1,0:T(8,128)(2,1)}, u32[]{:S(2)}, u32[]{:S(2)}) collective-permute-start(bf16[640,4096]{1,0:T(8,128)(2,1)} %tokens_ref.3), channel_id=1, source_target_pairs={{0,16},{16,0},{1,17},{17,1},{2,18},{18,2},{3,19},{19,3},{4,20},{20... | collective-permute-start | bytes 15728648 | tf_op jit(solution)/shard_map/ppermute | solution.py:214
  0.0 3.3 %copy-start.11 = (s32[640,2]{0,1:T(2,128)S(1)}, s32[640,2]{0,1:T(2,128)}, u32[]{:S(2)}) copy-start(s32[640,2]{0,1:T(2,128)} %param.17) | copy-start | bytes 15364
  0.0 3.3 %copy-start.10 = (f32[640,2]{0,1:T(2,128)S(1)}, f32[640,2]{0,1:T(2,128)}, u32[]{:S(2)}) copy-start(f32[640,2]{0,1:T(2,128)} %param.18) | copy-start | bytes 15364
  0.0 3.3 %copy-start.12 = (s32[16]{0:T(128)S(1)}, s32[16]{0:T(128)}, u32[]{:S(2)}) copy-start(s32[16]{0:T(128)} %constant.83.clone) | copy-start | bytes 196
  0.0 3.3 %copy-start.13 = (s32[16]{0:T(128)S(1)}, s32[16]{0:T(128)}, u32[]{:S(2)}) copy-start(s32[16]{0:T(128)} %constant.84.clone) | copy-start | bytes 196
  2.7 15.0 %collective-permute-start.8 = (bf16[512,1024]{1,0:T(8,128)(2,1)S(1)}, bf16[512,1024]{1,0:T(8,128)(2,1)}, u32[]{:S(2)}, u32[]{:S(2)}) collective-permute-start(bf16[512,1024]{1,0:T(8,128)(2,1)S(1)} %get-tuple-element.81), channel_id=1, source_target_pairs={{0,16},{16,0},{1,17},{17,1},{2,18},{18,2},{3,19},{19,3},{4,20},{20... | collective-permute-start | bytes 3145736 | tf_op jit(solution)/shard_map/ppermute | solution.py:214
  10.9 34.6 %collective-permute-start.22 = (bf16[200,4096]{1,0:T(8,128)(2,1)}, bf16[200,4096]{1,0:T(8,128)(2,1)S(1)}, u32[]{:S(2)}, u32[]{:S(2)}) collective-permute-start(bf16[200,4096]{1,0:T(8,128)(2,1)} %get-tuple-element.61), channel_id=1, source_target_pairs={{0,1},{1,2},{2,3},{3,0},{4,5},{5,6},{6,7},{7,4},{8,9},{9,10},{10,1... | collective-permute-start | bytes 4915208 | tf_op jit(solution)/shard_map/ppermute | solution.py:210
  12.4 2.1 collective-permute-start
  12.5 28.2 %collective-permute-start.27 = (bf16[512,1024]{1,0:T(8,128)(2,1)}, bf16[512,1024]{1,0:T(8,128)(2,1)}, u32[]{:S(2)}, u32[]{:S(2)}) collective-permute-start(bf16[512,1024]{1,0:T(8,128)(2,1)} %get-tuple-element.82.refs_4_), channel_id=1, source_target_pairs={{0,32},{32,64},{64,96},{96,0},{1,33},{33,65},{65,97},{97,1},{2,34}... | collective-permute-start | bytes 3145736 | tf_op jit(solution)/shard_map/ppermute | solution.py:214
  14.5 27.4 %collective-permute-start.29 = (bf16[512,1024]{1,0:T(8,128)(2,1)}, bf16[512,1024]{1,0:T(8,128)(2,1)}, u32[]{:S(2)}, u32[]{:S(2)}) collective-permute-start(bf16[512,1024]{1,0:T(8,128)(2,1)} %get-tuple-element.82.refs_4_), channel_id=1, source_target_pairs={{32,0},{64,32},{96,64},{0,96},{33,1},{65,33},{97,65},{1,97},{34,2}... | collective-permute-start | bytes 3145736 | tf_op jit(solution)/shard_map/ppermute | solution.py:214
  17.7 29.7 %collective-permute-start.2 = (bf16[200,4096]{1,0:T(8,128)(2,1)}, bf16[200,4096]{1,0:T(8,128)(2,1)S(1)}, u32[]{:S(2)}, u32[]{:S(2)}) collective-permute-start(bf16[200,4096]{1,0:T(8,128)(2,1)} %get-tuple-element.44), channel_id=1, source_target_pairs={{0,3},{1,0},{2,1},{3,2},{4,7},{5,4},{6,5},{7,6},{8,11},{9,8},{10,9... | collective-permute-start | bytes 4915208 | tf_op jit(solution)/shard_map/ppermute | solution.py:210
  18.2 26.2 %collective-permute-start.7 = (bf16[512,1024]{1,0:T(8,128)(2,1)}, bf16[512,1024]{1,0:T(8,128)(2,1)}, u32[]{:S(2)}, u32[]{:S(2)}) collective-permute-start(bf16[512,1024]{1,0:T(8,128)(2,1)} %get-tuple-element.82.refs_4_), channel_id=1, source_target_pairs={{0,1},{1,2},{2,3},{3,0},{4,5},{5,6},{6,7},{7,4},{8,9},{9,10},{10,1... | collective-permute-start | bytes 3145736 | tf_op jit(solution)/shard_map/ppermute | solution.py:210
  40.7 55.8 %collective-permute-start.23 = (bf16[200,4096]{1,0:T(8,128)(2,1)}, bf16[200,4096]{1,0:T(8,128)(2,1)}, u32[]{:S(2)}, u32[]{:S(2)}) collective-permute-start(bf16[200,4096]{1,0:T(8,128)(2,1)} %get-tuple-element.62), channel_id=1, source_target_pairs={{0,1},{1,2},{2,3},{3,0},{4,5},{5,6},{6,7},{7,4},{8,9},{9,10},{10,1... | collective-permute-start | bytes 4915208 | tf_op jit(solution)/shard_map/ppermute | solution.py:210
  41.9 25.3 %collective-permute-start.30 = (bf16[512,1024]{1,0:T(8,128)(2,1)}, bf16[512,1024]{1,0:T(8,128)(2,1)}, u32[]{:S(2)}, u32[]{:S(2)}) collective-permute-start(bf16[512,1024]{1,0:T(8,128)(2,1)} %collective-permute-done.8.refs_5_), channel_id=1, source_target_pairs={{32,0},{64,32},{96,64},{0,96},{33,1},{65,33},{97,65},{1,97},{34,2}... | collective-permute-start | bytes 3145736 | tf_op jit(solution)/shard_map/ppermute | solution.py:214
  44.5 27.6 %collective-permute-start.31 = (bf16[512,1024]{1,0:T(8,128)(2,1)}, bf16[512,1024]{1,0:T(8,128)(2,1)}, u32[]{:S(2)}, u32[]{:S(2)}) collective-permute-start(bf16[512,1024]{1,0:T(8,128)(2,1)} %collective-permute-done.27.refs_6_), channel_id=1, source_target_pairs={{0,32},{32,64},{64,96},{96,0},{1,33},{33,65},{65,97},{97,1},{2,34}... | collective-permute-start | bytes 3145736 | tf_op jit(solution)/shard_map/ppermute | solution.py:214
  45.5 57.9 %copy-start.1 = (bf16[200,4096]{1,0:T(8,128)(2,1)}, bf16[200,4096]{1,0:T(8,128)(2,1)S(1)}, u32[]{:S(2)}) copy-start(bf16[200,4096]{1,0:T(8,128)(2,1)S(1)} %collective-permute-done.22.refs_2_) | copy-start | bytes 4915204
  45.5 49.0 %collective-permute-start.28 = (bf16[512,1024]{1,0:T(8,128)(2,1)}, bf16[512,1024]{1,0:T(8,128)(2,1)}, u32[]{:S(2)}, u32[]{:S(2)}) collective-permute-start(bf16[512,1024]{1,0:T(8,128)(2,1)} %collective-permute-done.8.refs_5_), channel_id=1, source_target_pairs={{0,32},{32,64},{64,96},{96,0},{1,33},{33,65},{65,97},{97,1},{2,34}... | collective-permute-start | bytes 3145736 | tf_op jit(solution)/shard_map/ppermute | solution.py:214
  47.4 56.0 %copy-start = (bf16[200,4096]{1,0:T(8,128)(2,1)}, bf16[200,4096]{1,0:T(8,128)(2,1)S(1)}, u32[]{:S(2)}) copy-start(bf16[200,4096]{1,0:T(8,128)(2,1)S(1)} %collective-permute-done.2.refs_2_) | copy-start | bytes 4915204
  47.4 68.7 %collective-permute-start.9 = (bf16[512,1024]{1,0:T(8,128)(2,1)}, bf16[512,1024]{1,0:T(8,128)(2,1)}, u32[]{:S(2)}, u32[]{:S(2)}) collective-permute-start(bf16[512,1024]{1,0:T(8,128)(2,1)} %collective-permute-done.8.refs_5_), channel_id=1, source_target_pairs={{0,1},{1,2},{2,3},{3,0},{4,5},{5,6},{6,7},{7,4},{8,9},{9,10},{10,1... | collective-permute-start | bytes 3145736 | tf_op jit(solution)/shard_map/ppermute | solution.py:210
  67.2 79.1 %collective-permute-start.3 = (bf16[200,4096]{1,0:T(8,128)(2,1)}, bf16[200,4096]{1,0:T(8,128)(2,1)}, u32[]{:S(2)}, u32[]{:S(2)}) collective-permute-start(bf16[200,4096]{1,0:T(8,128)(2,1)} %get-tuple-element.45), channel_id=1, source_target_pairs={{0,3},{1,0},{2,1},{3,2},{4,7},{5,4},{6,5},{7,6},{8,11},{9,8},{10,9... | collective-permute-start | bytes 4915208 | tf_op jit(solution)/shard_map/ppermute | solution.py:210
  72.0 45.8 %collective-permute-start.10 = (bf16[512,1024]{1,0:T(8,128)(2,1)}, bf16[512,1024]{1,0:T(8,128)(2,1)}, u32[]{:S(2)}, u32[]{:S(2)}) collective-permute-start(bf16[512,1024]{1,0:T(8,128)(2,1)} %collective-permute-done.7.refs_4_), channel_id=1, source_target_pairs={{0,32},{32,64},{64,96},{96,0},{1,33},{33,65},{65,97},{97,1},{2,34}... | collective-permute-start | bytes 3145736 | tf_op jit(solution)/shard_map/ppermute | solution.py:214
  94.5 26.3 %collective-permute-start.12 = (bf16[512,1024]{1,0:T(8,128)(2,1)}, bf16[512,1024]{1,0:T(8,128)(2,1)}, u32[]{:S(2)}, u32[]{:S(2)}) collective-permute-start(bf16[512,1024]{1,0:T(8,128)(2,1)} %collective-permute-done.7.refs_4_), channel_id=1, source_target_pairs={{32,0},{64,32},{96,64},{0,96},{33,1},{65,33},{97,65},{1,97},{34,2}... | collective-permute-start | bytes 3145736 | tf_op jit(solution)/shard_map/ppermute | solution.py:214
  96.4 46.9 %collective-permute-start.32 = (bf16[512,1024]{1,0:T(8,128)(2,1)}, bf16[512,1024]{1,0:T(8,128)(2,1)}, u32[]{:S(2)}, u32[]{:S(2)}) collective-permute-start(bf16[512,1024]{1,0:T(8,128)(2,1)} %collective-permute-done.30.refs_9_), channel_id=1, source_target_pairs={{32,0},{64,32},{96,64},{0,96},{33,1},{65,33},{97,65},{1,97},{34,2}... | collective-permute-start | bytes 3145736 | tf_op jit(solution)/shard_map/ppermute | solution.py:214
  110.0 37.0 %copy-start.3 = (bf16[896,32]{1,0:T(8,128)(2,1)S(1)}, bf16[896,32]{1,0:T(8,128)(2,1)}, u32[]{:S(2)}) copy-start(bf16[896,32]{1,0:T(8,128)(2,1)} %constant.90.clone) | copy-start | bytes 172036
  110.0 37.0 %copy-start.22 = (f32[896]{0:T(1024)S(1)}, f32[896]{0:T(1024)}, u32[]{:S(2)}) copy-start(f32[896]{0:T(1024)} %constant.89.clone) | copy-start | bytes 10756
  116.1 50.8 %collective-permute-start.24 = (bf16[200,4096]{1,0:T(8,128)(2,1)}, bf16[200,4096]{1,0:T(8,128)(2,1)}, u32[]{:S(2)}, u32[]{:S(2)}) collective-permute-start(bf16[200,4096]{1,0:T(8,128)(2,1)} %get-tuple-element.63), channel_id=1, source_target_pairs={{0,4},{1,5},{2,6},{3,7},{4,8},{5,9},{6,10},{7,11},{8,12},{9,13},{1... | collective-permute-start | bytes 4915208 | tf_op jit(solution)/shard_map/ppermute | solution.py:210
  117.8 45.9 %collective-permute-start.13 = (bf16[512,1024]{1,0:T(8,128)(2,1)}, bf16[512,1024]{1,0:T(8,128)(2,1)}, u32[]{:S(2)}, u32[]{:S(2)}) collective-permute-start(bf16[512,1024]{1,0:T(8,128)(2,1)} %collective-permute-done.9.refs_5_), channel_id=1, source_target_pairs={{32,0},{64,32},{96,64},{0,96},{33,1},{65,33},{97,65},{1,97},{34,2}... | collective-permute-start | bytes 3145736 | tf_op jit(solution)/shard_map/ppermute | solution.py:214
  120.8 42.8 %collective-permute-start.14 = (bf16[512,1024]{1,0:T(8,128)(2,1)}, bf16[512,1024]{1,0:T(8,128)(2,1)}, u32[]{:S(2)}, u32[]{:S(2)}) collective-permute-start(bf16[512,1024]{1,0:T(8,128)(2,1)} %collective-permute-done.10.refs_6_), channel_id=1, source_target_pairs={{0,32},{32,64},{64,96},{96,0},{1,33},{33,65},{65,97},{97,1},{2,34}... | collective-permute-start | bytes 3145736 | tf_op jit(solution)/shard_map/ppermute | solution.py:214
  143.3 39.5 %collective-permute-start.25 = (bf16[200,4096]{1,0:T(8,128)(2,1)}, bf16[200,4096]{1,0:T(8,128)(2,1)}, u32[]{:S(2)}, u32[]{:S(2)}) collective-permute-start(bf16[200,4096]{1,0:T(8,128)(2,1)} %get-tuple-element.64), channel_id=1, source_target_pairs={{0,12},{1,13},{2,14},{3,15},{4,0},{5,1},{6,2},{7,3},{8,4},{9,5},{1... | collective-permute-start | bytes 4915208 | tf_op jit(solution)/shard_map/ppermute | solution.py:210
  146.3 1.2 copy-start.2
  146.3 36.5 %collective-permute-start.26 = (bf16[200,4096]{1,0:T(8,128)(2,1)}, bf16[200,4096]{1,0:T(8,128)(2,1)}, u32[]{:S(2)}, u32[]{:S(2)}) collective-permute-start(bf16[200,4096]{1,0:T(8,128)(2,1)} %get-tuple-element.65), channel_id=1, source_target_pairs={{0,8},{1,9},{2,10},{3,11},{4,12},{5,13},{6,14},{7,15},{8,0},{9,1},... | collective-permute-start | bytes 4915208 | tf_op jit(solution)/shard_map/ppermute | solution.py:210
  163.6 42.8 %collective-permute-start.4 = (bf16[200,4096]{1,0:T(8,128)(2,1)}, bf16[200,4096]{1,0:T(8,128)(2,1)}, u32[]{:S(2)}, u32[]{:S(2)}) collective-permute-start(bf16[200,4096]{1,0:T(8,128)(2,1)} %get-tuple-element.46), channel_id=1, source_target_pairs={{0,4},{1,5},{2,6},{3,7},{4,8},{5,9},{6,10},{7,11},{8,12},{9,13},{1... | collective-permute-start | bytes 4915208 | tf_op jit(solution)/shard_map/ppermute | solution.py:210
  163.6 54.3 %collective-permute-start.5 = (bf16[200,4096]{1,0:T(8,128)(2,1)}, bf16[200,4096]{1,0:T(8,128)(2,1)}, u32[]{:S(2)}, u32[]{:S(2)}) collective-permute-start(bf16[200,4096]{1,0:T(8,128)(2,1)} %get-tuple-element.47), channel_id=1, source_target_pairs={{0,12},{1,13},{2,14},{3,15},{4,0},{5,1},{6,2},{7,3},{8,4},{9,5},{1... | collective-permute-start | bytes 4915208 | tf_op jit(solution)/shard_map/ppermute | solution.py:210
  166.9 51.1 %collective-permute-start.6 = (bf16[200,4096]{1,0:T(8,128)(2,1)}, bf16[200,4096]{1,0:T(8,128)(2,1)}, u32[]{:S(2)}, u32[]{:S(2)}) collective-permute-start(bf16[200,4096]{1,0:T(8,128)(2,1)} %get-tuple-element.48), channel_id=1, source_target_pairs={{0,8},{1,9},{2,10},{3,11},{4,12},{5,13},{6,14},{7,15},{8,0},{9,1},... | collective-permute-start | bytes 4915208 | tf_op jit(solution)/shard_map/ppermute | solution.py:210
  182.8 18.5 %collective-permute-start.11 = (bf16[512,1024]{1,0:T(8,128)(2,1)}, bf16[512,1024]{1,0:T(8,128)(2,1)S(1)}, u32[]{:S(2)}, u32[]{:S(2)}) collective-permute-start(bf16[512,1024]{1,0:T(8,128)(2,1)} %collective-permute-done.9.refs_5_), channel_id=1, source_target_pairs={{0,32},{32,64},{64,96},{96,0},{1,33},{33,65},{65,97},{97,1},{2,34}... | collective-permute-start | bytes 3145736 | tf_op jit(solution)/shard_map/ppermute | solution.py:214
  182.8 23.2 %collective-permute-start.15 = (bf16[512,1024]{1,0:T(8,128)(2,1)}, bf16[512,1024]{1,0:T(8,128)(2,1)S(1)}, u32[]{:S(2)}, u32[]{:S(2)}) collective-permute-start(bf16[512,1024]{1,0:T(8,128)(2,1)} %collective-permute-done.13.refs_9_), channel_id=1, source_target_pairs={{32,0},{64,32},{96,64},{0,96},{33,1},{65,33},{97,65},{1,97},{34,2}... | collective-permute-start | bytes 3145736 | tf_op jit(solution)/shard_map/ppermute | solution.py:214
  201.4 1.0 copy-start.14
  202.3 33.0 %collective-permute-start.33 = (bf16[200,1024]{1,0:T(8,128)(2,1)}, bf16[200,1024]{1,0:T(8,128)(2,1)S(1)}, u32[]{:S(2)}, u32[]{:S(2)}) collective-permute-start(bf16[200,1024]{1,0:T(8,128)(2,1)} %get-tuple-element.68), channel_id=1, source_target_pairs={{4,0},{5,1},{6,2},{7,3},{8,4},{9,5},{10,6},{11,7},{12,8},{13,9},{1... | collective-permute-start | bytes 1228808 | tf_op jit(solution)/shard_map/ppermute | solution.py:210
  206.0 1.0 copy-start.15
  206.0 29.7 %collective-permute-start.34 = (bf16[200,1024]{1,0:T(8,128)(2,1)}, bf16[200,1024]{1,0:T(8,128)(2,1)S(1)}, u32[]{:S(2)}, u32[]{:S(2)}) collective-permute-start(bf16[200,1024]{1,0:T(8,128)(2,1)} %get-tuple-element.69), channel_id=1, source_target_pairs={{8,0},{9,1},{10,2},{11,3},{12,4},{13,5},{14,6},{15,7},{0,8},{1,9},... | collective-permute-start | bytes 1228808 | tf_op jit(solution)/shard_map/ppermute | solution.py:210
  207.1 28.7 %collective-permute-start.35 = (bf16[200,1024]{1,0:T(8,128)(2,1)}, bf16[200,1024]{1,0:T(8,128)(2,1)S(1)}, u32[]{:S(2)}, u32[]{:S(2)}) collective-permute-start(bf16[200,1024]{1,0:T(8,128)(2,1)} %get-tuple-element.70), channel_id=1, source_target_pairs={{12,0},{13,1},{14,2},{15,3},{0,4},{1,5},{2,6},{3,7},{4,8},{5,9},{6... | collective-permute-start | bytes 1228808 | tf_op jit(solution)/shard_map/ppermute | solution.py:210
  231.0 17.3 %collective-permute-start.16 = (bf16[200,1024]{1,0:T(8,128)(2,1)}, bf16[200,1024]{1,0:T(8,128)(2,1)S(1)}, u32[]{:S(2)}, u32[]{:S(2)}) collective-permute-start(bf16[200,1024]{1,0:T(8,128)(2,1)} %get-tuple-element.51), channel_id=1, source_target_pairs={{4,0},{5,1},{6,2},{7,3},{8,4},{9,5},{10,6},{11,7},{12,8},{13,9},{1... | collective-permute-start | bytes 1228808 | tf_op jit(solution)/shard_map/ppermute | solution.py:210
  234.8 13.5 %collective-permute-start.17 = (bf16[200,1024]{1,0:T(8,128)(2,1)}, bf16[200,1024]{1,0:T(8,128)(2,1)S(1)}, u32[]{:S(2)}, u32[]{:S(2)}) collective-permute-start(bf16[200,1024]{1,0:T(8,128)(2,1)} %get-tuple-element.52), channel_id=1, source_target_pairs={{8,0},{9,1},{10,2},{11,3},{12,4},{13,5},{14,6},{15,7},{0,8},{1,9},... | collective-permute-start | bytes 1228808 | tf_op jit(solution)/shard_map/ppermute | solution.py:210
  235.3 0.8 copy-start.4
  235.3 13.5 %collective-permute-start.18 = (bf16[200,1024]{1,0:T(8,128)(2,1)}, bf16[200,1024]{1,0:T(8,128)(2,1)S(1)}, u32[]{:S(2)}, u32[]{:S(2)}) collective-permute-start(bf16[200,1024]{1,0:T(8,128)(2,1)} %get-tuple-element.53), channel_id=1, source_target_pairs={{12,0},{13,1},{14,2},{15,3},{0,4},{1,5},{2,6},{3,7},{4,8},{5,9},{6... | collective-permute-start | bytes 1228808 | tf_op jit(solution)/shard_map/ppermute | solution.py:210
  235.7 0.8 copy-start.5
  235.7 0.9 copy-start.7
  239.2 16.2 %collective-permute-start.36 = (bf16[200,1024]{1,0:T(8,128)(2,1)}, bf16[200,1024]{1,0:T(8,128)(2,1)S(1)}, u32[]{:S(2)}, u32[]{:S(2)}) collective-permute-start(bf16[200,1024]{1,0:T(8,128)(2,1)} %get-tuple-element.72), channel_id=1, source_target_pairs={{1,0},{2,1},{3,2},{0,3},{5,4},{6,5},{7,6},{4,7},{9,8},{10,9},{11,1... | collective-permute-start | bytes 1228808 | tf_op jit(solution)/shard_map/ppermute | solution.py:210
  240.9 14.6 %collective-permute-start.37 = (bf16[200,1024]{1,0:T(8,128)(2,1)}, bf16[200,1024]{1,0:T(8,128)(2,1)S(1)}, u32[]{:S(2)}, u32[]{:S(2)}) collective-permute-start(bf16[200,1024]{1,0:T(8,128)(2,1)} %get-tuple-element.73), channel_id=1, source_target_pairs={{0,16},{1,17},{2,18},{3,19},{4,20},{5,21},{6,22},{7,23},{8,24},{9,... | collective-permute-start | bytes 1228808 | tf_op jit(solution)/shard_map/ppermute | solution.py:210
  248.3 0.8 copy-start.6
  248.3 7.6 %collective-permute-start.38 = (bf16[200,1024]{1,0:T(8,128)(2,1)}, bf16[200,1024]{1,0:T(8,128)(2,1)S(1)}, u32[]{:S(2)}, u32[]{:S(2)}) collective-permute-start(bf16[200,1024]{1,0:T(8,128)(2,1)} %get-tuple-element.74), channel_id=1, source_target_pairs={{1,16},{2,17},{3,18},{0,19},{5,20},{6,21},{7,22},{4,23},{9,24},{10... | collective-permute-start | bytes 1228808 | tf_op jit(solution)/shard_map/ppermute | solution.py:210
  248.3 0.9 copy-start.8
  248.8 0.8 copy-start.9
  252.2 11.2 %collective-permute-start.19 = (bf16[200,1024]{1,0:T(8,128)(2,1)}, bf16[200,1024]{1,0:T(8,128)(2,1)S(1)}, u32[]{:S(2)}, u32[]{:S(2)}) collective-permute-start(bf16[200,1024]{1,0:T(8,128)(2,1)} %get-tuple-element.55), channel_id=1, source_target_pairs={{3,0},{0,1},{1,2},{2,3},{7,4},{4,5},{5,6},{6,7},{11,8},{8,9},{9,10... | collective-permute-start | bytes 1228808 | tf_op jit(solution)/shard_map/ppermute | solution.py:210
  253.6 9.8 %collective-permute-start.20 = (bf16[200,1024]{1,0:T(8,128)(2,1)}, bf16[200,1024]{1,0:T(8,128)(2,1)S(1)}, u32[]{:S(2)}, u32[]{:S(2)}) collective-permute-start(bf16[200,1024]{1,0:T(8,128)(2,1)} %get-tuple-element.56), channel_id=1, source_target_pairs={{0,16},{1,17},{2,18},{3,19},{4,20},{5,21},{6,22},{7,23},{8,24},{9,... | collective-permute-start | bytes 1228808 | tf_op jit(solution)/shard_map/ppermute | solution.py:210
  255.4 0.8 copy-start.16
  255.4 12.8 %collective-permute-start.21 = (bf16[200,1024]{1,0:T(8,128)(2,1)}, bf16[200,1024]{1,0:T(8,128)(2,1)S(1)}, u32[]{:S(2)}, u32[]{:S(2)}) collective-permute-start(bf16[200,1024]{1,0:T(8,128)(2,1)} %get-tuple-element.57), channel_id=1, source_target_pairs={{3,16},{0,17},{1,18},{2,19},{7,20},{4,21},{5,22},{6,23},{11,24},{8... | collective-permute-start | bytes 1228808 | tf_op jit(solution)/shard_map/ppermute | solution.py:210
  255.5 0.9 copy-start.17
  255.9 0.8 copy-start.18
  263.3 4.9 %copy-start.19 = (bf16[200,1024]{1,0:T(8,128)(2,1)}, bf16[200,1024]{1,0:T(8,128)(2,1)S(1)}, u32[]{:S(2)}) copy-start(bf16[200,1024]{1,0:T(8,128)(2,1)S(1)} %collective-permute-done.19.refs_1_) | copy-start | bytes 1228804
  263.4 4.9 %copy-start.20 = (bf16[200,1024]{1,0:T(8,128)(2,1)}, bf16[200,1024]{1,0:T(8,128)(2,1)S(1)}, u32[]{:S(2)}) copy-start(bf16[200,1024]{1,0:T(8,128)(2,1)S(1)} %collective-permute-done.20.refs_2_) | copy-start | bytes 1228804
  268.2 0.8 copy-start.21

commit v4 on v3

--- a/solution.py
+++ b/solution.py
@@ -15,6 +15,7 @@
 SETS = (((0, 0), (1, 1)), ((0, -1), (-1, 2)))
 BLOCKS = SETS[0] + SETS[1]
 EXPERT_CALLS = (((1, 3, 2, 0),), ((1, 3, 2, 0),))
+SUMS = ((0, 1, 2), (3,))
 INTERPRET = False
 
 
@@ -71,6 +72,7 @@
         out_shape=[jax.ShapeDtypeStruct((rows, width), arrays[0].dtype)] * SIDE,
         cost_estimate=pl.CostEstimate(flops=size, bytes_accessed=2 * size, transcendentals=0),
         interpret=INTERPRET,
+        compiler_params=pltpu.CompilerParams(vmem_limit_bytes=6 * SIDE * step * rows * 2 + (4 << 20)),
         name="regroup",
     )(*arrays)
 
@@ -114,6 +116,7 @@
             transcendentals=0,
         ),
         interpret=INTERPRET,
+        compiler_params=pltpu.CompilerParams(vmem_limit_bytes=12 << 20),
         name="dispatch",
     )(spread, row_slot, slot, tokens)
 
@@ -153,6 +156,7 @@
             transcendentals=0,
         ),
         interpret=INTERPRET,
+        compiler_params=pltpu.CompilerParams(vmem_limit_bytes=26 << 20),
         name="expert",
     )(place, *values, *parts)
 
@@ -161,37 +165,41 @@
     blocks, base, out_ref, rows_ref = refs[:count], refs[count:-2], refs[-2], refs[-1]
     rows = blocks[0].shape[0]
     stride = -(-rows // 16) * 16
-    rows_ref[...] = jnp.zeros_like(rows_ref)
-    for i, block in enumerate(blocks):
-        rows_ref[i * stride : i * stride + rows] = block[...]
-    both = jnp.dot(share_ref[...], rows_ref[...], preferred_element_type=jnp.float32)
-    tokens = out_ref.shape[0]
-    total = both[:tokens] + both[tokens:]
+
+    @pl.when(pl.program_id(0) == 0)
+    def _():
+        rows_ref[...] = jnp.zeros_like(rows_ref)
+        for i, block in enumerate(blocks):
+            rows_ref[i * stride : i * stride + rows] = block[...]
+
+    total = jnp.dot(share_ref[0], rows_ref[...], preferred_element_type=jnp.float32)
+    total += jnp.dot(share_ref[1], rows_ref[...], preferred_element_type=jnp.float32)
     for other in base:
         total += other[...]
     out_ref[...] = total.astype(out_ref.dtype)
 
 
 def combine(share, blocks, base, dtype):
-    depth = share.shape[1]
-    count = share.shape[0] // 2
+    _, count, depth = share.shape
     hidden = blocks[0].shape[1]
-    step = min(hidden, 256)
-    right = pl.BlockSpec((blocks[0].shape[0], step), lambda i: (0, i))
-    sums = pl.BlockSpec((count, step), lambda i: (0, i))
+    step = count // 4
+    right = pl.BlockSpec(blocks[0].shape, lambda i: (0, 0))
+    sums = pl.BlockSpec((step, hidden), lambda i: (i, 0))
+    left = pl.BlockSpec((2, step, depth), lambda i: (0, i, 0))
     return pl.pallas_call(
         functools.partial(combine_kernel, len(blocks)),
-        grid=(hidden // step,),
-        in_specs=[pl.BlockSpec(share.shape, lambda i: (0, 0))] + [right] * len(blocks) + [sums] * len(base),
+        grid=(count // step,),
+        in_specs=[left] + [right] * len(blocks) + [sums] * len(base),
         out_specs=sums,
         out_shape=jax.ShapeDtypeStruct((count, hidden), dtype),
-        scratch_shapes=[pltpu.VMEM((depth, step), blocks[0].dtype)],
+        scratch_shapes=[pltpu.VMEM((depth, hidden), blocks[0].dtype)],
         cost_estimate=pl.CostEstimate(
             flops=4 * count * depth * hidden,
             bytes_accessed=4 * count * (depth + hidden) + 2 * depth * hidden,
             transcendentals=0,
         ),
         interpret=INTERPRET,
+        compiler_params=pltpu.CompilerParams(vmem_limit_bytes=32 << 20),
         name="combine",
     )(share, *blocks, *base)
 
@@ -294,9 +302,9 @@
     high = lax.reduce_precision(gate, 8, 7)
     turned = (((0,), (1,)), ((), ()))
     per_set = len(BLOCKS) // len(SETS)
-    for s in range(len(SETS)):
-        held = CORES * per_set * length
-        spread, row_slot = layout(range(s * per_set, (s + 1) * per_set), CORES, -(-held // 128) * 128)
+    for group in SUMS:
+        held = CORES * len(group) * length
+        spread, row_slot = layout(group, CORES, -(-held // 128) * 128)
         at_row = lax.dot_general(slot, spread, turned, preferred_element_type=jnp.float32)
         share = []
         for part in (high, gate - high):
@@ -304,7 +312,7 @@
                 part.astype(jnp.bfloat16), spread, turned, preferred_element_type=jnp.float32
             )
             share.append(jnp.where(at_row == row_slot[None, :], part, 0.0).astype(jnp.bfloat16))
-        shares.append(jnp.concatenate(share))
+        shares.append(jnp.stack(share))
 
     total = ()
     for s in range(len(SETS)):
@@ -323,9 +331,9 @@
         if s == 0:
             first_members, early = members, grouped
         else:
-            finish = ((0, first_members, early), (1, members, grouped))
-    for s, members, grouped in finish:
-        blocks = {}
+            finish = ((first_members, early), (members, grouped))
+    blocks = {}
+    for members, grouped in finish:
         for (q, b), block in zip(members, grouped):
             moves = back(pairs(BLOCKS[b][0], 0))
             if q:
@@ -333,9 +341,10 @@
             if q or BLOCKS[b][0]:
                 block = move(block, moves)
             blocks[q, b] = block
-        ordered = [blocks[q, s * per_set + i] for q in range(CORES) for i in range(per_set)]
-        last = s == len(SETS) - 1
-        total = (combine(shares[s], ordered, total, jnp.bfloat16 if last else jnp.float32),)
+    for i, group in enumerate(SUMS):
+        ordered = [blocks[q, b] for q in range(CORES) for b in group]
+        kind = jnp.bfloat16 if i == len(SUMS) - 1 else jnp.float32
+        total = (combine(shares[i], ordered, total, kind),)
     return total[0]
 
 

time: 277 us -> 267 us (0.964)
  the two profiles are of different devices: /device:TPU:2 before, /device:TPU:64 now
where the time goes in v4:
time: 267 us; the launch traced here: 263 us
  waiting for transfers between devices  139 us (52%)
  Pallas kernels  57.6 us (22%)
  starting transfers between devices  43.2 us (16%)
  local copies, waits for them, and re-layouts  15.1 us (6%)
  matrix products  5.53 us (2%)
    ppermute x15, waiting for transfers between devices, across(): return lax.ppermute(array, axis, moves)  91 us
    ppermute x24, waiting for transfers between devices, move(): return lax.ppermute(array, PLANE, moves)  48.2 us
    ppermute x24, starting transfers between devices, move(): return lax.ppermute(array, PLANE, moves)  28.9 us
    pallas_call x2, Pallas kernels, expert(): pl.pallas_call(functools.partial(expert_kernel, len(values)), grid=(hidde...  23.5 us
    pallas_call x4, Pallas kernels, dispatch(): pl.pallas_call(dispatch_kernel, grid=(width // step,), in_specs=[pl.Block...  19.9 us
    ppermute x15, starting transfers between devices, across(): return lax.ppermute(array, axis, moves)  14.3 us
    unnamed x86, local copies, waits for them, and re-layouts  13.2 us
    pallas_call x2, Pallas kernels, combine(): pl.pallas_call(functools.partial(combine_kernel, len(blocks)), grid=(coun...  7.69 us
  transfers between devices with their start and end apart: 39, of which 17 were waited for; matrix products, arithmetic and copies ran while one was open for 4% of the time, Pallas kernels for 21%

profile of v4, /device:TPU:64, one launch (start us, length us, event | category | flops | bytes accessed | tf_op | source)
XLA Modules:
  0.0 263.0 jit_solution(14993044633505755011)
XLA Ops:
  0.1 1.8 dynamic-slice_bitcast_fusion
  1.9 0.6 collective-permute-start.8
  3.0 2.5 copy-done
  5.4 4.2 %dispatch.6 = (bf16[200,4096]{1,0:T(8,128)(2,1)S(1)}, bf16[200,4096]{1,0:T(8,128)(2,1)S(1)}) custom-call(bf16[416,16]{1,0:T(8,128)(2,1)S(1)} %copy-done.31, f32[416,1]{1,0:T(8,128)S(1)} %copy-done.29, bf16[16,640]{1,0:T(8,128)(2,1)S(1)} %slice.33.slot_ref, bf16[640,4096]{1,0:T(8,128)(2,1)S(1)} %copy-done), custom_call_target="tpu_custom_call" | custom-call | flops 2181038080 | bytes 8650752 | tf_op jit(solution)/shard_map/dispatch/pallas_call | solution.py:101
  9.6 1.6 collective-permute-start.21
  11.3 1.7 collective-permute-start.26
  13.4 2.5 collective-permute-start.2
  16.3 5.8 %dispatch.7 = (bf16[200,4096]{1,0:T(8,128)(2,1)S(1)}, bf16[200,4096]{1,0:T(8,128)(2,1)S(1)}) custom-call(bf16[416,16]{1,0:T(8,128)(2,1)S(1)} %copy-done.31, f32[416,1]{1,0:T(8,128)S(1)} %copy-done.29, bf16[16,640]{1,0:T(8,128)(2,1)S(1)} %fusion.15.slot_ref, bf16[640,4096]{1,0:T(8,128)(2,1)} %collective-permute-done.1.tokens_ref), custom_call_target="tpu_custom_call" | custom-call | flops 2181038080 | bytes 8650752 | tf_op jit(solution)/shard_map/dispatch/pallas_call | solution.py:101
  22.0 14.8 %collective-permute-done.26.refs_6_ = bf16[512,1024]{1,0:T(8,128)(2,1)S(1)} collective-permute-done((bf16[512,1024]{1,0:T(8,128)(2,1)S(1)}, bf16[512,1024]{1,0:T(8,128)(2,1)S(1)}, u32[]{:S(2)}, u32[]{:S(2)}) %collective-permute-start.26) | collective-permute-done | bytes 1048608 | tf_op jit(solution)/shard_map/ppermute | solution.py:222
  36.9 1.5 collective-permute-start.22
  38.4 1.0 copy-done.9
  39.6 3.7 %collective-permute-done.7.refs_4_ = bf16[512,1024]{1,0:T(8,128)(2,1)S(1)} collective-permute-done((bf16[512,1024]{1,0:T(8,128)(2,1)S(1)}, bf16[512,1024]{1,0:T(8,128)(2,1)S(1)}, u32[]{:S(2)}, u32[]{:S(2)}) %collective-permute-start.7) | collective-permute-done | bytes 1048608 | tf_op jit(solution)/shard_map/ppermute | solution.py:218
  43.3 1.6 collective-permute-start.30
  44.9 1.0 copy-done.7
  45.9 1.3 collective-permute-start.9
  47.3 17.1 %collective-permute-done.29.refs_9_ = bf16[512,1024]{1,0:T(8,128)(2,1)S(1)} collective-permute-done((bf16[512,1024]{1,0:T(8,128)(2,1)}, bf16[512,1024]{1,0:T(8,128)(2,1)S(1)}, u32[]{:S(2)}, u32[]{:S(2)}) %collective-permute-start.29) | collective-permute-done | bytes 1048608 | tf_op jit(solution)/shard_map/ppermute | solution.py:222
  64.4 2.6 %collective-permute-start.3 = (bf16[200,4096]{1,0:T(8,128)(2,1)S(1)}, bf16[200,4096]{1,0:T(8,128)(2,1)S(1)}, u32[]{:S(2)}, u32[]{:S(2)}) collective-permute-start(bf16[200,4096]{1,0:T(8,128)(2,1)S(1)} %get-tuple-element.45), channel_id=1, source_target_pairs={{0,3},{1,0},{2,1},{3,2},{4,7},{5,4},{6,5},{7,6},{8,11},{9,8},{10,9... | collective-permute-start | bytes 4915208 | tf_op jit(solution)/shard_map/ppermute | solution.py:218
  67.0 2.3 collective-permute-done.30.refs_10_
  69.3 1.0 copy-done.19
  70.3 1.6 collective-permute-start.10
  71.9 19.9 %collective-permute-done.27.refs_7_ = bf16[512,1024]{1,0:T(8,128)(2,1)S(1)} collective-permute-done((bf16[512,1024]{1,0:T(8,128)(2,1)}, bf16[512,1024]{1,0:T(8,128)(2,1)S(1)}, u32[]{:S(2)}, u32[]{:S(2)}) %collective-permute-start.27) | collective-permute-done | bytes 1048608 | tf_op jit(solution)/shard_map/ppermute | solution.py:222
  91.8 1.0 copy-done.21
  92.9 2.1 collective-permute-start.31
  95.0 4.2 %dispatch.4 = (bf16[200,4096]{1,0:T(8,128)(2,1)S(1)}, bf16[200,4096]{1,0:T(8,128)(2,1)S(1)}) custom-call(bf16[416,16]{1,0:T(8,128)(2,1)S(1)} %copy-done.30, f32[416,1]{1,0:T(8,128)S(1)} %copy-done.29, bf16[16,640]{1,0:T(8,128)(2,1)S(1)} %slice.33.slot_ref, bf16[640,4096]{1,0:T(8,128)(2,1)S(1)} %bitcast.31), custom_call_target="tpu_custom_call" | custom-call | flops 2181038080 | bytes 8650752 | tf_op jit(solution)/shard_map/dispatch/pallas_call | solution.py:101
  99.3 5.7 %dispatch.5 = (bf16[200,4096]{1,0:T(8,128)(2,1)S(1)}, bf16[200,4096]{1,0:T(8,128)(2,1)S(1)}) custom-call(bf16[416,16]{1,0:T(8,128)(2,1)S(1)} %copy-done.30, f32[416,1]{1,0:T(8,128)S(1)} %copy-done.29, bf16[16,640]{1,0:T(8,128)(2,1)S(1)} %fusion.15.slot_ref, bf16[640,4096]{1,0:T(8,128)(2,1)} %collective-permute-done.1.tokens_ref), custom_call_target="tpu_custom_call" | custom-call | flops 2181038080 | bytes 8650752 | tf_op jit(solution)/shard_map/dispatch/pallas_call | solution.py:101
  105.0 2.9 %regroup.6 = (bf16[200,4096]{1,0:T(8,128)(2,1)S(1)}, bf16[200,4096]{1,0:T(8,128)(2,1)S(1)}, bf16[200,4096]{1,0:T(8,128)(2,1)}, bf16[200,4096]{1,0:T(8,128)(2,1)}) custom-call(bf16[200,4096]{1,0:T(8,128)(2,1)S(1)} %get-tuple-element.57.refs_0_, bf16[200,4096]{1,0:T(8,128)(2,1)S(1)} %get-tuple-element.58.refs_1_, ...), custom_call_target="tpu_custom_call" | custom-call | flops 6553600 | bytes 13107200 | tf_op jit(solution)/shard_map/regroup/pallas_call | solution.py:67
  107.9 1.6 collective-permute-start.23
  109.5 3.1 %collective-permute-done.10.refs_6_ = bf16[512,1024]{1,0:T(8,128)(2,1)S(1)} collective-permute-done((bf16[512,1024]{1,0:T(8,128)(2,1)S(1)}, bf16[512,1024]{1,0:T(8,128)(2,1)S(1)}, u32[]{:S(2)}, u32[]{:S(2)}) %collective-permute-start.10) | collective-permute-done | bytes 1048608 | tf_op jit(solution)/shard_map/ppermute | solution.py:222
  112.7 6.1 %collective-permute-done.12.refs_8_ = bf16[512,1024]{1,0:T(8,128)(2,1)S(1)} collective-permute-done((bf16[512,1024]{1,0:T(8,128)(2,1)S(1)}, bf16[512,1024]{1,0:T(8,128)(2,1)S(1)}, u32[]{:S(2)}, u32[]{:S(2)}) %collective-permute-start.12) | collective-permute-done | bytes 1048608 | tf_op jit(solution)/shard_map/ppermute | solution.py:222
  118.8 2.8 %collective-permute-start.14 = (bf16[512,1024]{1,0:T(8,128)(2,1)S(1)}, bf16[512,1024]{1,0:T(8,128)(2,1)S(1)}, u32[]{:S(2)}, u32[]{:S(2)}) collective-permute-start(bf16[512,1024]{1,0:T(8,128)(2,1)S(1)} %collective-permute-done.10.refs_6_), channel_id=1, source_target_pairs={{0,32},{32,64},{64,96},{96,0},{1,33},{33,65},{65,97},{97,1},{2,34}... | collective-permute-start | bytes 3145736 | tf_op jit(solution)/shard_map/ppermute | solution.py:222
  121.6 19.6 %collective-permute-done.31.refs_11_ = bf16[512,1024]{1,0:T(8,128)(2,1)S(1)} collective-permute-done((bf16[512,1024]{1,0:T(8,128)(2,1)S(1)}, bf16[512,1024]{1,0:T(8,128)(2,1)S(1)}, u32[]{:S(2)}, u32[]{:S(2)}) %collective-permute-start.31) | collective-permute-done | bytes 1048608 | tf_op jit(solution)/shard_map/ppermute | solution.py:222
  141.3 1.0 copy-done.27
  142.2 3.0 %collective-permute-start.24 = (bf16[200,4096]{1,0:T(8,128)(2,1)}, bf16[200,4096]{1,0:T(8,128)(2,1)}, u32[]{:S(2)}, u32[]{:S(2)}) collective-permute-start(bf16[200,4096]{1,0:T(8,128)(2,1)} %get-tuple-element.62), channel_id=1, source_target_pairs={{0,12},{1,13},{2,14},{3,15},{4,0},{5,1},{6,2},{7,3},{8,4},{9,5},{1... | collective-permute-start | bytes 4915208 | tf_op jit(solution)/shard_map/ppermute | solution.py:218
  145.3 0.6 collective-permute-start.25
  146.3 1.3 fusion.8
  147.6 0.6 convolution_compare_fusion
  148.2 3.3 %regroup.4 = (bf16[200,4096]{1,0:T(8,128)(2,1)S(1)}, bf16[200,4096]{1,0:T(8,128)(2,1)}, bf16[200,4096]{1,0:T(8,128)(2,1)}, bf16[200,4096]{1,0:T(8,128)(2,1)}) custom-call(bf16[200,4096]{1,0:T(8,128)(2,1)S(1)} %get-tuple-element.42.refs_0_, bf16[200,4096]{1,0:T(8,128)(2,1)S(1)} %get-tuple-element.43.refs_1_, ...), custom_call_target="tpu_custom_call" | custom-call | flops 6553600 | bytes 13107200 | tf_op jit(solution)/shard_map/regroup/pallas_call | solution.py:67
  151.6 1.2 copy-done.1
  152.7 6.8 %collective-permute-done.13.refs_9_ = bf16[512,1024]{1,0:T(8,128)(2,1)S(1)} collective-permute-done((bf16[512,1024]{1,0:T(8,128)(2,1)S(1)}, bf16[512,1024]{1,0:T(8,128)(2,1)S(1)}, u32[]{:S(2)}, u32[]{:S(2)}) %collective-permute-start.13) | collective-permute-done | bytes 1048608 | tf_op jit(solution)/shard_map/ppermute | solution.py:222
  159.5 1.1 copy-done.25
  160.6 3.2 %collective-permute-start.5 = (bf16[200,4096]{1,0:T(8,128)(2,1)}, bf16[200,4096]{1,0:T(8,128)(2,1)}, u32[]{:S(2)}, u32[]{:S(2)}) collective-permute-start(bf16[200,4096]{1,0:T(8,128)(2,1)} %get-tuple-element.47), channel_id=1, source_target_pairs={{0,12},{1,13},{2,14},{3,15},{4,0},{5,1},{6,2},{7,3},{8,4},{9,5},{1... | collective-permute-start | bytes 4915208 | tf_op jit(solution)/shard_map/ppermute | solution.py:218
  163.8 1.2 copy-done.3
  164.9 1.3 fusion.9
  166.3 1.5 pad_maximum_fusion.1.share_ref
  167.7 0.7 fusion.3
  168.5 0.7 fusion.2
  169.2 12.6 %collective-permute-done.24.refs_1_ = bf16[200,4096]{1,0:T(8,128)(2,1)} collective-permute-done((bf16[200,4096]{1,0:T(8,128)(2,1)}, bf16[200,4096]{1,0:T(8,128)(2,1)}, u32[]{:S(2)}, u32[]{:S(2)}) %collective-permute-start.24) | collective-permute-done | bytes 1638432 | tf_op jit(solution)/shard_map/ppermute | solution.py:218
  181.8 2.8 %collective-permute-start.11 = (bf16[512,1024]{1,0:T(8,128)(2,1)S(1)}, bf16[512,1024]{1,0:T(8,128)(2,1)S(1)}, u32[]{:S(2)}, u32[]{:S(2)}) collective-permute-start(bf16[512,1024]{1,0:T(8,128)(2,1)S(1)} %copy-done.12), channel_id=1, source_target_pairs={{0,32},{32,64},{64,96},{96,0},{1,33},{33,65},{65,97},{97,1},{2,34}... | collective-permute-start | bytes 3145736 | tf_op jit(solution)/shard_map/ppermute | solution.py:222
  185.0 1.1 copy-done.4
  187.4 11.5 %expert.3 = (bf16[200,1024]{1,0:T(8,128)(2,1)S(1)}, bf16[200,1024]{1,0:T(8,128)(2,1)S(1)}, bf16[200,1024]{1,0:T(8,128)(2,1)S(1)}, bf16[200,1024]{1,0:T(8,128)(2,1)S(1)}) custom-call(s32[2]{0:T(128)S(1)} %pad_add_fusion.place_ref, bf16[200,4096]{1,0:T(8,128)(2,1)S(1)} %copy-done.4, bf16[200,4096]{1,0:T(8,128)(2,1)} %collective-permute-done.24.refs_1_, ...), custom_call_target="tpu_custom_call" | custom-call | flops 6710886400 | bytes 16580608 | tf_op jit(solution)/shard_map/expert/pallas_call | solution.py:146
  198.9 1.2 collective-permute-done.11.refs_7_
  200.1 2.6 collective-permute-start.32
  202.7 1.3 collective-permute-start.34
  204.0 12.9 %collective-permute-done.5.refs_1_ = bf16[200,4096]{1,0:T(8,128)(2,1)} collective-permute-done((bf16[200,4096]{1,0:T(8,128)(2,1)}, bf16[200,4096]{1,0:T(8,128)(2,1)}, u32[]{:S(2)}, u32[]{:S(2)}) %collective-permute-start.5) | collective-permute-done | bytes 1638432 | tf_op jit(solution)/shard_map/ppermute | solution.py:218
  216.9 12.0 %expert.2 = (bf16[200,1024]{1,0:T(8,128)(2,1)S(1)}, bf16[200,1024]{1,0:T(8,128)(2,1)S(1)}, bf16[200,1024]{1,0:T(8,128)(2,1)S(1)}, bf16[200,1024]{1,0:T(8,128)(2,1)S(1)}) custom-call(s32[2]{0:T(128)S(1)} %pad_add_fusion.place_ref, bf16[200,4096]{1,0:T(8,128)(2,1)} %collective-permute-done.4.refs_0_, bf16[200,4096]{1,0:T(8,128)(2,1)} %collective-permute-done.5.refs_1_, ...), custom_call_target="tpu_custom_call" | custom-call | flops 6710886400 | bytes 16580608 | tf_op jit(solution)/shard_map/expert/pallas_call | solution.py:146
  228.9 3.8 %collective-permute-start.16 = (bf16[200,1024]{1,0:T(8,128)(2,1)S(1)}, bf16[200,1024]{1,0:T(8,128)(2,1)S(1)}, u32[]{:S(2)}, u32[]{:S(2)}) collective-permute-start(bf16[200,1024]{1,0:T(8,128)(2,1)S(1)} %get-tuple-element.51), channel_id=1, source_target_pairs={{4,0},{5,1},{6,2},{7,3},{8,4},{9,5},{10,6},{11,7},{12,8},{13,9},{1... | collective-permute-start | bytes 1228808 | tf_op jit(solution)/shard_map/ppermute | solution.py:218
  233.7 1.8 collective-permute-start.35
  235.6 6.9 %collective-permute-done.16.refs_1_ = bf16[200,1024]{1,0:T(8,128)(2,1)S(1)} collective-permute-done((bf16[200,1024]{1,0:T(8,128)(2,1)S(1)}, bf16[200,1024]{1,0:T(8,128)(2,1)S(1)}, u32[]{:S(2)}, u32[]{:S(2)}) %collective-permute-start.16) | collective-permute-done | bytes 409632 | tf_op jit(solution)/shard_map/ppermute | solution.py:218
  242.5 4.0 %collective-permute-done.18.refs_3_ = bf16[200,1024]{1,0:T(8,128)(2,1)S(1)} collective-permute-done((bf16[200,1024]{1,0:T(8,128)(2,1)S(1)}, bf16[200,1024]{1,0:T(8,128)(2,1)S(1)}, u32[]{:S(2)}, u32[]{:S(2)}) %collective-permute-start.18) | collective-permute-done | bytes 409632 | tf_op jit(solution)/shard_map/ppermute | solution.py:218
  247.1 2.7 %collective-permute-done.37.refs_4_ = bf16[200,1024]{1,0:T(8,128)(2,1)S(1)} collective-permute-done((bf16[200,1024]{1,0:T(8,128)(2,1)S(1)}, bf16[200,1024]{1,0:T(8,128)(2,1)S(1)}, u32[]{:S(2)}, u32[]{:S(2)}) %collective-permute-start.37) | collective-permute-done | bytes 409632 | tf_op jit(solution)/shard_map/ppermute | solution.py:218
  249.9 4.5 %combine.2.refs_2_ = f32[640,1024]{1,0:T(8,128)S(1)} custom-call(bf16[2,640,1280]{2,1,0:T(8,128)(2,1)S(1)} %pad_maximum_fusion.share_ref, bf16[200,1024]{1,0:T(8,128)(2,1)S(1)} %get-tuple-element.69.refs_0_, bf16[200,1024]{1,0:T(8,128)(2,1)S(1)} %collective-permute-done.35.refs_1_, bf16[200,1024]{1,0:T(8,128)(2,1)S(1)} %get-tuple-element.71.refs_2_, ...), custom_call_target="tpu_custom_call" | custom-call | flops 3355443200 | bytes 8519680 | tf_op jit(solution)/shard_map/combine/pallas_call | solution.py:189
  254.4 1.6 collective-permute-done.19.refs_0_
  256.0 3.8 %collective-permute-done.20.refs_1_ = bf16[200,1024]{1,0:T(8,128)(2,1)S(1)} collective-permute-done((bf16[200,1024]{1,0:T(8,128)(2,1)S(1)}, bf16[200,1024]{1,0:T(8,128)(2,1)S(1)}, u32[]{:S(2)}, u32[]{:S(2)}) %collective-permute-start.20) | collective-permute-done | bytes 409632 | tf_op jit(solution)/shard_map/ppermute | solution.py:218
  259.8 3.2 %combine.3 = bf16[640,1024]{1,0:T(8,128)(2,1)} custom-call(bf16[2,640,512]{2,1,0:T(8,128)(2,1)S(1)} %pad_maximum_fusion.1.share_ref, bf16[200,1024]{1,0:T(8,128)(2,1)S(1)} %collective-permute-done.19.refs_0_, bf16[200,1024]{1,0:T(8,128)(2,1)S(1)} %collective-permute-done.20.refs_1_, f32[640,1024]{1,0:T(8,128)S(1)} %combine.2.refs_2_), custom_call_target="tpu_custom_call" | custom-call | flops 1342177280 | bytes 4980736 | tf_op jit(solution)/shard_map/combine/pallas_call | solution.py:189
  (132 shorter events, 5.6 us)
Async XLA Ops:
  0.0 16.0 %collective-permute-start.1 = (bf16[640,4096]{1,0:T(8,128)(2,1)}, bf16[640,4096]{1,0:T(8,128)(2,1)}, u32[]{:S(2)}, u32[]{:S(2)}) collective-permute-start(bf16[640,4096]{1,0:T(8,128)(2,1)} %tokens_ref.3), channel_id=1, source_target_pairs={{0,16},{16,0},{1,17},{17,1},{2,18},{18,2},{3,19},{19,3},{4,20},{20... | collective-permute-start | bytes 15728648 | tf_op jit(solution)/shard_map/ppermute | solution.py:222
  0.0 2.5 copy-start.37
  0.0 2.9 %copy-start.29 = (f32[416,1]{1,0:T(8,128)S(1)}, f32[416,1]{1,0:T(8,128)}, u32[]{:S(2)}) copy-start(f32[416,1]{1,0:T(8,128)} %constant.95.row_slot_ref) | copy-start | bytes 4996
  0.0 2.9 %copy-start.31 = (bf16[416,16]{1,0:T(8,128)(2,1)S(1)}, bf16[416,16]{1,0:T(8,128)(2,1)}, u32[]{:S(2)}) copy-start(bf16[416,16]{1,0:T(8,128)(2,1)} %constant.87.clone.spread_ref) | copy-start | bytes 39940
  1.9 11.6 %collective-permute-start.8 = (bf16[512,1024]{1,0:T(8,128)(2,1)S(1)}, bf16[512,1024]{1,0:T(8,128)(2,1)}, u32[]{:S(2)}, u32[]{:S(2)}) collective-permute-start(bf16[512,1024]{1,0:T(8,128)(2,1)S(1)} %get-tuple-element.81), channel_id=1, source_target_pairs={{0,16},{16,0},{1,17},{17,1},{2,18},{18,2},{3,19},{19,3},{4,20},{20... | collective-permute-start | bytes 3145736 | tf_op jit(solution)/shard_map/ppermute | solution.py:222
  2.9 2.5 copy-start
  5.4 89.6 %slice-start = ((s8[5242880]{0:T(1024)(128)(4,1)}), s8[4194304]{0:T(1024)(128)(4,1)S(1)}, s32[]{:S(2)}) async-start(s8[5242880]{0:T(1024)(128)(4,1)} %bitcast.30), calls=%async_computation | async-start | bytes 8388608
  9.6 36.2 %collective-permute-start.21 = (bf16[200,4096]{1,0:T(8,128)(2,1)S(1)}, bf16[200,4096]{1,0:T(8,128)(2,1)S(1)}, u32[]{:S(2)}, u32[]{:S(2)}) collective-permute-start(bf16[200,4096]{1,0:T(8,128)(2,1)S(1)} %get-tuple-element.59), channel_id=1, source_target_pairs={{0,1},{1,2},{2,3},{3,0},{4,5},{5,6},{6,7},{7,4},{8,9},{9,10},{10,1... | collective-permute-start | bytes 4915208 | tf_op jit(solution)/shard_map/ppermute | solution.py:218
  11.2 1.8 collective-permute-start
  11.3 25.6 %collective-permute-start.26 = (bf16[512,1024]{1,0:T(8,128)(2,1)S(1)}, bf16[512,1024]{1,0:T(8,128)(2,1)S(1)}, u32[]{:S(2)}, u32[]{:S(2)}) collective-permute-start(bf16[512,1024]{1,0:T(8,128)(2,1)S(1)} %get-tuple-element.82.refs_4_), channel_id=1, source_target_pairs={{0,32},{32,64},{64,96},{96,0},{1,33},{33,65},{65,97},{97,1},{2,34}... | collective-permute-start | bytes 3145736 | tf_op jit(solution)/shard_map/ppermute | solution.py:222
  13.0 25.4 %collective-permute-start.28 = (bf16[512,1024]{1,0:T(8,128)(2,1)S(1)}, bf16[512,1024]{1,0:T(8,128)(2,1)S(1)}, u32[]{:S(2)}, u32[]{:S(2)}) collective-permute-start(bf16[512,1024]{1,0:T(8,128)(2,1)S(1)} %get-tuple-element.82.refs_4_), channel_id=1, source_target_pairs={{32,0},{64,32},{96,64},{0,96},{33,1},{65,33},{97,65},{1,97},{34,2}... | collective-permute-start | bytes 3145736 | tf_op jit(solution)/shard_map/ppermute | solution.py:222
  13.4 32.5 %collective-permute-start.2 = (bf16[200,4096]{1,0:T(8,128)(2,1)S(1)}, bf16[200,4096]{1,0:T(8,128)(2,1)S(1)}, u32[]{:S(2)}, u32[]{:S(2)}) collective-permute-start(bf16[200,4096]{1,0:T(8,128)(2,1)S(1)} %get-tuple-element.44), channel_id=1, source_target_pairs={{0,3},{1,0},{2,1},{3,2},{4,7},{5,4},{6,5},{7,6},{8,11},{9,8},{10,9... | collective-permute-start | bytes 4915208 | tf_op jit(solution)/shard_map/ppermute | solution.py:218
  16.0 27.3 %collective-permute-start.7 = (bf16[512,1024]{1,0:T(8,128)(2,1)S(1)}, bf16[512,1024]{1,0:T(8,128)(2,1)S(1)}, u32[]{:S(2)}, u32[]{:S(2)}) collective-permute-start(bf16[512,1024]{1,0:T(8,128)(2,1)S(1)} %get-tuple-element.82.refs_4_), channel_id=1, source_target_pairs={{0,1},{1,2},{2,3},{3,0},{4,5},{5,6},{6,7},{7,4},{8,9},{9,10},{10,1... | collective-permute-start | bytes 3145736 | tf_op jit(solution)/shard_map/ppermute | solution.py:218
  16.0 79.0 %slice-start.1 = ((s8[5242880]{0:T(1024)(128)(4,1)}), s8[1048576]{0:T(1024)(128)(4,1)S(1)}, s32[]{:S(2)}) async-start(s8[5242880]{0:T(1024)(128)(4,1)} %bitcast.30), calls=%async_computation.1 | async-start | bytes 2097152
  16.2 78.8 %copy-start.30 = (bf16[416,16]{1,0:T(8,128)(2,1)S(1)}, bf16[416,16]{1,0:T(8,128)(2,1)}, u32[]{:S(2)}) copy-start(bf16[416,16]{1,0:T(8,128)(2,1)} %constant.89.clone.spread_ref) | copy-start | bytes 39940
  36.9 56.0 %collective-permute-start.22 = (bf16[200,4096]{1,0:T(8,128)(2,1)S(1)}, bf16[200,4096]{1,0:T(8,128)(2,1)S(1)}, u32[]{:S(2)}, u32[]{:S(2)}) collective-permute-start(bf16[200,4096]{1,0:T(8,128)(2,1)S(1)} %get-tuple-element.60), channel_id=1, source_target_pairs={{0,1},{1,2},{2,3},{3,0},{4,5},{5,6},{6,7},{7,4},{8,9},{9,10},{10,1... | collective-permute-start | bytes 4915208 | tf_op jit(solution)/shard_map/ppermute | solution.py:218
  39.4 25.0 %collective-permute-start.29 = (bf16[512,1024]{1,0:T(8,128)(2,1)}, bf16[512,1024]{1,0:T(8,128)(2,1)S(1)}, u32[]{:S(2)}, u32[]{:S(2)}) collective-permute-start(bf16[512,1024]{1,0:T(8,128)(2,1)} %collective-permute-done.8.refs_5_), channel_id=1, source_target_pairs={{32,0},{64,32},{96,64},{0,96},{33,1},{65,33},{97,65},{1,97},{34,2}... | collective-permute-start | bytes 3145736 | tf_op jit(solution)/shard_map/ppermute | solution.py:222
  43.3 56.0 %copy-start.5 = (bf16[512,1024]{1,0:T(8,128)(2,1)}, bf16[512,1024]{1,0:T(8,128)(2,1)S(1)}, u32[]{:S(2)}) copy-start(bf16[512,1024]{1,0:T(8,128)(2,1)S(1)} %collective-permute-done.7.refs_4_) | copy-start | bytes 3145732
  43.3 26.0 %collective-permute-start.30 = (bf16[512,1024]{1,0:T(8,128)(2,1)S(1)}, bf16[512,1024]{1,0:T(8,128)(2,1)S(1)}, u32[]{:S(2)}, u32[]{:S(2)}) collective-permute-start(bf16[512,1024]{1,0:T(8,128)(2,1)S(1)} %collective-permute-done.26.refs_6_), channel_id=1, source_target_pairs={{0,32},{32,64},{64,96},{96,0},{1,33},{33,65},{65,97},{97,1},{2,34}... | collective-permute-start | bytes 3145736 | tf_op jit(solution)/shard_map/ppermute | solution.py:222
  45.9 45.9 %collective-permute-start.27 = (bf16[512,1024]{1,0:T(8,128)(2,1)}, bf16[512,1024]{1,0:T(8,128)(2,1)S(1)}, u32[]{:S(2)}, u32[]{:S(2)}) collective-permute-start(bf16[512,1024]{1,0:T(8,128)(2,1)} %collective-permute-done.8.refs_5_), channel_id=1, source_target_pairs={{0,32},{32,64},{64,96},{96,0},{1,33},{33,65},{65,97},{97,1},{2,34}... | collective-permute-start | bytes 3145736 | tf_op jit(solution)/shard_map/ppermute | solution.py:222
  45.9 62.0 %collective-permute-start.9 = (bf16[512,1024]{1,0:T(8,128)(2,1)}, bf16[512,1024]{1,0:T(8,128)(2,1)S(1)}, u32[]{:S(2)}, u32[]{:S(2)}) collective-permute-start(bf16[512,1024]{1,0:T(8,128)(2,1)} %collective-permute-done.8.refs_5_), channel_id=1, source_target_pairs={{0,1},{1,2},{2,3},{3,0},{4,5},{5,6},{6,7},{7,4},{8,9},{9,10},{10,1... | collective-permute-start | bytes 3145736 | tf_op jit(solution)/shard_map/ppermute | solution.py:218
  64.4 34.9 %copy-start.17 = (bf16[512,1024]{1,0:T(8,128)(2,1)}, bf16[512,1024]{1,0:T(8,128)(2,1)S(1)}, u32[]{:S(2)}) copy-start(bf16[512,1024]{1,0:T(8,128)(2,1)S(1)} %collective-permute-done.29.refs_9_) | copy-start | bytes 3145732
  64.4 80.9 %collective-permute-start.3 = (bf16[200,4096]{1,0:T(8,128)(2,1)S(1)}, bf16[200,4096]{1,0:T(8,128)(2,1)S(1)}, u32[]{:S(2)}, u32[]{:S(2)}) collective-permute-start(bf16[200,4096]{1,0:T(8,128)(2,1)S(1)} %get-tuple-element.45), channel_id=1, source_target_pairs={{0,3},{1,0},{2,1},{3,2},{4,7},{5,4},{6,5},{7,6},{8,11},{9,8},{10,9... | collective-permute-start | bytes 4915208 | tf_op jit(solution)/shard_map/ppermute | solution.py:218
  70.3 42.3 %collective-permute-start.10 = (bf16[512,1024]{1,0:T(8,128)(2,1)S(1)}, bf16[512,1024]{1,0:T(8,128)(2,1)S(1)}, u32[]{:S(2)}, u32[]{:S(2)}) collective-permute-start(bf16[512,1024]{1,0:T(8,128)(2,1)S(1)} %collective-permute-done.7.refs_4_), channel_id=1, source_target_pairs={{0,32},{32,64},{64,96},{96,0},{1,33},{33,65},{65,97},{97,1},{2,34}... | collective-permute-start | bytes 3145736 | tf_op jit(solution)/shard_map/ppermute | solution.py:222
  92.8 26.0 %collective-permute-start.12 = (bf16[512,1024]{1,0:T(8,128)(2,1)S(1)}, bf16[512,1024]{1,0:T(8,128)(2,1)S(1)}, u32[]{:S(2)}, u32[]{:S(2)}) collective-permute-start(bf16[512,1024]{1,0:T(8,128)(2,1)S(1)} %collective-permute-done.7.refs_4_), channel_id=1, source_target_pairs={{32,0},{64,32},{96,64},{0,96},{33,1},{65,33},{97,65},{1,97},{34,2}... | collective-permute-start | bytes 3145736 | tf_op jit(solution)/shard_map/ppermute | solution.py:222
  92.9 48.4 %collective-permute-start.31 = (bf16[512,1024]{1,0:T(8,128)(2,1)S(1)}, bf16[512,1024]{1,0:T(8,128)(2,1)S(1)}, u32[]{:S(2)}, u32[]{:S(2)}) collective-permute-start(bf16[512,1024]{1,0:T(8,128)(2,1)S(1)} %collective-permute-done.29.refs_9_), channel_id=1, source_target_pairs={{32,0},{64,32},{96,64},{0,96},{33,1},{65,33},{97,65},{1,97},{34,2}... | collective-permute-start | bytes 3145736 | tf_op jit(solution)/shard_map/ppermute | solution.py:222
  105.0 40.9 %copy-start.34 = (bf16[512,32]{1,0:T(8,128)(2,1)S(1)}, bf16[512,32]{1,0:T(8,128)(2,1)}, u32[]{:S(2)}) copy-start(bf16[512,32]{1,0:T(8,128)(2,1)} %constant.92.clone) | copy-start | bytes 98308
  105.0 40.9 %copy-start.40 = (f32[512]{0:T(512)S(1)}, f32[512]{0:T(512)}, u32[]{:S(2)}) copy-start(f32[512]{0:T(512)} %constant.93.clone) | copy-start | bytes 6148
  107.9 39.7 %copy-start.11 = (bf16[512,1024]{1,0:T(8,128)(2,1)}, bf16[512,1024]{1,0:T(8,128)(2,1)S(1)}, u32[]{:S(2)}) copy-start(bf16[512,1024]{1,0:T(8,128)(2,1)S(1)} %collective-permute-done.9.refs_5_) | copy-start | bytes 3145732
  107.9 55.9 %collective-permute-start.23 = (bf16[200,4096]{1,0:T(8,128)(2,1)S(1)}, bf16[200,4096]{1,0:T(8,128)(2,1)S(1)}, u32[]{:S(2)}, u32[]{:S(2)}) collective-permute-start(bf16[200,4096]{1,0:T(8,128)(2,1)S(1)} %get-tuple-element.61), channel_id=1, source_target_pairs={{0,4},{1,5},{2,6},{3,7},{4,8},{5,9},{6,10},{7,11},{8,12},{9,13},{1... | collective-permute-start | bytes 4915208 | tf_op jit(solution)/shard_map/ppermute | solution.py:218
  112.6 35.0 %copy-start.13 = (bf16[512,1024]{1,0:T(8,128)(2,1)}, bf16[512,1024]{1,0:T(8,128)(2,1)S(1)}, u32[]{:S(2)}) copy-start(bf16[512,1024]{1,0:T(8,128)(2,1)S(1)} %collective-permute-done.10.refs_6_) | copy-start | bytes 3145732
  112.6 46.9 %collective-permute-start.13 = (bf16[512,1024]{1,0:T(8,128)(2,1)S(1)}, bf16[512,1024]{1,0:T(8,128)(2,1)S(1)}, u32[]{:S(2)}, u32[]{:S(2)}) collective-permute-start(bf16[512,1024]{1,0:T(8,128)(2,1)S(1)} %collective-permute-done.9.refs_5_), channel_id=1, source_target_pairs={{32,0},{64,32},{96,64},{0,96},{33,1},{65,33},{97,65},{1,97},{34,2}... | collective-permute-start | bytes 3145736 | tf_op jit(solution)/shard_map/ppermute | solution.py:222
  118.8 28.8 %copy-start.15 = (bf16[512,1024]{1,0:T(8,128)(2,1)}, bf16[512,1024]{1,0:T(8,128)(2,1)S(1)}, u32[]{:S(2)}) copy-start(bf16[512,1024]{1,0:T(8,128)(2,1)S(1)} %collective-permute-done.12.refs_8_) | copy-start | bytes 3145732
  118.8 40.7 %collective-permute-start.14 = (bf16[512,1024]{1,0:T(8,128)(2,1)S(1)}, bf16[512,1024]{1,0:T(8,128)(2,1)S(1)}, u32[]{:S(2)}, u32[]{:S(2)}) collective-permute-start(bf16[512,1024]{1,0:T(8,128)(2,1)S(1)} %collective-permute-done.10.refs_6_), channel_id=1, source_target_pairs={{0,32},{32,64},{64,96},{96,0},{1,33},{33,65},{65,97},{97,1},{2,34}... | collective-permute-start | bytes 3145736 | tf_op jit(solution)/shard_map/ppermute | solution.py:222
  142.2 39.5 %collective-permute-start.24 = (bf16[200,4096]{1,0:T(8,128)(2,1)}, bf16[200,4096]{1,0:T(8,128)(2,1)}, u32[]{:S(2)}, u32[]{:S(2)}) collective-permute-start(bf16[200,4096]{1,0:T(8,128)(2,1)} %get-tuple-element.62), channel_id=1, source_target_pairs={{0,12},{1,13},{2,14},{3,15},{4,0},{5,1},{6,2},{7,3},{8,4},{9,5},{1... | collective-permute-start | bytes 4915208 | tf_op jit(solution)/shard_map/ppermute | solution.py:218
  145.3 39.3 %collective-permute-start.25 = (bf16[200,4096]{1,0:T(8,128)(2,1)}, bf16[200,4096]{1,0:T(8,128)(2,1)}, u32[]{:S(2)}, u32[]{:S(2)}) collective-permute-start(bf16[200,4096]{1,0:T(8,128)(2,1)} %get-tuple-element.63), channel_id=1, source_target_pairs={{0,8},{1,9},{2,10},{3,11},{4,12},{5,13},{6,14},{7,15},{8,0},{9,1},... | collective-permute-start | bytes 4915208 | tf_op jit(solution)/shard_map/ppermute | solution.py:218
  159.5 4.3 %copy-start.23 = (bf16[512,1024]{1,0:T(8,128)(2,1)}, bf16[512,1024]{1,0:T(8,128)(2,1)S(1)}, u32[]{:S(2)}) copy-start(bf16[512,1024]{1,0:T(8,128)(2,1)S(1)} %collective-permute-done.13.refs_9_) | copy-start | bytes 3145732
  159.5 43.2 %collective-permute-start.4 = (bf16[200,4096]{1,0:T(8,128)(2,1)}, bf16[200,4096]{1,0:T(8,128)(2,1)}, u32[]{:S(2)}, u32[]{:S(2)}) collective-permute-start(bf16[200,4096]{1,0:T(8,128)(2,1)} %get-tuple-element.46), channel_id=1, source_target_pairs={{0,4},{1,5},{2,6},{3,7},{4,8},{5,9},{6,10},{7,11},{8,12},{9,13},{1... | collective-permute-start | bytes 4915208 | tf_op jit(solution)/shard_map/ppermute | solution.py:218
  160.6 56.3 %collective-permute-start.5 = (bf16[200,4096]{1,0:T(8,128)(2,1)}, bf16[200,4096]{1,0:T(8,128)(2,1)}, u32[]{:S(2)}, u32[]{:S(2)}) collective-permute-start(bf16[200,4096]{1,0:T(8,128)(2,1)} %get-tuple-element.47), channel_id=1, source_target_pairs={{0,12},{1,13},{2,14},{3,15},{4,0},{5,1},{6,2},{7,3},{8,4},{9,5},{1... | collective-permute-start | bytes 4915208 | tf_op jit(solution)/shard_map/ppermute | solution.py:218
  164.9 51.9 %collective-permute-start.6 = (bf16[200,4096]{1,0:T(8,128)(2,1)}, bf16[200,4096]{1,0:T(8,128)(2,1)}, u32[]{:S(2)}, u32[]{:S(2)}) collective-permute-start(bf16[200,4096]{1,0:T(8,128)(2,1)} %get-tuple-element.48), channel_id=1, source_target_pairs={{0,8},{1,9},{2,10},{3,11},{4,12},{5,13},{6,14},{7,15},{8,0},{9,1},... | collective-permute-start | bytes 4915208 | tf_op jit(solution)/shard_map/ppermute | solution.py:218
  167.7 16.9 %copy-start.24 = (bf16[512,1024]{1,0:T(8,128)(2,1)S(1)}, bf16[512,1024]{1,0:T(8,128)(2,1)}, u32[]{:S(2)}) copy-start(bf16[512,1024]{1,0:T(8,128)(2,1)} %copy-done.23) | copy-start | bytes 3145732
  168.4 13.3 %copy-start.12 = (bf16[512,1024]{1,0:T(8,128)(2,1)S(1)}, bf16[512,1024]{1,0:T(8,128)(2,1)}, u32[]{:S(2)}) copy-start(bf16[512,1024]{1,0:T(8,128)(2,1)} %copy-done.11) | copy-start | bytes 3145732
  168.5 16.6 %copy-start.22 = (bf16[512,1024]{1,0:T(8,128)(2,1)S(1)}, bf16[512,1024]{1,0:T(8,128)(2,1)}, u32[]{:S(2)}) copy-start(bf16[512,1024]{1,0:T(8,128)(2,1)} %copy-done.21) | copy-start | bytes 3145732
  168.5 16.6 %copy-start.28 = (bf16[512,1024]{1,0:T(8,128)(2,1)S(1)}, bf16[512,1024]{1,0:T(8,128)(2,1)}, u32[]{:S(2)}) copy-start(bf16[512,1024]{1,0:T(8,128)(2,1)} %copy-done.27) | copy-start | bytes 3145732
  181.8 18.4 %collective-permute-start.11 = (bf16[512,1024]{1,0:T(8,128)(2,1)S(1)}, bf16[512,1024]{1,0:T(8,128)(2,1)S(1)}, u32[]{:S(2)}, u32[]{:S(2)}) collective-permute-start(bf16[512,1024]{1,0:T(8,128)(2,1)S(1)} %copy-done.12), channel_id=1, source_target_pairs={{0,32},{32,64},{64,96},{96,0},{1,33},{33,65},{65,97},{97,1},{2,34}... | collective-permute-start | bytes 3145736 | tf_op jit(solution)/shard_map/ppermute | solution.py:222
  184.6 18.1 %collective-permute-start.15 = (bf16[512,1024]{1,0:T(8,128)(2,1)S(1)}, bf16[512,1024]{1,0:T(8,128)(2,1)S(1)}, u32[]{:S(2)}, u32[]{:S(2)}) collective-permute-start(bf16[512,1024]{1,0:T(8,128)(2,1)S(1)} %copy-done.24), channel_id=1, source_target_pairs={{32,0},{64,32},{96,64},{0,96},{33,1},{65,33},{97,65},{1,97},{34,2}... | collective-permute-start | bytes 3145736 | tf_op jit(solution)/shard_map/ppermute | solution.py:222
  184.7 2.7 %copy-start.20 = (bf16[512,1024]{1,0:T(8,128)(2,1)S(1)}, bf16[512,1024]{1,0:T(8,128)(2,1)}, u32[]{:S(2)}) copy-start(bf16[512,1024]{1,0:T(8,128)(2,1)} %copy-done.19) | copy-start | bytes 3145732
  187.3 29.5 %copy-start.2 = (bf16[200,4096]{1,0:T(8,128)(2,1)S(1)}, bf16[200,4096]{1,0:T(8,128)(2,1)}, u32[]{:S(2)}) copy-start(bf16[200,4096]{1,0:T(8,128)(2,1)} %copy-done.1) | copy-start | bytes 4915204
  187.3 29.5 %copy-start.6 = (bf16[512,1024]{1,0:T(8,128)(2,1)S(1)}, bf16[512,1024]{1,0:T(8,128)(2,1)}, u32[]{:S(2)}) copy-start(bf16[512,1024]{1,0:T(8,128)(2,1)} %copy-done.5) | copy-start | bytes 3145732
  187.4 29.5 %copy-start.14 = (bf16[512,1024]{1,0:T(8,128)(2,1)S(1)}, bf16[512,1024]{1,0:T(8,128)(2,1)}, u32[]{:S(2)}) copy-start(bf16[512,1024]{1,0:T(8,128)(2,1)} %copy-done.13) | copy-start | bytes 3145732
  187.4 29.5 %copy-start.16 = (bf16[512,1024]{1,0:T(8,128)(2,1)S(1)}, bf16[512,1024]{1,0:T(8,128)(2,1)}, u32[]{:S(2)}) copy-start(bf16[512,1024]{1,0:T(8,128)(2,1)} %copy-done.15) | copy-start | bytes 3145732
  187.4 29.5 %copy-start.26 = (bf16[512,1024]{1,0:T(8,128)(2,1)S(1)}, bf16[512,1024]{1,0:T(8,128)(2,1)}, u32[]{:S(2)}) copy-start(bf16[512,1024]{1,0:T(8,128)(2,1)} %copy-done.25) | copy-start | bytes 3145732
  200.1 33.1 %collective-permute-start.32 = (bf16[200,1024]{1,0:T(8,128)(2,1)S(1)}, bf16[200,1024]{1,0:T(8,128)(2,1)S(1)}, u32[]{:S(2)}, u32[]{:S(2)}) collective-permute-start(bf16[200,1024]{1,0:T(8,128)(2,1)S(1)} %get-tuple-element.66), channel_id=1, source_target_pairs={{4,0},{5,1},{6,2},{7,3},{8,4},{9,5},{10,6},{11,7},{12,8},{13,9},{1... | collective-permute-start | bytes 1228808 | tf_op jit(solution)/shard_map/ppermute | solution.py:218
  202.7 30.9 %collective-permute-start.33 = (bf16[200,1024]{1,0:T(8,128)(2,1)S(1)}, bf16[200,1024]{1,0:T(8,128)(2,1)S(1)}, u32[]{:S(2)}, u32[]{:S(2)}) collective-permute-start(bf16[200,1024]{1,0:T(8,128)(2,1)S(1)} %get-tuple-element.67), channel_id=1, source_target_pairs={{8,0},{9,1},{10,2},{11,3},{12,4},{13,5},{14,6},{15,7},{0,8},{1,9},... | collective-permute-start | bytes 1228808 | tf_op jit(solution)/shard_map/ppermute | solution.py:218
  202.7 30.9 %collective-permute-start.34 = (bf16[200,1024]{1,0:T(8,128)(2,1)S(1)}, bf16[200,1024]{1,0:T(8,128)(2,1)S(1)}, u32[]{:S(2)}, u32[]{:S(2)}) collective-permute-start(bf16[200,1024]{1,0:T(8,128)(2,1)S(1)} %get-tuple-element.68), channel_id=1, source_target_pairs={{12,0},{13,1},{14,2},{15,3},{0,4},{1,5},{2,6},{3,7},{4,8},{5,9},{6... | collective-permute-start | bytes 1228808 | tf_op jit(solution)/shard_map/ppermute | solution.py:218
  228.9 13.6 %collective-permute-start.16 = (bf16[200,1024]{1,0:T(8,128)(2,1)S(1)}, bf16[200,1024]{1,0:T(8,128)(2,1)S(1)}, u32[]{:S(2)}, u32[]{:S(2)}) collective-permute-start(bf16[200,1024]{1,0:T(8,128)(2,1)S(1)} %get-tuple-element.51), channel_id=1, source_target_pairs={{4,0},{5,1},{6,2},{7,3},{8,4},{9,5},{10,6},{11,7},{12,8},{13,9},{1... | collective-permute-start | bytes 1228808 | tf_op jit(solution)/shard_map/ppermute | solution.py:218
  232.6 9.9 %collective-permute-start.17 = (bf16[200,1024]{1,0:T(8,128)(2,1)S(1)}, bf16[200,1024]{1,0:T(8,128)(2,1)S(1)}, u32[]{:S(2)}, u32[]{:S(2)}) collective-permute-start(bf16[200,1024]{1,0:T(8,128)(2,1)S(1)} %get-tuple-element.52), channel_id=1, source_target_pairs={{8,0},{9,1},{10,2},{11,3},{12,4},{13,5},{14,6},{15,7},{0,8},{1,9},... | collective-permute-start | bytes 1228808 | tf_op jit(solution)/shard_map/ppermute | solution.py:218
  233.2 13.3 %collective-permute-start.18 = (bf16[200,1024]{1,0:T(8,128)(2,1)S(1)}, bf16[200,1024]{1,0:T(8,128)(2,1)S(1)}, u32[]{:S(2)}, u32[]{:S(2)}) collective-permute-start(bf16[200,1024]{1,0:T(8,128)(2,1)S(1)} %get-tuple-element.53), channel_id=1, source_target_pairs={{12,0},{13,1},{14,2},{15,3},{0,4},{1,5},{2,6},{3,7},{4,8},{5,9},{6... | collective-permute-start | bytes 1228808 | tf_op jit(solution)/shard_map/ppermute | solution.py:218
  233.7 13.3 %collective-permute-start.35 = (bf16[200,1024]{1,0:T(8,128)(2,1)S(1)}, bf16[200,1024]{1,0:T(8,128)(2,1)S(1)}, u32[]{:S(2)}, u32[]{:S(2)}) collective-permute-start(bf16[200,1024]{1,0:T(8,128)(2,1)S(1)} %get-tuple-element.70), channel_id=1, source_target_pairs={{1,0},{2,1},{3,2},{0,3},{5,4},{6,5},{7,6},{4,7},{9,8},{10,9},{11,1... | collective-permute-start | bytes 1228808 | tf_op jit(solution)/shard_map/ppermute | solution.py:218
  235.6 11.5 %collective-permute-start.36 = (bf16[200,1024]{1,0:T(8,128)(2,1)S(1)}, bf16[200,1024]{1,0:T(8,128)(2,1)S(1)}, u32[]{:S(2)}, u32[]{:S(2)}) collective-permute-start(bf16[200,1024]{1,0:T(8,128)(2,1)S(1)} %get-tuple-element.72), channel_id=1, source_target_pairs={{0,16},{1,17},{2,18},{3,19},{4,20},{5,21},{6,22},{7,23},{8,24},{9,... | collective-permute-start | bytes 1228808 | tf_op jit(solution)/shard_map/ppermute | solution.py:218
  242.5 7.4 %collective-permute-start.37 = (bf16[200,1024]{1,0:T(8,128)(2,1)S(1)}, bf16[200,1024]{1,0:T(8,128)(2,1)S(1)}, u32[]{:S(2)}, u32[]{:S(2)}) collective-permute-start(bf16[200,1024]{1,0:T(8,128)(2,1)S(1)} %get-tuple-element.73), channel_id=1, source_target_pairs={{1,16},{2,17},{3,18},{0,19},{5,20},{6,21},{7,22},{4,23},{9,24},{10... | collective-permute-start | bytes 1228808 | tf_op jit(solution)/shard_map/ppermute | solution.py:218
  246.6 3.2 %collective-permute-start.38 = (bf16[200,1024]{1,0:T(8,128)(2,1)S(1)}, bf16[200,1024]{1,0:T(8,128)(2,1)S(1)}, u32[]{:S(2)}, u32[]{:S(2)}) collective-permute-start(bf16[200,1024]{1,0:T(8,128)(2,1)S(1)} %get-tuple-element.74), channel_id=1, source_target_pairs={{0,16},{1,17},{2,18},{3,19},{4,20},{5,21},{6,22},{7,23},{8,24},{9,... | collective-permute-start | bytes 1228808 | tf_op jit(solution)/shard_map/ppermute | solution.py:218
  246.7 9.2 %collective-permute-start.19 = (bf16[200,1024]{1,0:T(8,128)(2,1)S(1)}, bf16[200,1024]{1,0:T(8,128)(2,1)S(1)}, u32[]{:S(2)}, u32[]{:S(2)}) collective-permute-start(bf16[200,1024]{1,0:T(8,128)(2,1)S(1)} %get-tuple-element.54), channel_id=1, source_target_pairs={{3,0},{0,1},{1,2},{2,3},{7,4},{4,5},{5,6},{6,7},{11,8},{8,9},{9,10... | collective-permute-start | bytes 1228808 | tf_op jit(solution)/shard_map/ppermute | solution.py:218
  247.1 12.7 %collective-permute-start.20 = (bf16[200,1024]{1,0:T(8,128)(2,1)S(1)}, bf16[200,1024]{1,0:T(8,128)(2,1)S(1)}, u32[]{:S(2)}, u32[]{:S(2)}) collective-permute-start(bf16[200,1024]{1,0:T(8,128)(2,1)S(1)} %get-tuple-element.55), channel_id=1, source_target_pairs={{3,16},{0,17},{1,18},{2,19},{7,20},{4,21},{5,22},{6,23},{11,24},{8... | collective-permute-start | bytes 1228808 | tf_op jit(solution)/shard_map/ppermute | solution.py:218
  (18 other events, 29.3 us)
